TPU v7x, 128 devices: a whole 4x4x4 slice. The times are simulated.
128 devices in a mesh: grp: 8 (over y, core), inner: 16 (over z, x).
Axes of the slice: x: 4, y: 4, z: 4, core: 2. Of those that a mesh axis runs over, the one named last changes fastest.
Arguments:
- grad_out: bfloat16 [16384, 2048], P(('grp', 'inner')), may hold values from -6 to 6
- hidden: bfloat16 [16384, 2048], P(('grp', 'inner')), may hold values from -6 to 6
- norm_gain: float32 [2048], replicated, may hold values from 0.25 to 1.75
- expert_ids: int32 [16384, 8], P(('grp', 'inner')), may hold values from 0 to 127, all different within a row; in each aligned block of 128 rows (0 to 127, 128 to 255, ...) at most 10 rows name the same one
- gate_weights: float32 [16384, 8], P(('grp', 'inner')), may hold values from 0.02 to 0.5
- w_gate: bfloat16 [128, 2048, 768], P(('grp', 'inner')), may hold values from -0.125 to 0.125
- w_up: bfloat16 [128, 2048, 768], P(('grp', 'inner')), may hold values from -0.125 to 0.125
- w_down: bfloat16 [128, 768, 2048], P(('grp', 'inner')), may hold values from -0.21875 to 0.21875
- w_out: bfloat16 [4096, 2048], P('inner'), may hold values from -0.09375 to 0.09375
- queries: bfloat16 [16384, 4096], P(('grp', 'inner')), may hold values from -0.6 to 0.6
- keys: bfloat16 [16384, 512], P(('grp', 'inner')), may hold values from -0.6 to 0.6
- values: bfloat16 [16384, 512], P(('grp', 'inner')), may hold values from -6 to 6
- attn_out: bfloat16 [16384, 4096], P(('grp', 'inner')), may hold values from -6 to 6
- lse: float32 [32, 16384], P('inner', 'grp'), as said below
Outputs:
- grad_resid: bfloat16 [16384, 2048], P(('grp', 'inner'))
- queries_gradient: bfloat16 [16384, 4096], P(('grp', 'inner'))
- keys_gradient: bfloat16 [16384, 512], P(('grp', 'inner'))
- values_gradient: bfloat16 [16384, 512], P(('grp', 'inner'))
Inputs may be any that keep to these rules, and one draw needn't show every extreme that they name: `expert_ids`: each token names 8 different experts. Among the 128 tokens of one device (aligned blocks of rows), no expert is named by more than 10 tokens; in some device's tokens one expert is named by exactly 10. lse[h, t] minus log(1 + the position of token t in its sequence of 2048) lies between 0 and 1.5.
All inputs are finite; a program needn't handle non-finite values.
Results may differ from a plain program's by a relative error of at most 0.012.
Values may be sent and summed in bfloat16 or wider, within the bound.
No kernel may reach another device: no remote copies, remote signals or barrier semaphores. Data moves between devices by JAX's collectives and lax.ppermute only.
A program may use at most 192 MiB of HBM per device.

v0:
```python
import jax
import jax.numpy as jnp
from jax import lax
from jax.sharding import PartitionSpec as P

KEY_VALUE_HEADS = 4
HEAD_SIZE = 128


EPSILON = 1e-06


def grouped_exchange(value, axis, split_dim, concat_dim, work, item_dim, out_dim):
    items = jax.tree.leaves(value)[0].shape[item_dim]
    count = 2 if items % 2 == 0 else 1
    finished = []
    for k in range(count):
        group = jax.tree.map(
            lambda a: lax.slice_in_dim(
                a, k * (items // count), (k + 1) * (items // count), axis=item_dim
            ),
            value,
        )
        finished.append(
            work(
                lax.all_to_all(
                    group, axis, split_axis=split_dim, concat_axis=concat_dim, tiled=True
                )
            )
        )
    return jax.tree.map(lambda *parts: jnp.concatenate(parts, axis=out_dim), *finished)


def contract_last(left, right):
    return lax.dot_general(
        left, right, (((1,), (1,)), ((), ())), preferred_element_type=jnp.float32
    )


def contract_first(left, right):
    return lax.dot_general(
        left, right, (((0,), (0,)), ((), ())), preferred_element_type=jnp.float32
    )


def expert_grads(received, w_gate, w_up, w_down):
    local = w_gate.shape[0]
    width = w_gate.shape[1]
    shaped = received.reshape((-1, local) + received.shape[1:])
    inputs = shaped[..., :width]
    upstream = shaped[..., width:]
    gate_pre = jnp.einsum("nlcd,ldf->nlcf", inputs, w_gate, preferred_element_type=jnp.float32)
    up_pre = jnp.einsum("nlcd,ldf->nlcf", inputs, w_up, preferred_element_type=jnp.float32)
    back_hidden = jnp.einsum("nlcd,lfd->nlcf", upstream, w_down, preferred_element_type=jnp.float32)
    sigmoid = jax.nn.sigmoid(gate_pre)
    grad_gate = (back_hidden * up_pre * sigmoid * (1.0 + gate_pre * (1.0 - sigmoid))).astype(
        jnp.bfloat16
    )
    grad_up = (back_hidden * gate_pre * sigmoid).astype(jnp.bfloat16)
    grad_in = jnp.einsum("nlcf,ldf->nlcd", grad_gate, w_gate, preferred_element_type=jnp.float32)
    grad_in = grad_in + jnp.einsum(
        "nlcf,ldf->nlcd", grad_up, w_up, preferred_element_type=jnp.float32
    )
    return grad_in.astype(jnp.bfloat16).reshape(received.shape[:-1] + (width,))


def per_device(
    grad_out,
    hidden,
    norm_gain,
    expert_ids,
    gate_weights,
    w_gate,
    w_up,
    w_down,
    w_out,
    queries,
    keys,
    values,
    attn_out,
    lse,
):
    token_rows, width = hidden.shape
    topk = expert_ids.shape[1]
    groups = lax.axis_size("grp")
    inner_product = lax.axis_size("inner")
    experts_all = w_gate.shape[0] * groups * inner_product
    capacity = max(2, 5 * token_rows * topk // (4 * experts_all))
    hidden_f = hidden.astype(jnp.float32)
    inverse = lax.rsqrt(jnp.mean(hidden_f * hidden_f, axis=1, keepdims=True) + EPSILON)
    normed = (hidden_f * inverse * norm_gain).astype(jnp.bfloat16)
    upstream = grad_out.astype(jnp.float32)
    flat_count = token_rows * topk
    flat_ids = expert_ids.reshape(-1)
    one_hot = (flat_ids[:, None] == jnp.arange(experts_all, dtype=jnp.int32)[None, :]).astype(
        jnp.int32
    )
    slot_rank = jnp.sum((jnp.cumsum(one_hot, axis=0) - one_hot) * one_hot, axis=1)
    target = flat_ids * capacity + slot_rank
    owner = (
        jnp.full((experts_all * capacity,), flat_count, jnp.int32)
        .at[target]
        .set(jnp.arange(flat_count, dtype=jnp.int32))
    )
    source_tok = owner // topk
    scaled = (
        (upstream[:, None, :] * gate_weights[:, :, None])
        .reshape(flat_count, width)
        .astype(jnp.bfloat16)
    )
    zero_row = jnp.zeros((1, width), jnp.bfloat16)
    slot_inputs = jnp.concatenate([normed, zero_row], axis=0)[source_tok]
    slot_grads = jnp.concatenate([scaled, zero_row], axis=0)[owner]
    outgoing = jnp.concatenate([slot_inputs, slot_grads], axis=1).reshape(
        experts_all, capacity, 2 * width
    )

    def expert_work(arrived):
        return lax.all_to_all(
            expert_grads(arrived, w_gate, w_up, w_down),
            ("grp", "inner"),
            split_axis=0,
            concat_axis=0,
            tiled=True,
        )

    returned = grouped_exchange(outgoing, ("grp", "inner"), 0, 0, expert_work, 1, 1)
    expert_rows = returned.reshape(-1, width)[target].astype(jnp.float32)
    grad_normed = jnp.sum(expert_rows.reshape(token_rows, topk, width), axis=1)
    gained = grad_normed * norm_gain
    statistic = jnp.mean(gained * hidden_f, axis=1, keepdims=True)
    grad_resid = (
        upstream + inverse * gained - hidden_f * inverse * inverse * inverse * statistic
    ).astype(jnp.bfloat16)
    head_width = queries.shape[1] // inner_product
    per_head = head_width // HEAD_SIZE
    shared_portion = inner_product // KEY_VALUE_HEADS
    key_value_pairs = jnp.concatenate(
        [
            keys.reshape(token_rows, KEY_VALUE_HEADS, 1, HEAD_SIZE),
            values.reshape(token_rows, KEY_VALUE_HEADS, 1, HEAD_SIZE),
        ],
        axis=2,
    )
    key_value_broadcast = jnp.broadcast_to(
        key_value_pairs[:, :, None], (token_rows, KEY_VALUE_HEADS, shared_portion, 2, HEAD_SIZE)
    ).reshape(token_rows, inner_product * 2 * HEAD_SIZE)
    head_query, head_output, head_kv = (
        lax.all_to_all(queries, "inner", split_axis=1, concat_axis=0, tiled=True),
        lax.all_to_all(attn_out, "inner", split_axis=1, concat_axis=0, tiled=True),
        lax.all_to_all(key_value_broadcast, "inner", split_axis=1, concat_axis=0, tiled=True),
    )
    head_grad = contract_last(
        lax.all_gather(grad_resid, "inner", axis=0, tiled=True), w_out
    ).astype(jnp.bfloat16)
    seq_len = head_query.shape[0]
    head_key = head_kv[:, :HEAD_SIZE]
    head_value = head_kv[:, HEAD_SIZE:]
    lse_rows = lse.T
    scale = float(HEAD_SIZE) ** (-0.5)
    blocks = 1
    while blocks < 8 and seq_len % (2 * blocks) == 0 and (seq_len // (2 * blocks) >= 512):
        blocks = blocks * 2
    block_len = seq_len // blocks
    grad_key_acc = jnp.zeros((seq_len, HEAD_SIZE), jnp.float32)
    grad_value_acc = jnp.zeros((seq_len, HEAD_SIZE), jnp.float32)
    query_parts = []
    for block_index in range(blocks):
        low = block_index * block_len
        high = low + block_len
        block_query = head_query[low:high].reshape(block_len * per_head, HEAD_SIZE)
        block_output = head_output[low:high].reshape(block_len * per_head, HEAD_SIZE)
        block_grad = head_grad[low:high].reshape(block_len * per_head, HEAD_SIZE)
        block_lse = lse_rows[low:high].reshape(-1)
        seen_key = head_key[:high]
        seen_value = head_value[:high]
        scores = contract_last(block_query, seen_key) * scale
        row_position = low + jnp.arange(block_len * per_head, dtype=jnp.int32) // per_head
        visible = jnp.arange(high, dtype=jnp.int32)[None, :] <= row_position[:, None]
        probs = jnp.where(visible, jnp.exp(scores - block_lse[:, None]), 0.0)
        grad_probs = contract_last(block_grad, seen_value)
        delta = jnp.sum(
            block_grad.astype(jnp.float32) * block_output.astype(jnp.float32), axis=1, keepdims=True
        )
        grad_scores = (probs * (grad_probs - delta)).astype(jnp.bfloat16)
        query_part = jnp.dot(grad_scores, seen_key, preferred_element_type=jnp.float32) * scale
        query_parts.append(query_part.reshape(block_len, head_width))
        grad_key_acc = grad_key_acc.at[:high].add(contract_first(grad_scores, block_query) * scale)
        grad_value_acc = grad_value_acc.at[:high].add(
            contract_first(probs.astype(jnp.bfloat16), block_grad)
        )
    grad_query_heads = jnp.concatenate(query_parts, axis=0)
    kv_heads = jnp.concatenate([grad_key_acc, grad_value_acc], axis=1)
    token_query, token_key_value = (
        lax.all_to_all(
            grad_query_heads.astype(jnp.bfloat16), "inner", split_axis=0, concat_axis=1, tiled=True
        ).astype(grad_query_heads.dtype),
        lax.all_to_all(
            kv_heads.astype(jnp.bfloat16), "inner", split_axis=0, concat_axis=1, tiled=True
        ).astype(kv_heads.dtype),
    )
    summed_total = jnp.sum(
        token_key_value.reshape(token_rows, KEY_VALUE_HEADS, shared_portion, 2, HEAD_SIZE), axis=2
    )
    keys_gradient = (
        summed_total[:, :, 0].reshape(token_rows, KEY_VALUE_HEADS * HEAD_SIZE).astype(jnp.bfloat16)
    )
    values_gradient = (
        summed_total[:, :, 1].reshape(token_rows, KEY_VALUE_HEADS * HEAD_SIZE).astype(jnp.bfloat16)
    )
    return (grad_resid, token_query.astype(jnp.bfloat16), keys_gradient, values_gradient)


def solution(mesh):
    placed = (
        P(("grp", "inner"), None),
        P(("grp", "inner"), None),
        P(),
        P(("grp", "inner"), None),
        P(("grp", "inner"), None),
        P(("grp", "inner"), None, None),
        P(("grp", "inner"), None, None),
        P(("grp", "inner"), None, None),
        P("inner", None),
        P(("grp", "inner"), None),
        P(("grp", "inner"), None),
        P(("grp", "inner"), None),
        P(("grp", "inner"), None),
        P("inner", "grp"),
    )
    return jax.shard_map(
        per_device,
        mesh=mesh,
        in_specs=placed,
        out_specs=(
            P(("grp", "inner"), None),
            P(("grp", "inner"), None),
            P(("grp", "inner"), None),
            P(("grp", "inner"), None),
        ),
        check_vma=False,
    )
```

profile of v0, /device:TPU:0, one launch (start us, length us, event | category | flops | bytes accessed | tf_op | source)
XLA Modules:
  0.0 660.2 jit_solution(1632442366203681859)
XLA Ops:
  13.8 4.3 scatter_custom_fusion
  28.1 12.0 %gather_fusion = bf16[1280,2048]{1,0:T(8,128)(2,1)} fusion(bf16[129,2048]{1,0:T(8,128)(2,1)} %concatenate.46, s32[2048]{0:T(1024)S(1)} %get-tuple-element.143), kind=kCustom, calls=%fused_computation | custom fusion | bytes 10490880 | tf_op jit(solution)/shard_map/gather | solution.py:112
  40.1 13.6 %gather_fusion.1 = bf16[1280,2048]{1,0:T(8,128)(2,1)} fusion(bf16[1025,2048]{1,0:T(8,128)(2,1)} %concatenate.47, s32[2048]{0:T(1024)S(1)} %get-tuple-element.142), kind=kCustom, calls=%fused_computation.1 | custom fusion | bytes 10490880 | tf_op jit(solution)/shard_map/gather | solution.py:113
  53.7 9.9 %pad_maximum_fusion = bf16[1280,4096]{1,0:T(8,128)(2,1)} fusion(bf16[1280,2048]{1,0:T(8,128)(2,1)} %gather_fusion.1, bf16[1280,2048]{1,0:T(8,128)(2,1)} %gather_fusion), kind=kLoop, calls=%fused_computation.4 | loop fusion | flops 20971520 | bytes 20971520 | tf_op jit(solution)/shard_map/concatenate | solution.py:114
  63.6 15.5 %reshape.473 = bf16[128,10,4096]{2,1,0:T(8,128)(2,1)} reshape(bf16[1280,4096]{1,0:T(8,128)(2,1)} %pad_maximum_fusion) | data formatting | bytes 20971520 | tf_op jit(solution)/shard_map/reshape | solution.py:114
  79.1 12.3 %fusion.138 = (bf16[128,5,4096]{2,1,0:T(8,128)(2,1)S(1)}, bf16[128,5,4096]{2,1,0:T(8,128)(2,1)}) fusion(bf16[128,10,4096]{2,1,0:T(8,128)(2,1)} %reshape.473), kind=kLoop, calls=%fused_computation.196 | loop fusion | bytes 20971520 | tf_op jit(solution)/shard_map/slice | solution.py:19
  91.4 107.2 %all_to_all.97 = bf16[128,5,4096]{2,1,0:T(8,128)(2,1)} all-to-all(bf16[128,5,4096]{2,1,0:T(8,128)(2,1)S(1)} %get-tuple-element.120), channel_id=1, replica_groups=mesh['grp'=8,'inner'=16] {'grp','inner'}, dimensions={0} | all-to-all | bytes 10485760 | tf_op jit(solution)/shard_map/all_to_all | solution.py:26
  198.6 6.3 all-to-all-start.2
  204.9 6.9 %copy.109 = bf16[128,5,4096]{2,0,1:T(8,128)(2,1)S(1)} copy(bf16[128,5,4096]{2,1,0:T(8,128)(2,1)} %all_to_all.97) | data formatting | bytes 10485760 | tf_op jit(solution)/shard_map/all_to_all | solution.py:26
  219.6 11.2 %fusion.8 = f32[128,5,2048]{2,0,1:T(8,128)} fusion(bf16[1,2048,768]{2,1,0:T(8,128)(2,1)} %param.39, f32[128,5,768]{2,0,1:T(8,128)} %fusion.10, bf16[1,2048,768]{2,1,0:T(8,128)(2,1)S(1)} %copy-done, bf16[128,1,5,4096]{3,0,2,1:T(8,128)(2,1)} %bitcast.323, f32[128,5,768]{2,0,1:T(8,128)} %fusion.20), kind=kOutput, calls=%fused_computation.28 | convolution fusion | flops 4031447040 | bytes 18087936 | tf_op jit(solution)/shard_map/nlcf,ldf->nlcd/dot_general | solution.py:60
  230.8 16.4 %add_convert_fusion.1 = bf16[128,5,2048]{2,0,1:T(8,128)(2,1)S(1)} fusion(f32[128,5,2048]{2,0,1:T(8,128)} %fusion.8, bf16[1,2048,768]{2,1,0:T(8,128)(2,1)S(1)} %copy-done, f32[128,5,768]{2,0,1:T(8,128)} %fusion.20, f32[128,5,768]{2,0,1:T(8,128)} %fusion.10), kind=kOutput, calls=%fused_computation.19 | convolution fusion | flops 2018836480 | bytes 14942208 | tf_op jit(solution)/shard_map/nlcf,ldf->nlcd/dot_general | solution.py:61
  250.6 51.8 %all-to-all-done.2 = bf16[128,5,4096]{2,1,0:T(8,128)(2,1)} async-done(((bf16[128,5,4096]{2,1,0:T(8,128)(2,1)}), bf16[128,5,4096]{2,1,0:T(8,128)(2,1)}, u32[]{:S(2)}, u32[]{:S(2)}) %all-to-all-start.2) | async-done | bytes 5242912 | tf_op jit(solution)/shard_map/all_to_all | solution.py:26
  302.4 17.9 %all-to-all-start.1 = ((bf16[128,5,2048]{2,1,0:T(8,128)(2,1)}), bf16[128,5,2048]{2,1,0:T(8,128)(2,1)}, u32[]{:S(2)}, u32[]{:S(2)}) async-start(bf16[128,5,2048]{2,1,0:T(8,128)(2,1)} %copy.79), calls=%async_computation.1 | async-start | bytes 8388608 | tf_op jit(solution)/shard_map/all_to_all | solution.py:119
  320.4 6.9 %copy.108 = bf16[128,5,4096]{2,0,1:T(8,128)(2,1)S(1)} copy(bf16[128,5,4096]{2,1,0:T(8,128)(2,1)} %all-to-all-done.2) | data formatting | bytes 10485760 | tf_op jit(solution)/shard_map/all_to_all | solution.py:26
  335.0 11.2 %fusion.4 = f32[128,5,2048]{2,0,1:T(8,128)} fusion(bf16[1,2048,768]{2,1,0:T(8,128)(2,1)} %param.39, f32[128,5,768]{2,0,1:T(8,128)} %fusion.6, bf16[1,2048,768]{2,1,0:T(8,128)(2,1)S(1)} %copy-done, bf16[128,1,5,4096]{3,0,2,1:T(8,128)(2,1)} %bitcast.326, f32[128,5,768]{2,0,1:T(8,128)} %fusion.18), kind=kOutput, calls=%fused_computation.24 | convolution fusion | flops 4031447040 | bytes 18087936 | tf_op jit(solution)/shard_map/nlcf,ldf->nlcd/dot_general | solution.py:60
  346.2 6.4 add_convert_fusion
  356.0 15.0 %all-to-all-done.1 = bf16[128,5,2048]{2,1,0:T(8,128)(2,1)} async-done(((bf16[128,5,2048]{2,1,0:T(8,128)(2,1)}), bf16[128,5,2048]{2,1,0:T(8,128)(2,1)}, u32[]{:S(2)}, u32[]{:S(2)}) %all-to-all-start.1) | async-done | bytes 2621472 | tf_op jit(solution)/shard_map/all_to_all | solution.py:119
  371.1 6.0 all-to-all-start.3
  377.1 50.7 %all-to-all-done.3 = bf16[128,5,2048]{2,1,0:T(8,128)(2,1)} async-done(((bf16[128,5,2048]{2,1,0:T(8,128)(2,1)}), bf16[128,5,2048]{2,1,0:T(8,128)(2,1)}, u32[]{:S(2)}, u32[]{:S(2)}) %all-to-all-start.3) | async-done | bytes 2621472 | tf_op jit(solution)/shard_map/all_to_all | solution.py:119
  427.8 10.5 %pad_maximum_fusion.1 = bf16[128,10,2048]{2,1,0:T(8,128)(2,1)} fusion(bf16[128,5,2048]{2,1,0:T(8,128)(2,1)} %all-to-all-done.3, bf16[128,5,2048]{2,1,0:T(8,128)(2,1)} %all-to-all-done.1), kind=kLoop, calls=%fused_computation.5 | loop fusion | flops 10485760 | bytes 10485760 | tf_op jit(solution)/shard_map/concatenate | solution.py:31
  438.3 9.8 %reshape.487 = bf16[1280,2048]{1,0:T(8,128)(2,1)} reshape(bf16[128,10,2048]{2,1,0:T(8,128)(2,1)} %pad_maximum_fusion.1) | data formatting | bytes 10485760 | tf_op jit(solution)/shard_map/reshape | solution.py:128
  448.1 12.0 %gather_fusion.2 = bf16[1024,2048]{1,0:T(8,128)(2,1)} fusion(bf16[1280,2048]{1,0:T(8,128)(2,1)} %reshape.487, s32[1024]{0:T(1024)S(1)} %broadcast_clamp_fusion), kind=kCustom, calls=%fused_computation.2 | custom fusion | bytes 8392704 | tf_op jit(solution)/shard_map/gather | solution.py:128
  460.1 5.2 convert_reduce_fusion
  468.8 4.7 all-to-all-start.6
  475.9 21.7 %all-to-all-done.6 = bf16[128,16,256]{2,0,1:T(8,128)(2,1)S(1)} async-done(((bf16[128,16,256]{2,0,1:T(8,128)(2,1)}), bf16[128,16,256]{2,0,1:T(8,128)(2,1)S(1)}, u32[]{:S(2)}, u32[]{:S(2)}) %all-to-all-start.6) | async-done | bytes 1048608 | tf_op jit(solution)/shard_map/all_to_all | solution.py:150
  505.9 20.9 %all-to-all-done.5 = bf16[128,16,256]{2,0,1:T(8,128)(2,1)S(1)} async-done(((bf16[128,16,256]{2,0,1:T(8,128)(2,1)}), bf16[128,16,256]{2,0,1:T(8,128)(2,1)S(1)}, u32[]{:S(2)}, u32[]{:S(2)}) %all-to-all-start.5) | async-done | bytes 1048608 | tf_op jit(solution)/shard_map/all_to_all | solution.py:149
  543.0 12.7 %all-to-all-done.4 = bf16[128,16,256]{2,0,1:T(8,128)(2,1)S(1)} async-done(((bf16[128,16,256]{2,0,1:T(8,128)(2,1)}), bf16[128,16,256]{2,0,1:T(8,128)(2,1)S(1)}, u32[]{:S(2)}, u32[]{:S(2)}) %all-to-all-start.4) | async-done | bytes 1048608 | tf_op jit(solution)/shard_map/all_to_all | solution.py:151
  561.1 5.2 bitcast_select_fusion.1
  566.3 4.5 fusion.110
  570.8 6.1 convolution_convert_fusion
  610.9 4.6 all-to-all-start.8
  629.0 6.0 all-to-all-start.7
  (206 shorter events, 139.7 us)
Async XLA Ops:
  7.2 212.5 %copy-start = (bf16[1,2048,768]{2,1,0:T(8,128)(2,1)S(1)}, bf16[1,2048,768]{2,1,0:T(8,128)(2,1)}, u32[]{:S(2)}) copy-start(bf16[1,2048,768]{2,1,0:T(8,128)(2,1)} %param.40) | copy-start | bytes 9437188
  7.2 14.3 %copy-start.33 = (f32[128,8]{0,1:T(8,128)S(1)}, f32[128,8]{0,1:T(8,128)}, u32[]{:S(2)}) copy-start(f32[128,8]{0,1:T(8,128)} %param.38) | copy-start | bytes 12292
  7.2 14.5 %copy-start.31 = (f32[2048]{0:T(1024)S(1)}, f32[2048]{0:T(1024)}, u32[]{:S(2)}) copy-start(f32[2048]{0:T(1024)} %param.36) | copy-start | bytes 24580
  198.6 103.9 %all-to-all-start.2 = ((bf16[128,5,4096]{2,1,0:T(8,128)(2,1)}), bf16[128,5,4096]{2,1,0:T(8,128)(2,1)}, u32[]{:S(2)}, u32[]{:S(2)}) async-start(bf16[128,5,4096]{2,1,0:T(8,128)(2,1)} %get-tuple-element.121), calls=%async_computation.2 | async-start | bytes 16777216 | tf_op jit(solution)/shard_map/all_to_all | solution.py:26
  204.9 7.0 %copy-start.36 = (bf16[1,2048,768]{2,1,0:T(8,128)(2,1)S(1)}, bf16[1,2048,768]{2,1,0:T(8,128)(2,1)}, u32[]{:S(2)}) copy-start(bf16[1,2048,768]{2,1,0:T(8,128)(2,1)} %param.39) | copy-start | bytes 9437188
  302.4 68.6 %all-to-all-start.1 = ((bf16[128,5,2048]{2,1,0:T(8,128)(2,1)}), bf16[128,5,2048]{2,1,0:T(8,128)(2,1)}, u32[]{:S(2)}, u32[]{:S(2)}) async-start(bf16[128,5,2048]{2,1,0:T(8,128)(2,1)} %copy.79), calls=%async_computation.1 | async-start | bytes 8388608 | tf_op jit(solution)/shard_map/all_to_all | solution.py:119
  320.3 7.0 %copy-start.35 = (bf16[1,768,2048]{2,1,0:T(8,128)(2,1)S(1)}, bf16[1,768,2048]{2,1,0:T(8,128)(2,1)}, u32[]{:S(2)}) copy-start(bf16[1,768,2048]{2,1,0:T(8,128)(2,1)} %param.41) | copy-start | bytes 9437188
  371.1 56.7 %all-to-all-start.3 = ((bf16[128,5,2048]{2,1,0:T(8,128)(2,1)}), bf16[128,5,2048]{2,1,0:T(8,128)(2,1)}, u32[]{:S(2)}, u32[]{:S(2)}) async-start(bf16[128,5,2048]{2,1,0:T(8,128)(2,1)} %copy.81), calls=%async_computation.3 | async-start | bytes 8388608 | tf_op jit(solution)/shard_map/all_to_all | solution.py:119
  377.0 193.7 %all-gather.2.cloned.1.call-start = ((), (), s32[]{:S(2)}) async-start(), calls=%async_computation.9 | async-start | bytes 8912896 | tf_op jit(solution)/shard_map/all_gather | solution.py:154
  460.1 5.2 copy-start.5
  460.1 5.4 copy-start.15
  460.1 6.7 %copy-start.24 = (bf16[128,4096]{1,0:T(8,128)(2,1)S(1)}, bf16[128,4096]{1,0:T(8,128)(2,1)}, u32[]{:S(2)}) copy-start(bf16[128,4096]{1,0:T(8,128)(2,1)} %param.46) | copy-start | bytes 3145732
  467.4 34.3 %copy-start.29 = (bf16[128,512]{1,0:T(8,128)(2,1)S(1)}, bf16[128,512]{1,0:T(8,128)(2,1)}, u32[]{:S(2)}) copy-start(bf16[128,512]{1,0:T(8,128)(2,1)} %param.44) | copy-start | bytes 393220
  467.4 34.3 %copy-start.30 = (bf16[128,512]{1,0:T(8,128)(2,1)S(1)}, bf16[128,512]{1,0:T(8,128)(2,1)}, u32[]{:S(2)}) copy-start(bf16[128,512]{1,0:T(8,128)(2,1)} %param.45) | copy-start | bytes 393220
  468.8 28.8 %all-to-all-start.6 = ((bf16[128,16,256]{2,0,1:T(8,128)(2,1)}), bf16[128,16,256]{2,0,1:T(8,128)(2,1)S(1)}, u32[]{:S(2)}, u32[]{:S(2)}) async-start(bf16[128,16,256]{2,0,1:T(8,128)(2,1)} %copy.86), calls=%async_computation.6 | async-start | bytes 2097152 | tf_op jit(solution)/shard_map/all_to_all | solution.py:150
  473.5 31.1 %copy-start.32 = (f32[2,2048]{1,0:T(2,128)S(1)}, f32[2,2048]{1,0:T(2,128)}, u32[]{:S(2)}) copy-start(f32[2,2048]{1,0:T(2,128)} %param.47) | copy-start | bytes 49156
  497.5 29.3 %all-to-all-start.5 = ((bf16[128,16,256]{2,0,1:T(8,128)(2,1)}), bf16[128,16,256]{2,0,1:T(8,128)(2,1)S(1)}, u32[]{:S(2)}, u32[]{:S(2)}) async-start(bf16[128,16,256]{2,0,1:T(8,128)(2,1)} %bitcast.304), calls=%async_computation.5 | async-start | bytes 2097152 | tf_op jit(solution)/shard_map/all_to_all | solution.py:149
  526.8 28.8 %all-to-all-start.4 = ((bf16[128,16,256]{2,0,1:T(8,128)(2,1)}), bf16[128,16,256]{2,0,1:T(8,128)(2,1)S(1)}, u32[]{:S(2)}, u32[]{:S(2)}) async-start(bf16[128,16,256]{2,0,1:T(8,128)(2,1)} %all_to_all.74), calls=%async_computation.4 | async-start | bytes 2097152 | tf_op jit(solution)/shard_map/all_to_all | solution.py:151
  532.1 8.3 %copy-start.20 = (f32[4,128,256]{2,1,0:T(8,128)S(1)}, f32[4,128,256]{2,1,0:T(8,128)}, u32[]{:S(2)}) copy-start(f32[4,128,256]{2,1,0:T(8,128)} %get-tuple-element.124) | copy-start | bytes 1572868
  532.1 10.0 %copy-start.19 = (f32[4,128,256]{2,1,0:T(8,128)S(1)}, f32[4,128,256]{2,1,0:T(8,128)}, u32[]{:S(2)}) copy-start(f32[4,128,256]{2,1,0:T(8,128)} %get-tuple-element.123) | copy-start | bytes 1572868
  535.0 7.9 %copy-start.27 = (bf16[4,128,256]{2,1,0:T(8,128)(2,1)S(1)}, bf16[4,128,256]{2,1,0:T(8,128)(2,1)}, u32[]{:S(2)}) copy-start(bf16[4,128,256]{2,1,0:T(8,128)(2,1)} %get-tuple-element.131) | copy-start | bytes 786436
  542.9 23.3 %copy-start.11 = (bf16[1024,128]{1,0:T(8,128)(2,1)}, bf16[1024,128]{1,0:T(8,128)(2,1)S(1)}, u32[]{:S(2)}) copy-start(bf16[1024,128]{1,0:T(8,128)(2,1)S(1)} %reshape.499) | copy-start | bytes 786436
  555.6 10.7 %copy-start.7 = (bf16[128,16,256]{2,0,1:T(8,128)(2,1)}, bf16[128,16,256]{2,0,1:T(8,128)(2,1)S(1)}, u32[]{:S(2)}) copy-start(bf16[128,16,256]{2,0,1:T(8,128)(2,1)S(1)} %all-to-all-done.4) | copy-start | bytes 3145732
  570.8 7.1 %copy-start.18 = (f32[1024,128]{1,0:T(8,128)S(1)}, f32[1024,128]{1,0:T(8,128)}, u32[]{:S(2)}) copy-start(f32[1024,128]{1,0:T(8,128)} %reshape.503) | copy-start | bytes 1572868
  580.6 7.6 %copy-start.4 = (bf16[1024,512]{0,1:T(8,128)(2,1)}, bf16[1024,512]{0,1:T(8,128)(2,1)S(1)}, u32[]{:S(2)}) copy-start(bf16[1024,512]{0,1:T(8,128)(2,1)S(1)} %multiply_convert_fusion.3) | copy-start | bytes 3145732
  592.9 7.9 %slice-start = ((s8[6291456]{0:T(1024)(128)(4,1)}), s8[4194304]{0:T(1024)(128)(4,1)S(1)}, s32[]{:S(2)}) async-start(s8[6291456]{0:T(1024)(128)(4,1)} %bitcast.305), calls=%async_computation.10 | async-start | bytes 8388608
  592.9 9.3 %slice-start.2 = ((s8[8388608]{0:T(1024)(128)(4,1)}), s8[4194304]{0:T(1024)(128)(4,1)S(1)}, s32[]{:S(2)}) async-start(s8[8388608]{0:T(1024)(128)(4,1)} %bitcast.307), calls=%async_computation.12 | async-start | bytes 8388608
  596.5 5.6 slice-start.3
  610.9 18.1 %all-to-all-start.8 = ((bf16[16,128,256]{2,1,0:T(8,128)(2,1)}), bf16[16,128,256]{2,1,0:T(8,128)(2,1)}, u32[]{:S(2)}, u32[]{:S(2)}) async-start(bf16[16,128,256]{2,1,0:T(8,128)(2,1)} %pad_maximum_fusion.3), calls=%async_computation.8 | async-start | bytes 2097152 | tf_op jit(solution)/shard_map/all_to_all | solution.py:198
  621.8 4.8 copy-start.28
  629.0 19.4 %all-to-all-start.7 = ((bf16[16,128,256]{2,1,0:T(8,128)(2,1)}), bf16[16,128,256]{2,1,0:T(8,128)(2,1)}, u32[]{:S(2)}, u32[]{:S(2)}) async-start(bf16[16,128,256]{2,1,0:T(8,128)(2,1)} %bitcast.60), calls=%async_computation.7 | async-start | bytes 2097152 | tf_op jit(solution)/shard_map/all_to_all | solution.py:195
  635.0 17.9 %copy-start.1 = (bf16[1,2048,768]{2,1,0:T(8,128)(2,1)S(1)}, bf16[1,2048,768]{2,1,0:T(8,128)(2,1)}, u32[]{:S(2)}) copy-start(bf16[1,2048,768]{2,1,0:T(8,128)(2,1)} %param.40) | copy-start | bytes 9437188
  (19 other events, 57.4 us)
Sparse Core Ops, SparseCore 0:
  466.9 93.0 all-gather.1
where the time goes:
time: 670 us; the launch traced here: 660 us
  waiting for transfers between devices  178 us (27%)
  local copies, waits for them, and re-layouts  146 us (22%)
  matrix products  115 us (17%)
  blocking collectives  107 us (16%)
  starting transfers between devices  53.6 us (8%)
  other arithmetic  45.1 us (7%)
  between operations  15.4 us (2%)
    all_to_all x1, blocking collectives, grouped_exchange(): lax.all_to_all(group, axis, split_axis=split_dim, concat_axis=concat_dim,...  107 us
    all_to_all x2, waiting for transfers between devices, expert_work(): lax.all_to_all(expert_grads(arrived, w_gate, w_up, w_down), ('grp', 'inne...  65.7 us
    all_to_all x1, waiting for transfers between devices, grouped_exchange(): lax.all_to_all(group, axis, split_axis=split_dim, concat_axis=concat_dim,...  51.8 us
    dot_general x9, matrix products, contract_last(): lax.dot_general(left, right, (((1,), (1,)), ((), ())), preferred_element_...  33.4 us
    all_to_all x2, starting transfers between devices, expert_work(): lax.all_to_all(expert_grads(arrived, w_gate, w_up, w_down), ('grp', 'inne...  23.9 us
    dot_general x2, matrix products, expert_grads(): jnp.einsum('nlcf,ldf->nlcd', grad_up, w_up, preferred_element_type=jnp.fl...  22.7 us
    dot_general x2, matrix products, expert_grads(): jnp.einsum('nlcf,ldf->nlcd', grad_gate, w_gate, preferred_element_type=jn...  22.3 us
    all_to_all x1, waiting for transfers between devices, per_device(): lax.all_to_all(attn_out, 'inner', split_axis=1, concat_axis=0, tiled=True)  21.7 us
  transfers between devices with their start and end apart: 9, of which 8 were waited for; matrix products, arithmetic and copies ran while one was open for 21% of the time, Pallas kernels for 0%

commit v1 on v0

v1 whole, which is shorter than its diff:
```python
import functools
import math

import jax
import jax.numpy as jnp
from jax import lax
from jax.experimental import pallas as pl
from jax.experimental.pallas import tpu as pltpu
from jax.sharding import PartitionSpec as P

KEY_VALUE_HEADS = 4
HEAD_SIZE = 128
EPSILON = 1e-06
BLOCK = 512
HALVES = 2
DELTA_ROWS = 16


def dot_nn(left, right):
    return lax.dot_general(
        left, right, (((1,), (0,)), ((), ())), preferred_element_type=jnp.float32
    )


def contract_last(left, right):
    return lax.dot_general(
        left, right, (((1,), (1,)), ((), ())), preferred_element_type=jnp.float32
    )


def contract_first(left, right):
    return lax.dot_general(
        left, right, (((0,), (0,)), ((), ())), preferred_element_type=jnp.float32
    )


def project_kernel(resid_ref, weight_ref, output_ref, out_ref, *, head):
    parts, devices = weight_ref.shape[:2]
    piece = weight_ref.shape[3]
    total = None
    for part in range(parts):
        weight = weight_ref[part].reshape(devices * HEAD_SIZE, piece)
        term = contract_last(weight, resid_ref[:, part * piece : (part + 1) * piece])
        total = term if total is None else total + term
    head_width = output_ref.shape[1] // devices
    row_at = lax.broadcasted_iota(jnp.int32, (DELTA_ROWS, resid_ref.shape[0]), 0)
    for device in range(devices):
        grad = total[device * HEAD_SIZE : (device + 1) * HEAD_SIZE].astype(jnp.bfloat16)
        start = device * head_width + head * HEAD_SIZE
        output = output_ref[:, start : start + HEAD_SIZE].astype(jnp.float32).T
        rest = jnp.sum(grad.astype(jnp.float32) * output, axis=0, keepdims=True)
        held = jnp.zeros(row_at.shape, jnp.float32)
        for row in range(3):
            digit = rest.astype(jnp.bfloat16).astype(jnp.float32)
            held = jnp.where(row_at == row, digit, held)
            rest = rest - digit
        out_ref[device, :HEAD_SIZE] = grad
        out_ref[device, HEAD_SIZE:] = held.astype(jnp.bfloat16)


def project(resid, weights, attn_out, head):
    tokens, width = resid.shape
    parts, devices, heads, _, piece = weights.shape
    step = min(4, devices)
    head_rows = HEAD_SIZE + DELTA_ROWS
    return pl.pallas_call(
        functools.partial(project_kernel, head=head),
        grid=(devices // step,),
        in_specs=[
            pl.BlockSpec((tokens, width), lambda n: (0, 0)),
            pl.BlockSpec(
                (parts, step, None, HEAD_SIZE, piece), lambda n: (0, n, head, 0, 0)
            ),
            pl.BlockSpec((tokens, step * heads * HEAD_SIZE), lambda n: (0, n)),
        ],
        out_specs=pl.BlockSpec((step, head_rows, tokens), lambda n: (n, 0, 0)),
        out_shape=jax.ShapeDtypeStruct((devices, head_rows, tokens), jnp.bfloat16),
        cost_estimate=pl.CostEstimate(
            flops=2 * tokens * width * devices * HEAD_SIZE,
            bytes_accessed=2 * devices * HEAD_SIZE * (width + 3 * tokens),
            transcendentals=0,
        ),
    )(resid, weights, attn_out)


def attention_kernel(packed_ref, grad_ref, lse_ref, *refs, head, heads):
    last = head == heads - 1
    before_ref = refs[0] if head > 0 else None
    if last:
        out_ref, delta_ref, grad_t_ref, dqt_ref = refs[-4:]
    else:
        dquery_ref, dkv_ref, delta_ref, grad_t_ref, dqt_ref = refs[-5:]
    j = pl.program_id(0)
    steps = pl.num_programs(0)
    length = packed_ref.shape[0]
    devices, _, tokens = grad_ref.shape
    block = min(BLOCK, length)
    scale = float(HEAD_SIZE) ** (-0.5)
    log2e = math.log2(math.e)
    key_from = heads * HEAD_SIZE
    value_from = key_from + HEAD_SIZE
    query_cols = slice(head * HEAD_SIZE, (head + 1) * HEAD_SIZE)

    @pl.when(j == 0)
    def _():
        dqt_ref[...] = jnp.zeros_like(dqt_ref)
        for device in range(devices):
            cols = slice(device * tokens, (device + 1) * tokens)
            grad_t_ref[:, cols] = grad_ref[device, :HEAD_SIZE]
            digits = grad_ref[device, HEAD_SIZE:].astype(jnp.float32)
            delta_ref[:, cols] = jnp.broadcast_to(
                jnp.sum(digits, axis=0, keepdims=True), (8, tokens)
            )

    key_rows = pl.ds(pl.multiple_of(j * block, block), block)
    key = packed_ref[key_rows, key_from:value_from]
    value = packed_ref[key_rows, value_from : value_from + HEAD_SIZE]
    key_t = key.astype(jnp.float32).T.astype(jnp.bfloat16)

    def one(i, masked):
        rows = pl.ds(pl.multiple_of(i * block, block), block)
        query = packed_ref[rows, query_cols]
        grad_t = grad_t_ref[:, rows]
        lse = lse_ref[head : head + 1, rows] * log2e
        delta = delta_ref[0:1, rows]
        scores = contract_last(key, query)
        probs = jnp.exp2(scores * (scale * log2e) - lse)
        if masked:
            key_at = lax.broadcasted_iota(jnp.int32, scores.shape, 0)
            query_at = lax.broadcasted_iota(jnp.int32, scores.shape, 1)
            probs = jnp.where(key_at <= query_at, probs, 0.0)
        grad_probs = dot_nn(value, grad_t)
        grad_scores = (probs * (grad_probs - delta)).astype(jnp.bfloat16)
        dkey = dot_nn(grad_scores, query)
        dvalue = contract_last(probs.astype(jnp.bfloat16), grad_t)
        dqt_ref[:, rows] += dot_nn(key_t, grad_scores)
        return dkey, dvalue

    def body(i, carry):
        dkey, dvalue = one(i, False)
        return carry[0] + dkey, carry[1] + dvalue

    dkey, dvalue = lax.fori_loop(j + 1, steps, body, one(j, True))
    dkey = dkey * scale
    if before_ref is not None:
        dkey = dkey + before_ref[key_rows, :HEAD_SIZE]
        dvalue = dvalue + before_ref[key_rows, HEAD_SIZE:]
    if last:
        out_ref[key_rows, HEAD_SIZE : 2 * HEAD_SIZE] = dkey.astype(jnp.bfloat16)
        out_ref[key_rows, 2 * HEAD_SIZE :] = dvalue.astype(jnp.bfloat16)
    else:
        dkv_ref[key_rows, :HEAD_SIZE] = dkey
        dkv_ref[key_rows, HEAD_SIZE:] = dvalue

    @pl.when(j == steps - 1)
    def _():
        dquery = (dqt_ref[...].T * scale).astype(jnp.bfloat16)
        if last:
            out_ref[:, :HEAD_SIZE] = dquery
        else:
            dquery_ref[...] = dquery


def attention(packed, grad, lse, head, before):
    length, packed_width = packed.shape
    heads = lse.shape[0]
    last = head == heads - 1
    block = min(BLOCK, length)
    operands = [packed, grad, lse] + ([before] if head > 0 else [])

    def whole(shape):
        return pl.BlockSpec(shape, lambda j: (0,) * len(shape))

    if last:
        shapes = [jax.ShapeDtypeStruct((length, 3 * HEAD_SIZE), jnp.bfloat16)]
    else:
        shapes = [
            jax.ShapeDtypeStruct((length, HEAD_SIZE), jnp.bfloat16),
            jax.ShapeDtypeStruct((length, 2 * HEAD_SIZE), jnp.float32),
        ]
    return pl.pallas_call(
        functools.partial(attention_kernel, head=head, heads=heads),
        grid=(length // block,),
        in_specs=[whole(operand.shape) for operand in operands],
        out_specs=[whole(shape.shape) for shape in shapes],
        out_shape=shapes,
        scratch_shapes=[
            pltpu.VMEM((8, length), jnp.float32),
            pltpu.VMEM((HEAD_SIZE, length), jnp.bfloat16),
            pltpu.VMEM((HEAD_SIZE, length), jnp.float32),
        ],
        compiler_params=pltpu.CompilerParams(
            dimension_semantics=("arbitrary",), vmem_limit_bytes=48 * 1024 * 1024
        ),
        cost_estimate=pl.CostEstimate(
            flops=10 * length * length * HEAD_SIZE // 2,
            bytes_accessed=2 * length * (packed_width + 6 * HEAD_SIZE),
            transcendentals=length * length // 2,
        ),
    )(*operands)


def per_device(
    grad_out,
    hidden,
    norm_gain,
    expert_ids,
    gate_weights,
    w_gate,
    w_up,
    w_down,
    w_out,
    queries,
    keys,
    values,
    attn_out,
    lse,
):
    bf16, f32 = jnp.bfloat16, jnp.float32
    rows, width = hidden.shape
    topk = expert_ids.shape[1]
    groups = lax.axis_size("grp")
    inner = lax.axis_size("inner")
    grp_at = lax.axis_index("grp")
    experts = groups * inner
    capacity = max(2, 5 * rows * topk // (4 * experts))
    slots = groups * capacity
    column = groups * rows
    ff = w_gate.shape[2]
    head_width = queries.shape[1] // inner
    shared = inner // KEY_VALUE_HEADS

    hidden_f = hidden.astype(f32)
    inverse = lax.rsqrt(jnp.mean(hidden_f * hidden_f, axis=1, keepdims=True) + EPSILON)
    normed = (hidden_f * inverse * norm_gain).astype(bf16)

    normed_all = lax.all_gather(normed, "grp", axis=0, tiled=True)
    upstream_all = lax.all_gather(grad_out, "grp", axis=0, tiled=True)
    routing = jnp.concatenate([expert_ids.astype(f32).T, gate_weights.T], axis=0)
    routing = lax.all_gather(routing, "grp", axis=0, tiled=False)

    piece = width // groups
    w_piece = lax.dynamic_slice_in_dim(w_out, grp_at * piece, piece, axis=1)
    w_piece = lax.all_to_all(
        jnp.broadcast_to(w_piece[None], (inner,) + w_piece.shape), "inner", 0, 0, tiled=True
    )
    normed_all, w_piece = lax.optimization_barrier((normed_all, w_piece))
    w_whole = lax.all_gather(w_piece, "grp", axis=0, tiled=False)
    w_whole = w_whole.reshape(groups, inner, head_width // HEAD_SIZE, HEAD_SIZE, piece)

    kv = jnp.stack(
        [
            keys.reshape(rows, KEY_VALUE_HEADS, HEAD_SIZE),
            values.reshape(rows, KEY_VALUE_HEADS, HEAD_SIZE),
        ],
        axis=2,
    ).reshape(rows, KEY_VALUE_HEADS, 2 * HEAD_SIZE)
    kv = jnp.repeat(kv.transpose(1, 0, 2), shared, axis=0)
    packed = jnp.concatenate(
        [queries.reshape(rows, inner, head_width).transpose(1, 0, 2), kv], axis=2
    )

    ids_all = routing[:, :topk]
    gates_all = routing[:, topk:]
    mine = (grp_at * inner + lax.broadcasted_iota(jnp.int32, (1, inner, 1, 1), 1)).astype(f32)
    match = ids_all[:, None] == mine
    named = jnp.any(match, axis=2)
    gate = jnp.sum(jnp.where(match, gates_all[:, None], 0.0), axis=2)
    before = (
        lax.broadcasted_iota(jnp.int32, (rows, rows), 0)
        < lax.broadcasted_iota(jnp.int32, (rows, rows), 1)
    ).astype(bf16)
    rank = dot_nn(named.astype(bf16).reshape(groups * inner, rows), before)
    rank = rank.reshape(groups, inner, rows)
    block_at = lax.broadcasted_iota(jnp.int32, (groups, 1, 1), 0).astype(f32)
    slot = jnp.where(named, block_at * capacity + rank, -1.0)
    slot = slot.transpose(1, 0, 2).reshape(inner, 1, column)
    gate = gate.transpose(1, 0, 2).reshape(inner, 1, column)
    slot_at = lax.broadcasted_iota(jnp.int32, (1, slots, 1), 1).astype(f32)
    chosen = slot == slot_at
    picks = chosen.astype(bf16).reshape(inner * slots, column)
    slot_gate = jnp.sum(jnp.where(chosen, gate, 0.0), axis=2).reshape(inner * slots, 1)

    def to_experts(array):
        array = array.astype(bf16).reshape(inner, slots, width)
        return lax.all_to_all(array, "inner", 0, 0, tiled=True).reshape(inner * slots, width)

    w_gate_up = jnp.concatenate([w_gate[0], w_up[0]], axis=1)
    inputs = to_experts(dot_nn(picks, normed_all))
    upstream_rows = to_experts(dot_nn(picks, upstream_all) * slot_gate)
    upstream_rows, w_whole, packed = lax.optimization_barrier((upstream_rows, w_whole, packed))
    pre = dot_nn(inputs, w_gate_up)
    gate_pre = pre[:, :ff]
    up_pre = pre[:, ff:]
    back_hidden = contract_last(upstream_rows, w_down[0])
    sigmoid = jax.nn.sigmoid(gate_pre)
    grad_gate = (back_hidden * up_pre * sigmoid * (1.0 + gate_pre * (1.0 - sigmoid))).astype(bf16)
    grad_up = (back_hidden * gate_pre * sigmoid).astype(bf16)
    grad_both = jnp.concatenate([grad_gate, grad_up], axis=1)

    half = width // HALVES
    sums = []
    for part in range(HALVES):
        grads = contract_last(grad_both, w_gate_up[part * half : (part + 1) * half])
        grads = grads.astype(bf16).reshape(inner, slots, half)
        grads = lax.all_to_all(grads, "inner", 0, 0, tiled=True).reshape(inner * slots, half)
        partial = contract_first(picks, grads).astype(bf16)
        sums.append(lax.psum_scatter(partial, "grp", scatter_dimension=0, tiled=True))

    packed, _ = lax.optimization_barrier((packed, partial))
    packed = lax.all_to_all(packed, "inner", 0, 0, tiled=True)
    packed = packed.reshape(inner * rows, head_width + 2 * HEAD_SIZE)
    packed, sums = lax.optimization_barrier((packed, sums))

    grad_normed = jnp.concatenate(sums, axis=1).astype(f32)

    gained = grad_normed * norm_gain
    statistic = jnp.mean(gained * hidden_f, axis=1, keepdims=True)
    grad_resid = (
        grad_out.astype(f32)
        + inverse * gained
        - hidden_f * inverse * inverse * inverse * statistic
    ).astype(bf16)

    heads = lse.shape[0]
    grads = []
    for head in range(heads):
        grad = project(grad_resid, w_whole, attn_out, head)
        grads.append(lax.all_to_all(grad, "inner", 0, 0, tiled=True))
    dkv = None
    token_query = []
    for head in range(heads - 1):
        dquery, dkv = attention(packed, grads[head], lse, head, dkv)
        dquery, grads[head + 1] = lax.optimization_barrier((dquery, grads[head + 1]))
        dquery = dquery.reshape(inner, rows, HEAD_SIZE)
        token_query.append(lax.all_to_all(dquery, "inner", 0, 0, tiled=True))
    (packed_grads,) = attention(packed, grads[-1], lse, heads - 1, dkv)
    packed_grads, token_query = lax.optimization_barrier((packed_grads, token_query))
    packed_grads = packed_grads.reshape(inner, rows, 3 * HEAD_SIZE)
    packed_grads = lax.all_to_all(packed_grads, "inner", 0, 0, tiled=True)
    token_query.append(packed_grads[:, :, :HEAD_SIZE])
    token_kv = packed_grads[:, :, HEAD_SIZE:]
    queries_gradient = jnp.concatenate(token_query, axis=2).transpose(1, 0, 2)
    queries_gradient = queries_gradient.reshape(rows, inner * head_width)
    totals = jnp.sum(
        token_kv.reshape(KEY_VALUE_HEADS, shared, rows, 2 * HEAD_SIZE).astype(f32), axis=1
    ).astype(bf16)
    kv_width = KEY_VALUE_HEADS * HEAD_SIZE
    keys_gradient = totals[:, :, :HEAD_SIZE].transpose(1, 0, 2).reshape(rows, kv_width)
    values_gradient = totals[:, :, HEAD_SIZE:].transpose(1, 0, 2).reshape(rows, kv_width)
    return (grad_resid, queries_gradient, keys_gradient, values_gradient)


def solution(mesh):
    token = P(("grp", "inner"), None)
    expert = P(("grp", "inner"), None, None)
    placed = (
        token,
        token,
        P(),
        token,
        token,
        expert,
        expert,
        expert,
        P("inner", None),
        token,
        token,
        token,
        token,
        P("inner", "grp"),
    )

    return jax.shard_map(
        per_device,
        mesh=mesh,
        in_specs=placed,
        out_specs=(token, token, token, token),
        check_vma=False,
    )
```

time: 670 us -> 487 us (0.73)
  the two profiles are of different devices: /device:TPU:0 before, /device:TPU:24 now
where the time goes in v1:
time: 487 us; the launch traced here: 479 us
  blocking collectives  182 us (37%)
  waiting for transfers between devices  137 us (28%)
  matrix products  62.5 us (13%)
  Pallas kernels  33.1 us (7%)
  starting transfers between devices  25.9 us (5%)
  between operations  14.5 us (3%)
  other arithmetic  12.5 us (3%)
  local copies, waits for them, and re-layouts  12.2 us (3%)
    all_to_all x2, waiting for transfers between devices, to_experts(): lax.all_to_all(array, 'inner', 0, 0, tiled=True)  127 us
    all_to_all x2, blocking collectives, per_device(): lax.all_to_all(grads, 'inner', 0, 0, tiled=True)  73.7 us
    all_to_all x1, blocking collectives, per_device(): lax.all_to_all(jnp.broadcast_to(w_piece[None], (inner,) + w_piece.shape),...  36.2 us
    dot_general x4, matrix products, dot_nn(): lax.dot_general(left, right, (((1,), (0,)), ((), ())), preferred_element_...  33.2 us
    all_to_all x1, blocking collectives, per_device(): packed_grads = lax.all_to_all(packed_grads, 'inner', 0, 0, tiled=True)  29.8 us
    all_to_all x1, blocking collectives, per_device(): packed = lax.all_to_all(packed, 'inner', 0, 0, tiled=True)  29.3 us
    dot_general x3, matrix products, contract_last(): lax.dot_general(left, right, (((1,), (1,)), ((), ())), preferred_element_...  20.8 us
    pallas_call x2, Pallas kernels, attention(): pl.pallas_call(functools.partial(attention_kernel, head=head, heads=heads...  20.1 us
  transfers between devices with their start and end apart: 10, of which 4 were waited for; matrix products, arithmetic and copies ran while one was open for 11% of the time, Pallas kernels for 6%

profile of v1, /device:TPU:24, one launch (start us, length us, event | category | flops | bytes accessed | tf_op | source)
XLA Modules:
  0.0 479.3 jit_solution(11491058295336168808)
XLA Ops:
  7.2 1.4 fusion.32
  8.6 2.0 fusion.27
  12.6 36.2 %all_to_all.50 = bf16[16,256,256]{2,1,0:T(8,128)(2,1)} all-to-all(bf16[16,256,256]{2,1,0:T(8,128)(2,1)S(1)} %broadcast_in_dim.51), channel_id=1, replica_groups=mesh['grp'=8,'inner'=16] {'inner'}, dimensions={0} | all-to-all | bytes 4194304 | tf_op jit(solution)/shard_map/all_to_all | solution.py:244
  49.0 12.9 %all-gather = f32[128,128]{1,0:T(8,128)S(1)} all-gather(f32[16,128]{1,0:T(8,128)S(1)} %pad_maximum_fusion.8), channel_id=2, replica_groups=mesh['grp'=8,'inner'=16] {'grp'}, dimensions={0}, use_global_device_ids=true | all-gather | bytes 73728 | tf_op jit(solution)/shard_map/all_gather | solution.py:240
  63.1 10.1 %convolution_convert_fusion = bf16[1280,2048]{1,0:T(8,128)(2,1)} fusion(pred[1280,1024]{1,0:T(32,128)(4,1)S(1)} %bitcast_compare_fusion, bf16[1024,2048]{1,0:T(8,128)(2,1)} %all-gather.8.cloned.1.call-done), kind=kOutput, calls=%fused_computation.11 | convolution fusion | flops 5371330560 | bytes 10747904 | tf_op jit(solution)/shard_map/dot_general | solution.py:20
  73.1 4.6 all-to-all-start.2
  78.8 9.6 %multiply_convert_fusion = bf16[1280,2048]{1,0:T(8,128)(2,1)} fusion(pred[1280,1024]{1,0:T(32,128)(4,1)} %copy-done.8, bf16[1024,2048]{1,0:T(8,128)(2,1)} %all-gather.6.cloned.1.call-done, f32[1280]{0:T(1024)S(1)} %mul.104), kind=kOutput, calls=%fused_computation | convolution fusion | flops 5373952000 | bytes 10753024 | tf_op jit(solution)/shard_map/dot_general | solution.py:20
  88.4 69.9 %all-to-all-done.2 = bf16[16,80,2048]{2,1,0:T(8,128)(2,1)} async-done(((bf16[16,80,2048]{2,1,0:T(8,128)(2,1)}), bf16[16,80,2048]{2,1,0:T(8,128)(2,1)}, u32[]{:S(2)}, u32[]{:S(2)}) %all-to-all-start.2) | async-done | bytes 5242912 | tf_op jit(solution)/shard_map/all_to_all | solution.py:286
  158.3 4.7 all-to-all-start
  166.6 1.5 copy.83
  168.1 1.6 pad_maximum_fusion.5
  170.5 13.4 %fusion.4 = f32[1280,1536]{0,1:T(8,128)} fusion(bf16[1280,2048]{1,0:T(8,128)(2,1)} %bitcast.18, bf16[2048,768]{1,0:T(8,128)(2,1)S(1)} %bitcast.105, bf16[2048,768]{1,0:T(8,128)(2,1)S(1)} %bitcast.102), kind=kOutput, calls=%fused_computation.12 | convolution fusion | flops 8065646592 | bytes 19398656 | tf_op jit(solution)/shard_map/dot_general | solution.py:20
  183.8 57.3 %all-to-all-done = bf16[16,80,2048]{2,1,0:T(8,128)(2,1)} async-done(((bf16[16,80,2048]{2,1,0:T(8,128)(2,1)}), bf16[16,80,2048]{2,1,0:T(8,128)(2,1)}, u32[]{:S(2)}, u32[]{:S(2)}) %all-to-all-start) | async-done | bytes 5242912 | tf_op jit(solution)/shard_map/all_to_all | solution.py:286
  241.2 9.2 %fusion.8 = (bf16[1280,768]{0,1:T(8,128)(2,1)S(1)}, bf16[1280,768]{0,1:T(8,128)(2,1)S(1)}) fusion(f32[1280,1536]{0,1:T(8,128)} %fusion.4, bf16[1280,2048]{1,0:T(8,128)(2,1)} %bitcast.8, bf16[1,768,2048]{2,1,0:T(8,128)(2,1)S(1)} %copy-done), kind=kOutput, calls=%fused_computation.20 | convolution fusion | flops 4039311360 | bytes 20185088 | tf_op jit(solution)/shard_map/dot_general | solution.py:26
  250.4 4.3 convolution_convert_fusion.1
  254.7 38.7 %all_to_all.51 = bf16[16,80,1024]{2,1,0:T(8,128)(2,1)S(1)} all-to-all(bf16[16,80,1024]{2,1,0:T(8,128)(2,1)S(1)} %bitcast.87), channel_id=1, replica_groups=mesh['grp'=8,'inner'=16] {'inner'}, dimensions={0} | all-to-all | bytes 5242880 | tf_op jit(solution)/shard_map/all_to_all | solution.py:306
  293.4 4.3 bitcast_convert_fusion
  297.7 7.4 %convolution_convert_fusion.2 = bf16[1280,1024]{1,0:T(8,128)(2,1)S(1)} fusion(bf16[2048,768]{1,0:T(8,128)(2,1)} %bitcast.101, bf16[2048,768]{1,0:T(8,128)(2,1)} %bitcast.104, bf16[1280,768]{0,1:T(8,128)(2,1)} %copy-done.18, bf16[1280,768]{0,1:T(8,128)(2,1)} %copy-done.17), kind=kOutput, calls=%fused_computation.25 | convolution fusion | flops 4041998336 | bytes 12845056 | tf_op jit(solution)/shard_map/dot_general | solution.py:26
  305.1 35.1 %all_to_all.52 = bf16[16,80,1024]{2,1,0:T(8,128)(2,1)S(1)} all-to-all(bf16[16,80,1024]{2,1,0:T(8,128)(2,1)S(1)} %bitcast.86), channel_id=1, replica_groups=mesh['grp'=8,'inner'=16] {'inner'}, dimensions={0} | all-to-all | bytes 5242880 | tf_op jit(solution)/shard_map/all_to_all | solution.py:306
  340.1 4.3 bitcast_convert_fusion.1
  344.4 29.3 %all_to_all.53 = bf16[16,128,512]{2,1,0:T(8,128)(2,1)S(1)} all-to-all(bf16[16,128,512]{2,1,0:T(8,128)(2,1)} %pad_maximum_fusion.5), channel_id=1, replica_groups=mesh['grp'=8,'inner'=16] {'inner'}, dimensions={0} | all-to-all | bytes 4194304 | tf_op jit(solution)/shard_map/all_to_all | solution.py:311
  375.1 2.3 fusion.31.resid_ref
  377.3 6.5 %shard_map.165 = bf16[16,144,128]{2,1,0:T(8,128)(2,1)} custom-call(bf16[128,2048]{1,0:T(8,128)(2,1)} %fusion.31.resid_ref, bf16[8,16,2,128,256]{4,3,2,1,0:T(8,128)(2,1)} %bitcast.80, bf16[128,4096]{1,0:T(8,128)(2,1)} %output_ref.3), custom_call_target="tpu_custom_call" | custom-call | flops 1073741824 | bytes 9961472 | tf_op jit(solution)/shard_map/pallas_call | solution.py:66
  383.8 5.8 %all-to-all-start.6 = ((bf16[16,144,128]{2,1,0:T(8,128)(2,1)}), bf16[16,144,128]{2,1,0:T(8,128)(2,1)S(1)}, u32[]{:S(2)}, u32[]{:S(2)}) async-start(bf16[16,144,128]{2,1,0:T(8,128)(2,1)} %shard_map.165), calls=%async_computation.8 | async-start | bytes 1179648 | tf_op jit(solution)/shard_map/all_to_all | solution.py:329
  389.7 6.5 %shard_map.167 = bf16[16,144,128]{2,1,0:T(8,128)(2,1)} custom-call(bf16[128,2048]{1,0:T(8,128)(2,1)} %fusion.31.resid_ref, bf16[8,16,2,128,256]{4,3,2,1,0:T(8,128)(2,1)} %bitcast.81, bf16[128,4096]{1,0:T(8,128)(2,1)} %output_ref.3), custom_call_target="tpu_custom_call" | custom-call | flops 1073741824 | bytes 9961472 | tf_op jit(solution)/shard_map/pallas_call | solution.py:66
  396.2 7.1 %all-to-all-done.6.grad_ref = bf16[16,144,128]{2,1,0:T(8,128)(2,1)S(1)} async-done(((bf16[16,144,128]{2,1,0:T(8,128)(2,1)}), bf16[16,144,128]{2,1,0:T(8,128)(2,1)S(1)}, u32[]{:S(2)}, u32[]{:S(2)}) %all-to-all-start.6) | async-done | bytes 589856 | tf_op jit(solution)/shard_map/all_to_all | solution.py:329
  403.3 4.2 all-to-all-start.7
  407.5 9.1 %shard_map.166 = (bf16[2048,128]{1,0:T(8,128)(2,1)S(1)}, f32[2048,256]{1,0:T(8,128)S(1)}) custom-call(bf16[2048,512]{1,0:T(8,128)(2,1)S(1)} %bitcast.76, bf16[16,144,128]{2,1,0:T(8,128)(2,1)S(1)} %all-to-all-done.6.grad_ref, f32[2,2048]{1,0:T(2,128)S(1)} %copy-done.4), custom_call_target="tpu_custom_call" | custom-call | flops 2684354560 | bytes 5242880 | tf_op jit(solution)/shard_map/pallas_call | solution.py:181
  418.8 1.5 all-to-all-done.7.grad_ref
  420.3 5.8 %all-to-all-start.8 = ((bf16[16,128,128]{2,1,0:T(8,128)(2,1)}), bf16[16,128,128]{2,1,0:T(8,128)(2,1)}, u32[]{:S(2)}, u32[]{:S(2)}) async-start(bf16[16,128,128]{2,1,0:T(8,128)(2,1)} %bitcast.79), calls=%async_computation.10 | async-start | bytes 1048576 | tf_op jit(solution)/shard_map/all_to_all | solution.py:336
  426.2 11.0 %shard_map.168 = bf16[2048,384]{1,0:T(8,128)(2,1)S(1)} custom-call(bf16[2048,512]{1,0:T(8,128)(2,1)S(1)} %bitcast.77, bf16[16,144,128]{2,1,0:T(8,128)(2,1)} %all-to-all-done.7.grad_ref, f32[2,2048]{1,0:T(2,128)S(1)} %copy-done.4, f32[2048,256]{1,0:T(8,128)} %copy-done.5), custom_call_target="tpu_custom_call" | custom-call | flops 2684354560 | bytes 5242880 | tf_op jit(solution)/shard_map/pallas_call | solution.py:181
  438.4 29.8 %all_to_all.54 = bf16[16,128,384]{2,1,0:T(8,128)(2,1)S(1)} all-to-all(bf16[16,128,384]{2,1,0:T(8,128)(2,1)} %bitcast.78), channel_id=1, replica_groups=mesh['grp'=8,'inner'=16] {'inner'}, dimensions={0} | all-to-all | bytes 3145728 | tf_op jit(solution)/shard_map/all_to_all | solution.py:340
  (89 shorter events, 17.6 us)
Async XLA Ops:
  7.2 234.0 %copy-start = (bf16[1,768,2048]{2,1,0:T(8,128)(2,1)S(1)}, bf16[1,768,2048]{2,1,0:T(8,128)(2,1)}, u32[]{:S(2)}) copy-start(bf16[1,768,2048]{2,1,0:T(8,128)(2,1)} %param.21) | copy-start | bytes 9437188
  7.2 41.6 %all-gather.8.cloned.1.call-start = ((), (), s32[]{:S(2)}) async-start(), calls=%async_computation.13 | async-start | bytes 4718592 | tf_op jit(solution)/shard_map/all_gather | solution.py:237
  10.7 68.1 %all-gather.6.cloned.1.call-start = ((), (), s32[]{:S(2)}) async-start(), calls=%async_computation.12 | async-start | bytes 4718592 | tf_op jit(solution)/shard_map/all_gather | solution.py:238
  11.4 229.7 %all-gather.10.cloned.1.call-start = ((), (), s32[]{:S(2)}) async-start(), calls=%async_computation.16 | async-start | bytes 18874368 | tf_op jit(solution)/shard_map/all_gather | solution.py:248
  12.4 36.5 %copy-start.11 = (s32[128,8]{0,1:T(8,128)S(1)}, s32[128,8]{0,1:T(8,128)}, u32[]{:S(2)}) copy-start(s32[128,8]{0,1:T(8,128)} %param.17) | copy-start | bytes 12292
  12.4 36.5 %copy-start.12 = (f32[128,8]{0,1:T(8,128)S(1)}, f32[128,8]{0,1:T(8,128)}, u32[]{:S(2)}) copy-start(f32[128,8]{0,1:T(8,128)} %param.18) | copy-start | bytes 12292
  63.1 10.1 %copy-start.8 = (pred[1280,1024]{1,0:T(32,128)(4,1)}, pred[1280,1024]{1,0:T(32,128)(4,1)S(1)}, u32[]{:S(2)}) copy-start(pred[1280,1024]{1,0:T(32,128)(4,1)S(1)} %bitcast_compare_fusion) | copy-start | bytes 3932164
  73.1 85.2 %all-to-all-start.2 = ((bf16[16,80,2048]{2,1,0:T(8,128)(2,1)}), bf16[16,80,2048]{2,1,0:T(8,128)(2,1)}, u32[]{:S(2)}, u32[]{:S(2)}) async-start(bf16[16,80,2048]{2,1,0:T(8,128)(2,1)} %bitcast.83), calls=%async_computation.2 | async-start | bytes 10485760 | tf_op jit(solution)/shard_map/all_to_all | solution.py:286
  158.3 5.2 %copy-start.9 = (bf16[128,512]{1,0:T(8,128)(2,1)S(1)}, bf16[128,512]{1,0:T(8,128)(2,1)}, u32[]{:S(2)}) copy-start(bf16[128,512]{1,0:T(8,128)(2,1)} %param.24) | copy-start | bytes 393220
  158.3 82.9 %all-to-all-start = ((bf16[16,80,2048]{2,1,0:T(8,128)(2,1)}), bf16[16,80,2048]{2,1,0:T(8,128)(2,1)}, u32[]{:S(2)}, u32[]{:S(2)}) async-start(bf16[16,80,2048]{2,1,0:T(8,128)(2,1)} %bitcast.82), calls=%async_computation | async-start | bytes 10485760 | tf_op jit(solution)/shard_map/all_to_all | solution.py:286
  163.0 210.7 %reduce-scatter.3.cloned.1.call-start = ((), (), s32[]{:S(2)}) async-start(), calls=%async_computation.14 | async-start | bytes 2359296 | tf_op jit(solution)/shard_map/reduce_scatter | solution.py:308
  166.5 3.2 copy-start.13
  166.5 3.9 copy-start.15
  241.2 9.2 %copy-start.14 = (bf16[1,2048,768]{2,1,0:T(8,128)(2,1)S(1)}, bf16[1,2048,768]{2,1,0:T(8,128)(2,1)}, u32[]{:S(2)}) copy-start(bf16[1,2048,768]{2,1,0:T(8,128)(2,1)} %param.19) | copy-start | bytes 9437188
  241.2 9.2 %copy-start.16 = (bf16[1,2048,768]{2,1,0:T(8,128)(2,1)S(1)}, bf16[1,2048,768]{2,1,0:T(8,128)(2,1)}, u32[]{:S(2)}) copy-start(bf16[1,2048,768]{2,1,0:T(8,128)(2,1)} %param.20) | copy-start | bytes 9437188
  250.3 4.3 copy-start.17
  250.3 4.3 copy-start.18
  297.7 76.1 %reduce-scatter.5.cloned.1.call-start = ((), (), s32[]{:S(2)}) async-start(), calls=%async_computation.15 | async-start | bytes 2359296 | tf_op jit(solution)/shard_map/reduce_scatter | solution.py:308
  344.4 29.4 %copy-start.6 = (bf16[128,2048]{1,0:T(8,128)(2,1)S(1)}, bf16[128,2048]{1,0:T(8,128)(2,1)}, u32[]{:S(2)}) copy-start(bf16[128,2048]{1,0:T(8,128)(2,1)} %param.15) | copy-start | bytes 1572868
  344.4 29.4 %copy-start.10 = (f32[2048]{0:T(1024)S(1)}, f32[2048]{0:T(1024)}, u32[]{:S(2)}) copy-start(f32[2048]{0:T(1024)} %param.16) | copy-start | bytes 24580
  344.4 30.7 %copy-start.7 = (bf16[128,2048]{1,0:T(8,128)(2,1)S(1)}, bf16[128,2048]{1,0:T(8,128)(2,1)}, u32[]{:S(2)}) copy-start(bf16[128,2048]{1,0:T(8,128)(2,1)} %param.14) | copy-start | bytes 1572868
  383.8 19.4 %all-to-all-start.6 = ((bf16[16,144,128]{2,1,0:T(8,128)(2,1)}), bf16[16,144,128]{2,1,0:T(8,128)(2,1)S(1)}, u32[]{:S(2)}, u32[]{:S(2)}) async-start(bf16[16,144,128]{2,1,0:T(8,128)(2,1)} %shard_map.165), calls=%async_computation.8 | async-start | bytes 1179648 | tf_op jit(solution)/shard_map/all_to_all | solution.py:329
  389.6 17.9 %copy-start.4 = (f32[2,2048]{1,0:T(2,128)S(1)}, f32[2,2048]{1,0:T(2,128)}, u32[]{:S(2)}) copy-start(f32[2,2048]{1,0:T(2,128)} %lse_ref.3) | copy-start | bytes 49156
  403.3 17.1 %all-to-all-start.7 = ((bf16[16,144,128]{2,1,0:T(8,128)(2,1)}), bf16[16,144,128]{2,1,0:T(8,128)(2,1)}, u32[]{:S(2)}, u32[]{:S(2)}) async-start(bf16[16,144,128]{2,1,0:T(8,128)(2,1)} %shard_map.167), calls=%async_computation.9 | async-start | bytes 1179648 | tf_op jit(solution)/shard_map/all_to_all | solution.py:329
  416.6 0.8 copy-start.3
  417.5 1.3 copy-start.5
  420.3 18.0 %all-to-all-start.8 = ((bf16[16,128,128]{2,1,0:T(8,128)(2,1)}), bf16[16,128,128]{2,1,0:T(8,128)(2,1)}, u32[]{:S(2)}, u32[]{:S(2)}) async-start(bf16[16,128,128]{2,1,0:T(8,128)(2,1)} %bitcast.79), calls=%async_computation.10 | async-start | bytes 1048576 | tf_op jit(solution)/shard_map/all_to_all | solution.py:336
  437.2 1.2 copy-start.2
  438.4 34.2 %copy-start.1 = (bf16[1,768,2048]{2,1,0:T(8,128)(2,1)S(1)}, bf16[1,768,2048]{2,1,0:T(8,128)(2,1)}, u32[]{:S(2)}) copy-start(bf16[1,768,2048]{2,1,0:T(8,128)(2,1)} %param.21) | copy-start | bytes 9437188
Sparse Core Ops, SparseCore 0:
  10.8 32.2 all-gather.7
  44.8 32.0 all-gather.5
  78.6 85.1 all-gather.9
  297.8 27.8 reduce-scatter.2
  344.5 28.2 reduce-scatter.4

commit v2 on v1

--- a/solution.py
+++ b/solution.py
@@ -117,7 +117,7 @@
     value = packed_ref[key_rows, value_from : value_from + HEAD_SIZE]
     key_t = key.astype(jnp.float32).T.astype(jnp.bfloat16)
 
-    def one(i, masked):
+    def one(i):
         rows = pl.ds(pl.multiple_of(i * block, block), block)
         query = packed_ref[rows, query_cols]
         grad_t = grad_t_ref[:, rows]
@@ -125,10 +125,9 @@
         delta = delta_ref[0:1, rows]
         scores = contract_last(key, query)
         probs = jnp.exp2(scores * (scale * log2e) - lse)
-        if masked:
-            key_at = lax.broadcasted_iota(jnp.int32, scores.shape, 0)
-            query_at = lax.broadcasted_iota(jnp.int32, scores.shape, 1)
-            probs = jnp.where(key_at <= query_at, probs, 0.0)
+        key_at = j * block + lax.broadcasted_iota(jnp.int32, scores.shape, 0)
+        query_at = i * block + lax.broadcasted_iota(jnp.int32, scores.shape, 1)
+        probs = jnp.where(key_at <= query_at, probs, 0.0)
         grad_probs = dot_nn(value, grad_t)
         grad_scores = (probs * (grad_probs - delta)).astype(jnp.bfloat16)
         dkey = dot_nn(grad_scores, query)
@@ -137,10 +136,11 @@
         return dkey, dvalue
 
     def body(i, carry):
-        dkey, dvalue = one(i, False)
+        dkey, dvalue = one(i)
         return carry[0] + dkey, carry[1] + dvalue
 
-    dkey, dvalue = lax.fori_loop(j + 1, steps, body, one(j, True))
+    zero = jnp.zeros((block, HEAD_SIZE), jnp.float32)
+    dkey, dvalue = lax.fori_loop(j, steps, body, (zero, zero))
     dkey = dkey * scale
     if before_ref is not None:
         dkey = dkey + before_ref[key_rows, :HEAD_SIZE]
@@ -241,9 +241,8 @@
 
     piece = width // groups
     w_piece = lax.dynamic_slice_in_dim(w_out, grp_at * piece, piece, axis=1)
-    w_piece = lax.all_to_all(
-        jnp.broadcast_to(w_piece[None], (inner,) + w_piece.shape), "inner", 0, 0, tiled=True
-    )
+    w_piece = jnp.broadcast_to(w_piece[None], (inner,) + w_piece.shape)
+    w_piece = lax.all_to_all(w_piece, "inner", 0, 0, tiled=True)
     normed_all, w_piece = lax.optimization_barrier((normed_all, w_piece))
     w_whole = lax.all_gather(w_piece, "grp", axis=0, tiled=False)
     w_whole = w_whole.reshape(groups, inner, head_width // HEAD_SIZE, HEAD_SIZE, piece)
@@ -278,7 +277,8 @@
     gate = gate.transpose(1, 0, 2).reshape(inner, 1, column)
     slot_at = lax.broadcasted_iota(jnp.int32, (1, slots, 1), 1).astype(f32)
     chosen = slot == slot_at
-    picks = chosen.astype(bf16).reshape(inner * slots, column)
+    picks = jnp.where(slot == slot_at, 1.0, 0.0).astype(bf16).reshape(inner * slots, column)
+    picks = lax.optimization_barrier(picks)
     slot_gate = jnp.sum(jnp.where(chosen, gate, 0.0), axis=2).reshape(inner * slots, 1)
 
     def to_experts(array):
@@ -288,24 +288,42 @@
     w_gate_up = jnp.concatenate([w_gate[0], w_up[0]], axis=1)
     inputs = to_experts(dot_nn(picks, normed_all))
     upstream_rows = to_experts(dot_nn(picks, upstream_all) * slot_gate)
-    upstream_rows, w_whole, packed = lax.optimization_barrier((upstream_rows, w_whole, packed))
     pre = dot_nn(inputs, w_gate_up)
     gate_pre = pre[:, :ff]
     up_pre = pre[:, ff:]
+    sigmoid = jax.nn.sigmoid(gate_pre)
+    gate_slope = up_pre * sigmoid * (1.0 + gate_pre * (1.0 - sigmoid))
+    up_slope = gate_pre * sigmoid
+    half = width // HALVES
+    w_halves = [
+        jnp.concatenate([w[0, part * half : (part + 1) * half] for w in (w_gate, w_up)], axis=1)
+        for part in range(HALVES)
+    ]
+    upstream_rows, w_whole, packed, gate_slope, up_slope, w_halves = lax.optimization_barrier(
+        (upstream_rows, w_whole, packed, gate_slope, up_slope, w_halves)
+    )
     back_hidden = contract_last(upstream_rows, w_down[0])
-    sigmoid = jax.nn.sigmoid(gate_pre)
-    grad_gate = (back_hidden * up_pre * sigmoid * (1.0 + gate_pre * (1.0 - sigmoid))).astype(bf16)
-    grad_up = (back_hidden * gate_pre * sigmoid).astype(bf16)
+    grad_gate = (back_hidden * gate_slope).astype(bf16)
+    grad_up = (back_hidden * up_slope).astype(bf16)
     grad_both = jnp.concatenate([grad_gate, grad_up], axis=1)
 
-    half = width // HALVES
+    def add_up(rows_back):
+        return contract_first(picks, rows_back.reshape(inner * slots, half)).astype(bf16)
+
     sums = []
+    grads = []
     for part in range(HALVES):
-        grads = contract_last(grad_both, w_gate_up[part * half : (part + 1) * half])
-        grads = grads.astype(bf16).reshape(inner, slots, half)
-        grads = lax.all_to_all(grads, "inner", 0, 0, tiled=True).reshape(inner * slots, half)
-        partial = contract_first(picks, grads).astype(bf16)
-        sums.append(lax.psum_scatter(partial, "grp", scatter_dimension=0, tiled=True))
+        grads.append(contract_last(grad_both, w_halves[part]))
+        grads[part] = grads[part].astype(bf16).reshape(inner, slots, half)
+    for part in range(HALVES):
+        if part > 0:
+            returned, grads[part] = lax.optimization_barrier((returned, grads[part]))
+        arrived = lax.all_to_all(grads[part], "inner", 0, 0, tiled=True)
+        if part > 0:
+            sums.append(lax.psum_scatter(add_up(returned), "grp", scatter_dimension=0, tiled=True))
+        returned = arrived
+    partial = add_up(returned)
+    sums.append(lax.psum_scatter(partial, "grp", scatter_dimension=0, tiled=True))
 
     packed, _ = lax.optimization_barrier((packed, partial))
     packed = lax.all_to_all(packed, "inner", 0, 0, tiled=True)

time: 487 us -> 482 us (0.990)
  the two profiles are of different devices: /device:TPU:24 before, /device:TPU:0 now
where the time goes in v2:
time: 482 us; the launch traced here: 478 us
  waiting for transfers between devices  185 us (38%)
  blocking collectives  113 us (23%)
  matrix products  63.6 us (13%)
  starting transfers between devices  35.5 us (7%)
  Pallas kernels  34.8 us (7%)
  other arithmetic  18 us (4%)
  local copies, waits for them, and re-layouts  14.3 us (3%)
  between operations  14.3 us (3%)
    all_to_all x2, waiting for transfers between devices, to_experts(): lax.all_to_all(array, 'inner', 0, 0, tiled=True)  122 us
    all_to_all x1, blocking collectives, per_device(): arrived = lax.all_to_all(grads[part], 'inner', 0, 0, tiled=True)  37.3 us
    all_to_all x1, blocking collectives, per_device(): w_piece = lax.all_to_all(w_piece, 'inner', 0, 0, tiled=True)  36.3 us
    dot_general x4, matrix products, dot_nn(): lax.dot_general(left, right, (((1,), (0,)), ((), ())), preferred_element_...  30.8 us
    all_to_all x1, waiting for transfers between devices, per_device(): packed = lax.all_to_all(packed, 'inner', 0, 0, tiled=True)  29.1 us
    all_to_all x1, waiting for transfers between devices, per_device(): arrived = lax.all_to_all(grads[part], 'inner', 0, 0, tiled=True)  28.2 us
    all_to_all x1, blocking collectives, per_device(): packed_grads = lax.all_to_all(packed_grads, 'inner', 0, 0, tiled=True)  26.3 us
    pallas_call x2, Pallas kernels, attention(): pl.pallas_call(functools.partial(attention_kernel, head=head, heads=heads...  21.9 us
  transfers between devices with their start and end apart: 12, of which 5 were waited for; matrix products, arithmetic and copies ran while one was open for 12% of the time, Pallas kernels for 6%

profile of v2, /device:TPU:0, one launch (start us, length us, event | category | flops | bytes accessed | tf_op | source)
XLA Modules:
  0.0 478.4 jit_solution(17229164176974446216)
XLA Ops:
  8.6 2.0 fusion.12
  12.6 36.3 %all_to_all.50 = bf16[16,256,256]{2,1,0:T(8,128)(2,1)} all-to-all(bf16[16,256,256]{2,1,0:T(8,128)(2,1)S(1)} %broadcast_in_dim.61), channel_id=1, replica_groups=mesh['grp'=8,'inner'=16] {'inner'}, dimensions={0} | all-to-all | bytes 4194304 | tf_op jit(solution)/shard_map/all_to_all | solution.py:245
  49.1 13.3 %all-gather = f32[128,128]{1,0:T(8,128)S(1)} all-gather(f32[16,128]{1,0:T(8,128)S(1)} %pad_maximum_fusion.8), channel_id=2, replica_groups=mesh['grp'=8,'inner'=16] {'grp'}, dimensions={0}, use_global_device_ids=true | all-gather | bytes 73728 | tf_op jit(solution)/shard_map/all_gather | solution.py:240
  63.5 10.5 %convolution_convert_fusion = bf16[1280,2048]{1,0:T(8,128)(2,1)} fusion(bf16[1280,1024]{1,0:T(8,128)(2,1)S(1)} %select_convert_fusion, bf16[1024,2048]{1,0:T(8,128)(2,1)} %all-gather.8.cloned.1.call-done), kind=kOutput, calls=%fused_computation.1 | convolution fusion | flops 5371330560 | bytes 12058624 | tf_op jit(solution)/shard_map/dot_general | solution.py:20
  74.1 4.6 all-to-all-start.2
  79.4 9.9 %multiply_convert_fusion = bf16[1280,2048]{1,0:T(8,128)(2,1)} fusion(bf16[1280,1024]{1,0:T(8,128)(2,1)} %copy-done.11, bf16[1024,2048]{1,0:T(8,128)(2,1)} %all-gather.6.cloned.1.call-done, f32[1280]{0:T(1024)S(1)} %mul.104), kind=kOutput, calls=%fused_computation | convolution fusion | flops 5373952000 | bytes 12063744 | tf_op jit(solution)/shard_map/dot_general | solution.py:20
  89.3 69.7 %all-to-all-done.2 = bf16[16,80,2048]{2,1,0:T(8,128)(2,1)} async-done(((bf16[16,80,2048]{2,1,0:T(8,128)(2,1)}), bf16[16,80,2048]{2,1,0:T(8,128)(2,1)}, u32[]{:S(2)}, u32[]{:S(2)}) %all-to-all-start.2) | async-done | bytes 5242912 | tf_op jit(solution)/shard_map/all_to_all | solution.py:286
  159.0 4.9 %all-to-all-start = ((bf16[16,80,2048]{2,1,0:T(8,128)(2,1)}), bf16[16,80,2048]{2,1,0:T(8,128)(2,1)}, u32[]{:S(2)}, u32[]{:S(2)}) async-start(bf16[16,80,2048]{2,1,0:T(8,128)(2,1)} %bitcast.93), calls=%async_computation | async-start | bytes 10485760 | tf_op jit(solution)/shard_map/all_to_all | solution.py:286
  172.1 2.8 pad_maximum_fusion.1
  174.9 10.2 %fusion = f32[1280,1536]{1,0:T(8,128)S(1)} fusion(bf16[1280,2048]{1,0:T(8,128)(2,1)} %bitcast.17, bf16[2048,768]{1,0:T(8,128)(2,1)S(1)} %bitcast.97, bf16[2048,768]{1,0:T(8,128)(2,1)S(1)} %bitcast.98), kind=kOutput, calls=%fused_computation.2 | convolution fusion | flops 8065646592 | bytes 19398656 | tf_op jit(solution)/shard_map/dot_general | solution.py:20
  185.1 4.0 fusion.5
  189.1 52.7 %all-to-all-done = bf16[16,80,2048]{2,1,0:T(8,128)(2,1)} async-done(((bf16[16,80,2048]{2,1,0:T(8,128)(2,1)}), bf16[16,80,2048]{2,1,0:T(8,128)(2,1)}, u32[]{:S(2)}, u32[]{:S(2)}) %all-to-all-start) | async-done | bytes 5242912 | tf_op jit(solution)/shard_map/all_to_all | solution.py:286
  241.8 8.4 %multiply_convert_fusion.2 = (bf16[1280,768]{1,0:T(8,128)(2,1)S(1)}, bf16[1280,768]{1,0:T(8,128)(2,1)S(1)}) fusion(f32[1280,768]{1,0:T(8,128)} %get-tuple-element.29, f32[1280,768]{1,0:T(8,128)} %get-tuple-element.30, bf16[1280,2048]{1,0:T(8,128)(2,1)} %bitcast.8, bf16[1,768,2048]{2,1,0:T(8,128)(2,1)S(1)} %copy-done), kind=kOutput, calls=%fused_computation.13 | convolution fusion | flops 4030464000 | bytes 20185088 | tf_op jit(solution)/shard_map/dot_general | solution.py:26
  250.2 5.6 %convolution_convert_fusion.2 = bf16[1280,1024]{1,0:T(8,128)(2,1)} fusion(bf16[1024,1536]{1,0:T(8,128)(2,1)S(1)} %copy-done.10, bf16[1280,768]{1,0:T(8,128)(2,1)S(1)} %get-tuple-element.61, bf16[1280,768]{1,0:T(8,128)(2,1)S(1)} %get-tuple-element.60), kind=kOutput, calls=%fused_computation.17 | convolution fusion | flops 4035706880 | bytes 9699328 | tf_op jit(solution)/shard_map/dot_general | solution.py:26
  255.9 5.6 %all-to-all-start.3 = ((bf16[16,80,1024]{2,1,0:T(8,128)(2,1)}), bf16[16,80,1024]{2,1,0:T(8,128)(2,1)}, u32[]{:S(2)}, u32[]{:S(2)}) async-start(bf16[16,80,1024]{2,1,0:T(8,128)(2,1)} %bitcast.100), calls=%async_computation.3 | async-start | bytes 5242880 | tf_op jit(solution)/shard_map/all_to_all | solution.py:321
  261.8 7.8 %convolution_convert_fusion.1 = bf16[1280,1024]{1,0:T(8,128)(2,1)} fusion(bf16[1024,1536]{1,0:T(8,128)(2,1)S(1)} %copy-done.9, bf16[1280,768]{1,0:T(8,128)(2,1)} %copy-done.22, bf16[1280,768]{1,0:T(8,128)(2,1)} %copy-done.21), kind=kOutput, calls=%fused_computation.16 | convolution fusion | flops 4035706880 | bytes 9699328 | tf_op jit(solution)/shard_map/dot_general | solution.py:26
  269.6 28.2 %all-to-all-done.3 = bf16[16,80,1024]{2,1,0:T(8,128)(2,1)} async-done(((bf16[16,80,1024]{2,1,0:T(8,128)(2,1)}), bf16[16,80,1024]{2,1,0:T(8,128)(2,1)}, u32[]{:S(2)}, u32[]{:S(2)}) %all-to-all-start.3) | async-done | bytes 2621472 | tf_op jit(solution)/shard_map/all_to_all | solution.py:321
  297.8 6.8 %convolution_convert_fusion.3 = bf16[1024,1024]{1,0:T(8,128)(2,1)} fusion(bf16[1280,1024]{1,0:T(8,128)(2,1)} %copy-done.11, bf16[1280,1024]{1,0:T(8,128)(2,1)} %bitcast.29), kind=kOutput, calls=%fused_computation.23 | convolution fusion | flops 2685403136 | bytes 7340032 | tf_op jit(solution)/shard_map/dot_general | solution.py:32
  304.7 37.3 %all_to_all.51 = bf16[16,80,1024]{2,1,0:T(8,128)(2,1)S(1)} all-to-all(bf16[16,80,1024]{2,1,0:T(8,128)(2,1)} %bitcast.99), channel_id=1, replica_groups=mesh['grp'=8,'inner'=16] {'inner'}, dimensions={0} | all-to-all | bytes 5242880 | tf_op jit(solution)/shard_map/all_to_all | solution.py:321
  342.0 4.3 convolution_convert_fusion.4
  346.3 3.9 all-to-all-start.5
  350.2 29.1 %all-to-all-done.5 = bf16[16,128,512]{2,1,0:T(8,128)(2,1)S(1)} async-done(((bf16[16,128,512]{2,1,0:T(8,128)(2,1)}), bf16[16,128,512]{2,1,0:T(8,128)(2,1)S(1)}, u32[]{:S(2)}, u32[]{:S(2)}) %all-to-all-start.5) | async-done | bytes 2097184 | tf_op jit(solution)/shard_map/all_to_all | solution.py:329
  380.6 2.3 fusion.16.resid_ref
  382.9 6.5 %shard_map.165 = bf16[16,144,128]{2,1,0:T(8,128)(2,1)} custom-call(bf16[128,2048]{1,0:T(8,128)(2,1)} %fusion.16.resid_ref, bf16[8,16,2,128,256]{4,3,2,1,0:T(8,128)(2,1)} %bitcast.91, bf16[128,4096]{1,0:T(8,128)(2,1)} %output_ref.3), custom_call_target="tpu_custom_call" | custom-call | flops 1073741824 | bytes 9961472 | tf_op jit(solution)/shard_map/pallas_call | solution.py:66
  389.4 5.5 %all-to-all-start.6 = ((bf16[16,144,128]{2,1,0:T(8,128)(2,1)}), bf16[16,144,128]{2,1,0:T(8,128)(2,1)S(1)}, u32[]{:S(2)}, u32[]{:S(2)}) async-start(bf16[16,144,128]{2,1,0:T(8,128)(2,1)} %shard_map.165), calls=%async_computation.8 | async-start | bytes 1179648 | tf_op jit(solution)/shard_map/all_to_all | solution.py:347
  394.9 6.5 %shard_map.167 = bf16[16,144,128]{2,1,0:T(8,128)(2,1)} custom-call(bf16[128,2048]{1,0:T(8,128)(2,1)} %fusion.16.resid_ref, bf16[8,16,2,128,256]{4,3,2,1,0:T(8,128)(2,1)} %bitcast.92, bf16[128,4096]{1,0:T(8,128)(2,1)} %output_ref.3), custom_call_target="tpu_custom_call" | custom-call | flops 1073741824 | bytes 9961472 | tf_op jit(solution)/shard_map/pallas_call | solution.py:66
  401.4 4.0 all-to-all-done.6.grad_ref
  405.3 3.6 all-to-all-start.7
  408.9 10.1 %shard_map.166 = (bf16[2048,128]{1,0:T(8,128)(2,1)S(1)}, f32[2048,256]{1,0:T(8,128)S(1)}) custom-call(bf16[2048,512]{1,0:T(8,128)(2,1)S(1)} %bitcast.87, bf16[16,144,128]{2,1,0:T(8,128)(2,1)S(1)} %all-to-all-done.6.grad_ref, f32[2,2048]{1,0:T(2,128)S(1)} %copy-done.4), custom_call_target="tpu_custom_call" | custom-call | flops 2684354560 | bytes 5242880 | tf_op jit(solution)/shard_map/pallas_call | solution.py:181
  421.2 7.1 %all-to-all-start.8 = ((bf16[16,128,128]{2,1,0:T(8,128)(2,1)}), bf16[16,128,128]{2,1,0:T(8,128)(2,1)S(1)}, u32[]{:S(2)}, u32[]{:S(2)}) async-start(bf16[16,128,128]{2,1,0:T(8,128)(2,1)} %bitcast.90), calls=%async_computation.10 | async-start | bytes 1048576 | tf_op jit(solution)/shard_map/all_to_all | solution.py:354
  428.3 11.8 %shard_map.168 = bf16[2048,384]{1,0:T(8,128)(2,1)S(1)} custom-call(bf16[2048,512]{1,0:T(8,128)(2,1)S(1)} %bitcast.88, bf16[16,144,128]{2,1,0:T(8,128)(2,1)S(1)} %all-to-all-done.7.grad_ref, f32[2,2048]{1,0:T(2,128)S(1)} %copy-done.4, f32[2048,256]{1,0:T(8,128)} %copy-done.5), custom_call_target="tpu_custom_call" | custom-call | flops 2684354560 | bytes 5242880 | tf_op jit(solution)/shard_map/pallas_call | solution.py:181
  442.1 26.3 %all_to_all.52 = bf16[16,128,384]{2,1,0:T(8,128)(2,1)S(1)} all-to-all(bf16[16,128,384]{2,1,0:T(8,128)(2,1)} %bitcast.89), channel_id=1, replica_groups=mesh['grp'=8,'inner'=16] {'inner'}, dimensions={0} | all-to-all | bytes 3145728 | tf_op jit(solution)/shard_map/all_to_all | solution.py:358
  (102 shorter events, 22.5 us)
Async XLA Ops:
  7.2 234.7 %copy-start = (bf16[1,768,2048]{2,1,0:T(8,128)(2,1)S(1)}, bf16[1,768,2048]{2,1,0:T(8,128)(2,1)}, u32[]{:S(2)}) copy-start(bf16[1,768,2048]{2,1,0:T(8,128)(2,1)} %param.21) | copy-start | bytes 9437188
  7.2 41.7 %all-gather.8.cloned.1.call-start = ((), (), s32[]{:S(2)}) async-start(), calls=%async_computation.13 | async-start | bytes 4718592 | tf_op jit(solution)/shard_map/all_gather | solution.py:237
  10.7 68.8 %all-gather.6.cloned.1.call-start = ((), (), s32[]{:S(2)}) async-start(), calls=%async_computation.12 | async-start | bytes 4718592 | tf_op jit(solution)/shard_map/all_gather | solution.py:238
  11.4 230.4 %all-gather.10.cloned.1.call-start = ((), (), s32[]{:S(2)}) async-start(), calls=%async_computation.16 | async-start | bytes 18874368 | tf_op jit(solution)/shard_map/all_gather | solution.py:247
  12.6 36.4 %copy-start.19 = (s32[128,8]{0,1:T(8,128)S(1)}, s32[128,8]{0,1:T(8,128)}, u32[]{:S(2)}) copy-start(s32[128,8]{0,1:T(8,128)} %param.17) | copy-start | bytes 12292
  12.6 36.4 %copy-start.20 = (f32[128,8]{0,1:T(8,128)S(1)}, f32[128,8]{0,1:T(8,128)}, u32[]{:S(2)}) copy-start(f32[128,8]{0,1:T(8,128)} %param.18) | copy-start | bytes 12292
  63.5 10.6 %copy-start.11 = (bf16[1280,1024]{1,0:T(8,128)(2,1)}, bf16[1280,1024]{1,0:T(8,128)(2,1)S(1)}, u32[]{:S(2)}) copy-start(bf16[1280,1024]{1,0:T(8,128)(2,1)S(1)} %select_convert_fusion) | copy-start | bytes 7864324
  74.1 85.0 %all-to-all-start.2 = ((bf16[16,80,2048]{2,1,0:T(8,128)(2,1)}), bf16[16,80,2048]{2,1,0:T(8,128)(2,1)}, u32[]{:S(2)}, u32[]{:S(2)}) async-start(bf16[16,80,2048]{2,1,0:T(8,128)(2,1)} %bitcast.94), calls=%async_computation.2 | async-start | bytes 10485760 | tf_op jit(solution)/shard_map/all_to_all | solution.py:286
  159.0 4.9 %copy-start.16 = (bf16[128,512]{1,0:T(8,128)(2,1)S(1)}, bf16[128,512]{1,0:T(8,128)(2,1)}, u32[]{:S(2)}) copy-start(bf16[128,512]{1,0:T(8,128)(2,1)} %param.24) | copy-start | bytes 393220
  159.0 5.0 %copy-start.17 = (bf16[128,512]{1,0:T(8,128)(2,1)S(1)}, bf16[128,512]{1,0:T(8,128)(2,1)}, u32[]{:S(2)}) copy-start(bf16[128,512]{1,0:T(8,128)(2,1)} %param.25) | copy-start | bytes 393220
  159.0 82.8 %all-to-all-start = ((bf16[16,80,2048]{2,1,0:T(8,128)(2,1)}), bf16[16,80,2048]{2,1,0:T(8,128)(2,1)}, u32[]{:S(2)}, u32[]{:S(2)}) async-start(bf16[16,80,2048]{2,1,0:T(8,128)(2,1)} %bitcast.93), calls=%async_computation | async-start | bytes 10485760 | tf_op jit(solution)/shard_map/all_to_all | solution.py:286
  167.3 2.6 copy-start.8
  170.0 1.9 copy-start.7
  241.8 8.4 %copy-start.10 = (bf16[1024,1536]{1,0:T(8,128)(2,1)S(1)}, bf16[1024,1536]{1,0:T(8,128)(2,1)}, u32[]{:S(2)}) copy-start(bf16[1024,1536]{1,0:T(8,128)(2,1)} %get-tuple-element.31) | copy-start | bytes 9437188
  250.2 5.7 %copy-start.21 = (bf16[1280,768]{1,0:T(8,128)(2,1)}, bf16[1280,768]{1,0:T(8,128)(2,1)S(1)}, u32[]{:S(2)}) copy-start(bf16[1280,768]{1,0:T(8,128)(2,1)S(1)} %get-tuple-element.60) | copy-start | bytes 5898244
  250.2 5.7 %copy-start.22 = (bf16[1280,768]{1,0:T(8,128)(2,1)}, bf16[1280,768]{1,0:T(8,128)(2,1)S(1)}, u32[]{:S(2)}) copy-start(bf16[1280,768]{1,0:T(8,128)(2,1)S(1)} %get-tuple-element.61) | copy-start | bytes 5898244
  255.9 5.9 %copy-start.9 = (bf16[1024,1536]{1,0:T(8,128)(2,1)S(1)}, bf16[1024,1536]{1,0:T(8,128)(2,1)}, u32[]{:S(2)}) copy-start(bf16[1024,1536]{1,0:T(8,128)(2,1)} %get-tuple-element.32) | copy-start | bytes 9437188
  255.9 41.9 %all-to-all-start.3 = ((bf16[16,80,1024]{2,1,0:T(8,128)(2,1)}), bf16[16,80,1024]{2,1,0:T(8,128)(2,1)}, u32[]{:S(2)}, u32[]{:S(2)}) async-start(bf16[16,80,1024]{2,1,0:T(8,128)(2,1)} %bitcast.100), calls=%async_computation.3 | async-start | bytes 5242880 | tf_op jit(solution)/shard_map/all_to_all | solution.py:321
  261.5 88.7 %reduce-scatter.3.cloned.1.call-start = ((), (), s32[]{:S(2)}) async-start(), calls=%async_computation.14 | async-start | bytes 2359296 | tf_op jit(solution)/shard_map/reduce_scatter | solution.py:323
  304.6 37.4 %copy-start.12 = (bf16[1280,1024]{1,0:T(8,128)(2,1)S(1)}, bf16[1280,1024]{1,0:T(8,128)(2,1)}, u32[]{:S(2)}) copy-start(bf16[1280,1024]{1,0:T(8,128)(2,1)} %copy-done.11) | copy-start | bytes 7864324
  304.6 74.7 %reduce-scatter.5.cloned.1.call-start = ((), (), s32[]{:S(2)}) async-start(), calls=%async_computation.15 | async-start | bytes 2359296 | tf_op jit(solution)/shard_map/reduce_scatter | solution.py:326
  346.3 33.1 %copy-start.6 = (bf16[128,2048]{1,0:T(8,128)(2,1)S(1)}, bf16[128,2048]{1,0:T(8,128)(2,1)}, u32[]{:S(2)}) copy-start(bf16[128,2048]{1,0:T(8,128)(2,1)} %param.15) | copy-start | bytes 1572868
  346.3 33.1 %copy-start.18 = (f32[2048]{0:T(1024)S(1)}, f32[2048]{0:T(1024)}, u32[]{:S(2)}) copy-start(f32[2048]{0:T(1024)} %param.16) | copy-start | bytes 24580
  346.3 34.3 %copy-start.13 = (bf16[128,2048]{1,0:T(8,128)(2,1)S(1)}, bf16[128,2048]{1,0:T(8,128)(2,1)}, u32[]{:S(2)}) copy-start(bf16[128,2048]{1,0:T(8,128)(2,1)} %param.14) | copy-start | bytes 1572868
  346.3 33.0 %all-to-all-start.5 = ((bf16[16,128,512]{2,1,0:T(8,128)(2,1)}), bf16[16,128,512]{2,1,0:T(8,128)(2,1)S(1)}, u32[]{:S(2)}, u32[]{:S(2)}) async-start(bf16[16,128,512]{2,1,0:T(8,128)(2,1)} %pad_maximum_fusion.5), calls=%async_computation.5 | async-start | bytes 4194304 | tf_op jit(solution)/shard_map/all_to_all | solution.py:329
  389.4 16.0 %all-to-all-start.6 = ((bf16[16,144,128]{2,1,0:T(8,128)(2,1)}), bf16[16,144,128]{2,1,0:T(8,128)(2,1)S(1)}, u32[]{:S(2)}, u32[]{:S(2)}) async-start(bf16[16,144,128]{2,1,0:T(8,128)(2,1)} %shard_map.165), calls=%async_computation.8 | async-start | bytes 1179648 | tf_op jit(solution)/shard_map/all_to_all | solution.py:347
  394.8 14.1 %copy-start.4 = (f32[2,2048]{1,0:T(2,128)S(1)}, f32[2,2048]{1,0:T(2,128)}, u32[]{:S(2)}) copy-start(f32[2,2048]{1,0:T(2,128)} %lse_ref.3) | copy-start | bytes 49156
  405.3 15.9 %all-to-all-start.7 = ((bf16[16,144,128]{2,1,0:T(8,128)(2,1)}), bf16[16,144,128]{2,1,0:T(8,128)(2,1)S(1)}, u32[]{:S(2)}, u32[]{:S(2)}) async-start(bf16[16,144,128]{2,1,0:T(8,128)(2,1)} %shard_map.167), calls=%async_computation.9 | async-start | bytes 1179648 | tf_op jit(solution)/shard_map/all_to_all | solution.py:347
  419.8 1.4 copy-start.5
  421.2 20.1 %all-to-all-start.8 = ((bf16[16,128,128]{2,1,0:T(8,128)(2,1)}), bf16[16,128,128]{2,1,0:T(8,128)(2,1)S(1)}, u32[]{:S(2)}, u32[]{:S(2)}) async-start(bf16[16,128,128]{2,1,0:T(8,128)(2,1)} %bitcast.90), calls=%async_computation.10 | async-start | bytes 1048576 | tf_op jit(solution)/shard_map/all_to_all | solution.py:354
  442.1 26.4 %copy-start.15 = (bf16[16,128,128]{2,1,0:T(8,128)(2,1)S(1)}, bf16[16,128,128]{2,1,0:T(8,128)(2,1)}, u32[]{:S(2)}) copy-start(bf16[16,128,128]{2,1,0:T(8,128)(2,1)} %copy-done.14) | copy-start | bytes 1572868
  468.5 3.4 copy-start.1
  (3 other events, 2.8 us)
Sparse Core Ops, SparseCore 0:
  10.8 34.5 all-gather.7
  47.1 32.0 all-gather.5
  80.9 84.7 all-gather.9
  304.7 31.5 reduce-scatter.2
  346.4 31.5 reduce-scatter.4

commit v3 on v2

--- a/solution.py
+++ b/solution.py
@@ -198,6 +198,107 @@
             transcendentals=length * length // 2,
         ),
     )(*operands)
+
+
+def gather_kernel(picks_ref, table_ref, out_ref):
+    rows = dot_nn(picks_ref[...], table_ref[...]).astype(jnp.bfloat16)
+    out_ref[...] = rows.reshape(out_ref.shape)
+
+
+def gather(picks, table, devices):
+    slots, tokens = picks.shape
+    width = table.shape[1]
+    piece = min(256, width)
+    out = (devices, slots // devices, width)
+    return pl.pallas_call(
+        gather_kernel,
+        grid=(width // piece,),
+        in_specs=[
+            pl.BlockSpec((slots, tokens), lambda n: (0, 0)),
+            pl.BlockSpec((tokens, piece), lambda n: (0, n)),
+        ],
+        out_specs=pl.BlockSpec(out[:2] + (piece,), lambda n: (0, 0, n)),
+        out_shape=jax.ShapeDtypeStruct(out, jnp.bfloat16),
+        cost_estimate=pl.CostEstimate(
+            flops=2 * slots * tokens * width,
+            bytes_accessed=2 * (slots * tokens + (tokens + slots) * width),
+            transcendentals=0,
+        ),
+        name="gather",
+    )(picks, table)
+
+
+def assemble_kernel(*refs):
+    earlier, packed_ref = refs[:-4], refs[-4]
+    query_ref, key_ref, value_ref = refs[-3:]
+    devices = packed_ref.shape[0]
+    heads = len(earlier) + 1
+    total = packed_ref[0, :, HEAD_SIZE:].astype(jnp.float32)
+    for device in range(1, devices):
+        total = total + packed_ref[device, :, HEAD_SIZE:].astype(jnp.float32)
+    key_ref[...] = total[:, :HEAD_SIZE].astype(jnp.bfloat16)
+    value_ref[...] = total[:, HEAD_SIZE:].astype(jnp.bfloat16)
+    for device in range(devices):
+        for head in range(heads):
+            start = (device * heads + head) * HEAD_SIZE
+            part = packed_ref[device, :, :HEAD_SIZE]
+            if head < heads - 1:
+                part = earlier[head][device]
+            query_ref[:, start : start + HEAD_SIZE] = part
+
+
+def assemble(earlier, packed):
+    devices, rows, packed_width = packed.shape
+    shared = devices // KEY_VALUE_HEADS
+    heads = len(earlier) + 1
+    query_width = shared * heads * HEAD_SIZE
+    bf16 = jnp.bfloat16
+    return pl.pallas_call(
+        assemble_kernel,
+        grid=(KEY_VALUE_HEADS,),
+        in_specs=[pl.BlockSpec((shared, rows, HEAD_SIZE), lambda n: (n, 0, 0))] * (heads - 1)
+        + [pl.BlockSpec((shared, rows, packed_width), lambda n: (n, 0, 0))],
+        out_specs=[
+            pl.BlockSpec((rows, query_width), lambda n: (0, n)),
+            pl.BlockSpec((rows, HEAD_SIZE), lambda n: (0, n)),
+            pl.BlockSpec((rows, HEAD_SIZE), lambda n: (0, n)),
+        ],
+        out_shape=[
+            jax.ShapeDtypeStruct((rows, KEY_VALUE_HEADS * query_width), bf16),
+            jax.ShapeDtypeStruct((rows, KEY_VALUE_HEADS * HEAD_SIZE), bf16),
+            jax.ShapeDtypeStruct((rows, KEY_VALUE_HEADS * HEAD_SIZE), bf16),
+        ],
+        name="assemble",
+    )(*earlier, packed)
+
+
+def pick(array, index, axis):
+    starts = [jnp.int32(0)] * array.ndim
+    starts[axis] = index.astype(jnp.int32)
+    sizes = list(array.shape)
+    sizes[axis] = 1
+    piece = lax.dynamic_slice(array, starts, sizes, allow_negative_indices=False)
+    return lax.squeeze(piece, (axis,))
+
+
+def scatter_sum(partial, groups, rows):
+    grp_at = lax.axis_index("grp")
+    core = lax.rem(grp_at, 2)
+    place = lax.div(grp_at, 2)
+    chips = groups // 2
+    f32 = jnp.float32
+    parts = partial.reshape(chips, 2, rows, partial.shape[1])
+    keep = pick(parts, core, 1)
+    send = pick(parts, 1 - core, 1)
+    other = lax.ppermute(send, "grp", [(g, g ^ 1) for g in range(groups)])
+    pair = (keep.astype(f32) + other.astype(f32)).astype(jnp.bfloat16)
+    total = pick(pair, place, 0).astype(f32)
+    for step in range(1, chips):
+        block = pick(pair, lax.rem(place + step, chips), 0)
+        moves = [(g, (g // 2 + step) % chips * 2 + g % 2) for g in range(groups)]
+        block = lax.ppermute(block, "grp", moves)
+        total = total + block.astype(f32)
+    return total
 
 
 def per_device(
@@ -247,18 +348,6 @@
     w_whole = lax.all_gather(w_piece, "grp", axis=0, tiled=False)
     w_whole = w_whole.reshape(groups, inner, head_width // HEAD_SIZE, HEAD_SIZE, piece)
 
-    kv = jnp.stack(
-        [
-            keys.reshape(rows, KEY_VALUE_HEADS, HEAD_SIZE),
-            values.reshape(rows, KEY_VALUE_HEADS, HEAD_SIZE),
-        ],
-        axis=2,
-    ).reshape(rows, KEY_VALUE_HEADS, 2 * HEAD_SIZE)
-    kv = jnp.repeat(kv.transpose(1, 0, 2), shared, axis=0)
-    packed = jnp.concatenate(
-        [queries.reshape(rows, inner, head_width).transpose(1, 0, 2), kv], axis=2
-    )
-
     ids_all = routing[:, :topk]
     gates_all = routing[:, topk:]
     mine = (grp_at * inner + lax.broadcasted_iota(jnp.int32, (1, inner, 1, 1), 1)).astype(f32)
@@ -279,15 +368,29 @@
     chosen = slot == slot_at
     picks = jnp.where(slot == slot_at, 1.0, 0.0).astype(bf16).reshape(inner * slots, column)
     picks = lax.optimization_barrier(picks)
-    slot_gate = jnp.sum(jnp.where(chosen, gate, 0.0), axis=2).reshape(inner * slots, 1)
 
     def to_experts(array):
-        array = array.astype(bf16).reshape(inner, slots, width)
         return lax.all_to_all(array, "inner", 0, 0, tiled=True).reshape(inner * slots, width)
 
+    slot_gate = jnp.sum(jnp.where(chosen, gate, 0.0), axis=2)
+    inputs = to_experts(gather(picks, normed_all, inner))
+    slot_gate = slot_gate.reshape(inner * slots, 1)
+    upstream_rows = (dot_nn(picks, upstream_all) * slot_gate).astype(bf16)
+    upstream_rows = to_experts(upstream_rows.reshape(inner, slots, width))
+
+    kv = jnp.stack(
+        [
+            keys.reshape(rows, KEY_VALUE_HEADS, HEAD_SIZE),
+            values.reshape(rows, KEY_VALUE_HEADS, HEAD_SIZE),
+        ],
+        axis=2,
+    ).reshape(rows, KEY_VALUE_HEADS, 2 * HEAD_SIZE)
+    kv = jnp.repeat(kv.transpose(1, 0, 2), shared, axis=0)
+    packed = jnp.concatenate(
+        [queries.reshape(rows, inner, head_width).transpose(1, 0, 2), kv], axis=2
+    )
+
     w_gate_up = jnp.concatenate([w_gate[0], w_up[0]], axis=1)
-    inputs = to_experts(dot_nn(picks, normed_all))
-    upstream_rows = to_experts(dot_nn(picks, upstream_all) * slot_gate)
     pre = dot_nn(inputs, w_gate_up)
     gate_pre = pre[:, :ff]
     up_pre = pre[:, ff:]
@@ -320,17 +423,13 @@
             returned, grads[part] = lax.optimization_barrier((returned, grads[part]))
         arrived = lax.all_to_all(grads[part], "inner", 0, 0, tiled=True)
         if part > 0:
-            sums.append(lax.psum_scatter(add_up(returned), "grp", scatter_dimension=0, tiled=True))
+            sums.append(scatter_sum(add_up(returned), groups, rows))
         returned = arrived
-    partial = add_up(returned)
-    sums.append(lax.psum_scatter(partial, "grp", scatter_dimension=0, tiled=True))
-
-    packed, _ = lax.optimization_barrier((packed, partial))
+    packed, returned = lax.optimization_barrier((packed, returned))
     packed = lax.all_to_all(packed, "inner", 0, 0, tiled=True)
     packed = packed.reshape(inner * rows, head_width + 2 * HEAD_SIZE)
-    packed, sums = lax.optimization_barrier((packed, sums))
-
-    grad_normed = jnp.concatenate(sums, axis=1).astype(f32)
+    sums.append(scatter_sum(add_up(returned), groups, rows))
+    grad_normed = jnp.concatenate(sums, axis=1)
 
     gained = grad_normed * norm_gain
     statistic = jnp.mean(gained * hidden_f, axis=1, keepdims=True)
@@ -344,6 +443,8 @@
     grads = []
     for head in range(heads):
         grad = project(grad_resid, w_whole, attn_out, head)
+        if head == 0:
+            grad, packed = lax.optimization_barrier((grad, packed))
         grads.append(lax.all_to_all(grad, "inner", 0, 0, tiled=True))
     dkv = None
     token_query = []
@@ -356,16 +457,7 @@
     packed_grads, token_query = lax.optimization_barrier((packed_grads, token_query))
     packed_grads = packed_grads.reshape(inner, rows, 3 * HEAD_SIZE)
     packed_grads = lax.all_to_all(packed_grads, "inner", 0, 0, tiled=True)
-    token_query.append(packed_grads[:, :, :HEAD_SIZE])
-    token_kv = packed_grads[:, :, HEAD_SIZE:]
-    queries_gradient = jnp.concatenate(token_query, axis=2).transpose(1, 0, 2)
-    queries_gradient = queries_gradient.reshape(rows, inner * head_width)
-    totals = jnp.sum(
-        token_kv.reshape(KEY_VALUE_HEADS, shared, rows, 2 * HEAD_SIZE).astype(f32), axis=1
-    ).astype(bf16)
-    kv_width = KEY_VALUE_HEADS * HEAD_SIZE
-    keys_gradient = totals[:, :, :HEAD_SIZE].transpose(1, 0, 2).reshape(rows, kv_width)
-    values_gradient = totals[:, :, HEAD_SIZE:].transpose(1, 0, 2).reshape(rows, kv_width)
+    queries_gradient, keys_gradient, values_gradient = assemble(token_query, packed_grads)
     return (grad_resid, queries_gradient, keys_gradient, values_gradient)
 
 

time: 482 us -> 487 us (1.010)
  blocking collectives: 113 us -> 77.2 us
  starting transfers between devices: 35.5 us -> 51.5 us
  waiting for transfers between devices: 185 us -> 201 us
  Pallas kernels: 34.8 us -> 50.1 us
  matrix products: 63.6 us -> 51.7 us
    all_to_all x1 -> x0, blocking collectives: 37.3 us -> none  [per_device(): arrived = lax.all_to_all(grads[part], 'inner', 0, 0, tiled=True)]
    all_to_all x1 -> x2, waiting for transfers between devices: 28.2 us -> 57.4 us  [per_device(): arrived = lax.all_to_all(grads[part], 'inner', 0, 0, tiled=True)]
    all_to_all x1, waiting for transfers between devices: 29.1 us -> 0.01 us  [per_device(): packed = lax.all_to_all(packed, 'inner', 0, 0, tiled=True)]
    ppermute x0 -> x8, waiting for transfers between devices: none -> 15.1 us  [the longest x6 15.1 us: scatter_sum(): block = lax.ppermute(block, 'grp', moves)]
    pallas_call x0 -> x2, Pallas kernels: none -> 14.9 us  [the longest x1 11.2 us: gather(): pl.pallas_call(gather_kernel, grid=(width // piece,), in_specs=[pl.BlockS...]
    dot_general x4 -> x3, matrix products: 30.8 us -> 20.2 us  [dot_nn(): lax.dot_general(left, right, (((1,), (0,)), ((), ())), preferred_element_...]
    ppermute x0 -> x8, starting transfers between devices: none -> 9.95 us  [the longest x6 9.94 us: scatter_sum(): block = lax.ppermute(block, 'grp', moves)]
    all_to_all x1 -> x2, starting transfers between devices: 5.58 us -> 9.98 us  [per_device(): arrived = lax.all_to_all(grads[part], 'inner', 0, 0, tiled=True)]
  transfers between devices with their start and end apart: 12 -> 19, of which waited for: 5 -> 9; matrix products, arithmetic and copies ran while one was open for 12% -> 13% of each run, Pallas kernels for 6% -> 10%
where the time goes in v3:
time: 487 us; the launch traced here: 485 us
  waiting for transfers between devices  201 us (41%)
  blocking collectives  77.2 us (16%)
  matrix products  51.7 us (11%)
  starting transfers between devices  51.5 us (11%)
  Pallas kernels  50.1 us (10%)
  other arithmetic  22.3 us (5%)
  local copies, waits for them, and re-layouts  16.9 us (3%)
  between operations  14.3 us (3%)
    all_to_all x2, waiting for transfers between devices, to_experts(): lax.all_to_all(array, 'inner', 0, 0, tiled=True)  122 us
    all_to_all x2, waiting for transfers between devices, per_device(): arrived = lax.all_to_all(grads[part], 'inner', 0, 0, tiled=True)  57.4 us
    all_to_all x1, blocking collectives, per_device(): w_piece = lax.all_to_all(w_piece, 'inner', 0, 0, tiled=True)  36.3 us
    all_to_all x1, blocking collectives, per_device(): packed_grads = lax.all_to_all(packed_grads, 'inner', 0, 0, tiled=True)  27.7 us
    pallas_call x2, Pallas kernels, attention(): pl.pallas_call(functools.partial(attention_kernel, head=head, heads=heads...  22.2 us
    dot_general x3, matrix products, contract_last(): lax.dot_general(left, right, (((1,), (1,)), ((), ())), preferred_element_...  21.8 us
    dot_general x3, matrix products, dot_nn(): lax.dot_general(left, right, (((1,), (0,)), ((), ())), preferred_element_...  20.2 us
    ppermute x6, waiting for transfers between devices, scatter_sum(): block = lax.ppermute(block, 'grp', moves)  15.1 us
  transfers between devices with their start and end apart: 19, of which 9 were waited for; matrix products, arithmetic and copies ran while one was open for 13% of the time, Pallas kernels for 10%

profile of v3, /device:TPU:0, one launch (start us, length us, event | category | flops | bytes accessed | tf_op | source)
XLA Modules:
  0.0 484.8 jit_solution(1237355634494016229)
XLA Ops:
  12.6 36.3 %all_to_all.50 = bf16[16,256,256]{2,1,0:T(8,128)(2,1)} all-to-all(bf16[16,256,256]{2,1,0:T(8,128)(2,1)S(1)} %broadcast_in_dim.61), channel_id=1, replica_groups=mesh['grp'=8,'inner'=16] {'inner'}, dimensions={0} | all-to-all | bytes 4194304 | tf_op jit(solution)/shard_map/all_to_all | solution.py:346
  49.1 13.3 %all-gather = f32[128,128]{1,0:T(8,128)S(1)} all-gather(f32[16,128]{1,0:T(8,128)S(1)} %pad_maximum_fusion.7), channel_id=2, replica_groups=mesh['grp'=8,'inner'=16] {'grp'}, dimensions={0}, use_global_device_ids=true | all-gather | bytes 73728 | tf_op jit(solution)/shard_map/all_gather | solution.py:341
  65.0 11.2 %gather.1 = bf16[16,80,2048]{2,1,0:T(8,128)(2,1)} custom-call(bf16[1280,1024]{1,0:T(8,128)(2,1)} %select_convert_fusion.picks_ref, bf16[1024,2048]{1,0:T(8,128)(2,1)} %all-gather.8.cloned.1.call-done.table_ref), custom_call_target="tpu_custom_call" | custom-call | flops 5368709120 | bytes 12058624 | tf_op jit(solution)/shard_map/gather/pallas_call | solution.py:213
  76.2 4.6 all-to-all-start.2
  81.5 9.9 %multiply_convert_fusion = bf16[1280,2048]{1,0:T(8,128)(2,1)} fusion(bf16[1280,1024]{1,0:T(8,128)(2,1)} %select_convert_fusion.picks_ref, bf16[1024,2048]{1,0:T(8,128)(2,1)} %all-gather.6.cloned.1.call-done, f32[1280]{0:T(1024)S(1)} %mul.104), kind=kOutput, calls=%fused_computation | convolution fusion | flops 5373952000 | bytes 12063744 | tf_op jit(solution)/shard_map/dot_general | solution.py:20
  91.4 69.4 %all-to-all-done.2 = bf16[16,80,2048]{2,1,0:T(8,128)(2,1)} async-done(((bf16[16,80,2048]{2,1,0:T(8,128)(2,1)}), bf16[16,80,2048]{2,1,0:T(8,128)(2,1)}, u32[]{:S(2)}, u32[]{:S(2)}) %all-to-all-start.2) | async-done | bytes 5242912 | tf_op jit(solution)/shard_map/all_to_all | solution.py:373
  160.8 4.9 %all-to-all-start = ((bf16[16,80,2048]{2,1,0:T(8,128)(2,1)}), bf16[16,80,2048]{2,1,0:T(8,128)(2,1)}, u32[]{:S(2)}, u32[]{:S(2)}) async-start(bf16[16,80,2048]{2,1,0:T(8,128)(2,1)} %bitcast.112), calls=%async_computation | async-start | bytes 10485760 | tf_op jit(solution)/shard_map/all_to_all | solution.py:373
  176.7 10.2 %fusion = f32[1280,1536]{1,0:T(8,128)S(1)} fusion(bf16[1280,2048]{1,0:T(8,128)(2,1)} %bitcast.16, bf16[2048,768]{1,0:T(8,128)(2,1)S(1)} %bitcast.115, bf16[2048,768]{1,0:T(8,128)(2,1)S(1)} %bitcast.116), kind=kOutput, calls=%fused_computation.1 | convolution fusion | flops 8065646592 | bytes 19398656 | tf_op jit(solution)/shard_map/dot_general | solution.py:20
  186.9 4.0 fusion.5
  190.9 52.6 %all-to-all-done = bf16[16,80,2048]{2,1,0:T(8,128)(2,1)} async-done(((bf16[16,80,2048]{2,1,0:T(8,128)(2,1)}), bf16[16,80,2048]{2,1,0:T(8,128)(2,1)}, u32[]{:S(2)}, u32[]{:S(2)}) %all-to-all-start) | async-done | bytes 5242912 | tf_op jit(solution)/shard_map/all_to_all | solution.py:373
  243.5 8.4 %multiply_convert_fusion.2 = (bf16[1280,768]{1,0:T(8,128)(2,1)S(1)}, bf16[1280,768]{1,0:T(8,128)(2,1)S(1)}) fusion(f32[1280,768]{1,0:T(8,128)} %get-tuple-element.31, f32[1280,768]{1,0:T(8,128)} %get-tuple-element.32, bf16[1280,2048]{1,0:T(8,128)(2,1)} %bitcast.8, bf16[1,768,2048]{2,1,0:T(8,128)(2,1)S(1)} %copy-done), kind=kOutput, calls=%fused_computation.12 | convolution fusion | flops 4030464000 | bytes 20185088 | tf_op jit(solution)/shard_map/dot_general | solution.py:26
  252.0 5.6 %convolution_convert_fusion.1 = bf16[1280,1024]{1,0:T(8,128)(2,1)} fusion(bf16[1024,1536]{1,0:T(8,128)(2,1)S(1)} %copy-done.13, bf16[1280,768]{1,0:T(8,128)(2,1)S(1)} %get-tuple-element.55, bf16[1280,768]{1,0:T(8,128)(2,1)S(1)} %get-tuple-element.54), kind=kOutput, calls=%fused_computation.16 | convolution fusion | flops 4035706880 | bytes 9699328 | tf_op jit(solution)/shard_map/dot_general | solution.py:26
  257.6 5.5 %all-to-all-start.3 = ((bf16[16,80,1024]{2,1,0:T(8,128)(2,1)}), bf16[16,80,1024]{2,1,0:T(8,128)(2,1)}, u32[]{:S(2)}, u32[]{:S(2)}) async-start(bf16[16,80,1024]{2,1,0:T(8,128)(2,1)} %bitcast.118), calls=%async_computation.3 | async-start | bytes 5242880 | tf_op jit(solution)/shard_map/all_to_all | solution.py:424
  263.1 7.8 %convolution_convert_fusion = bf16[1280,1024]{1,0:T(8,128)(2,1)} fusion(bf16[1024,1536]{1,0:T(8,128)(2,1)S(1)} %copy-done.12, bf16[1280,768]{1,0:T(8,128)(2,1)} %copy-done.24, bf16[1280,768]{1,0:T(8,128)(2,1)} %copy-done.23), kind=kOutput, calls=%fused_computation.15 | convolution fusion | flops 4035706880 | bytes 9699328 | tf_op jit(solution)/shard_map/dot_general | solution.py:26
  270.9 28.3 %all-to-all-done.3 = bf16[16,80,1024]{2,1,0:T(8,128)(2,1)} async-done(((bf16[16,80,1024]{2,1,0:T(8,128)(2,1)}), bf16[16,80,1024]{2,1,0:T(8,128)(2,1)}, u32[]{:S(2)}, u32[]{:S(2)}) %all-to-all-start.3) | async-done | bytes 2621472 | tf_op jit(solution)/shard_map/all_to_all | solution.py:424
  299.2 4.5 all-to-all-start.4
  303.7 4.9 %convolution_convert_fusion.3 = bf16[1024,1024]{1,0:T(8,128)(2,1)S(1)} fusion(bf16[1280,1024]{1,0:T(8,128)(2,1)S(1)} %copy-done.14, bf16[1280,1024]{1,0:T(8,128)(2,1)} %bitcast.26), kind=kOutput, calls=%fused_computation.27 | convolution fusion | flops 2685403136 | bytes 7340032 | tf_op jit(solution)/shard_map/dot_general | solution.py:32
  311.0 29.2 %all-to-all-done.4 = bf16[16,80,1024]{2,1,0:T(8,128)(2,1)} async-done(((bf16[16,80,1024]{2,1,0:T(8,128)(2,1)}), bf16[16,80,1024]{2,1,0:T(8,128)(2,1)}, u32[]{:S(2)}, u32[]{:S(2)}) %all-to-all-start.4) | async-done | bytes 2621472 | tf_op jit(solution)/shard_map/all_to_all | solution.py:424
  340.1 4.9 %convolution_convert_fusion.2 = bf16[1024,1024]{1,0:T(8,128)(2,1)S(1)} fusion(bf16[1280,1024]{1,0:T(8,128)(2,1)S(1)} %copy-done.14, bf16[1280,1024]{1,0:T(8,128)(2,1)} %bitcast.34), kind=kOutput, calls=%fused_computation.26 | convolution fusion | flops 2685403136 | bytes 7340032 | tf_op jit(solution)/shard_map/dot_general | solution.py:32
  349.4 3.7 all-to-all-start.5
  365.6 5.1 %collective-permute-done.2 = bf16[128,1024]{1,0:T(8,128)(2,1)S(1)} collective-permute-done((bf16[128,1024]{1,0:T(8,128)(2,1)S(1)}, bf16[128,1024]{1,0:T(8,128)(2,1)S(1)}, u32[]{:S(2)}, u32[]{:S(2)}) %collective-permute-start.2) | collective-permute-done | bytes 262176 | tf_op jit(solution)/shard_map/ppermute | solution.py:299
  375.2 6.3 %collective-permute-done.6 = bf16[128,1024]{1,0:T(8,128)(2,1)S(1)} collective-permute-done((bf16[128,1024]{1,0:T(8,128)(2,1)S(1)}, bf16[128,1024]{1,0:T(8,128)(2,1)S(1)}, u32[]{:S(2)}, u32[]{:S(2)}) %collective-permute-start.6) | collective-permute-done | bytes 262176 | tf_op jit(solution)/shard_map/ppermute | solution.py:299
  383.2 6.5 %shard_map.165 = bf16[16,144,128]{2,1,0:T(8,128)(2,1)} custom-call(bf16[128,2048]{1,0:T(8,128)(2,1)} %fusion.18.resid_ref, bf16[8,16,2,128,256]{4,3,2,1,0:T(8,128)(2,1)} %bitcast.110, bf16[128,4096]{1,0:T(8,128)(2,1)} %output_ref.3), custom_call_target="tpu_custom_call" | custom-call | flops 1073741824 | bytes 9961472 | tf_op jit(solution)/shard_map/pallas_call | solution.py:66
  389.6 6.9 %all-to-all-start.6 = ((bf16[16,144,128]{2,1,0:T(8,128)(2,1)}), bf16[16,144,128]{2,1,0:T(8,128)(2,1)S(1)}, u32[]{:S(2)}, u32[]{:S(2)}) async-start(bf16[16,144,128]{2,1,0:T(8,128)(2,1)} %shard_map.165), calls=%async_computation.6 | async-start | bytes 1179648 | tf_op jit(solution)/shard_map/all_to_all | solution.py:448
  396.5 6.5 %shard_map.167 = bf16[16,144,128]{2,1,0:T(8,128)(2,1)} custom-call(bf16[128,2048]{1,0:T(8,128)(2,1)} %fusion.18.resid_ref, bf16[8,16,2,128,256]{4,3,2,1,0:T(8,128)(2,1)} %bitcast.111, bf16[128,4096]{1,0:T(8,128)(2,1)} %output_ref.3), custom_call_target="tpu_custom_call" | custom-call | flops 1073741824 | bytes 9961472 | tf_op jit(solution)/shard_map/pallas_call | solution.py:66
  403.0 5.3 %all-to-all-done.6.grad_ref = bf16[16,144,128]{2,1,0:T(8,128)(2,1)S(1)} async-done(((bf16[16,144,128]{2,1,0:T(8,128)(2,1)}), bf16[16,144,128]{2,1,0:T(8,128)(2,1)S(1)}, u32[]{:S(2)}, u32[]{:S(2)}) %all-to-all-start.6) | async-done | bytes 589856 | tf_op jit(solution)/shard_map/all_to_all | solution.py:448
  408.3 4.2 all-to-all-start.7
  412.5 10.1 %shard_map.166 = (bf16[2048,128]{1,0:T(8,128)(2,1)S(1)}, f32[2048,256]{1,0:T(8,128)S(1)}) custom-call(bf16[2048,512]{1,0:T(8,128)(2,1)S(1)} %bitcast.106, bf16[16,144,128]{2,1,0:T(8,128)(2,1)S(1)} %all-to-all-done.6.grad_ref, f32[2,2048]{1,0:T(2,128)S(1)} %copy-done.6), custom_call_target="tpu_custom_call" | custom-call | flops 2684354560 | bytes 5242880 | tf_op jit(solution)/shard_map/pallas_call | solution.py:181
  424.8 7.2 %all-to-all-start.8 = ((bf16[16,128,128]{2,1,0:T(8,128)(2,1)}), bf16[16,128,128]{2,1,0:T(8,128)(2,1)}, u32[]{:S(2)}, u32[]{:S(2)}) async-start(bf16[16,128,128]{2,1,0:T(8,128)(2,1)} %bitcast.109), calls=%async_computation.8 | async-start | bytes 1048576 | tf_op jit(solution)/shard_map/all_to_all | solution.py:455
  433.6 12.1 %shard_map.168 = bf16[2048,384]{1,0:T(8,128)(2,1)S(1)} custom-call(bf16[2048,512]{1,0:T(8,128)(2,1)S(1)} %bitcast.107, bf16[16,144,128]{2,1,0:T(8,128)(2,1)} %all-to-all-done.7.grad_ref, f32[2,2048]{1,0:T(2,128)S(1)} %copy-done.6, f32[2048,256]{1,0:T(8,128)} %copy-done.7), custom_call_target="tpu_custom_call" | custom-call | flops 2684354560 | bytes 5242880 | tf_op jit(solution)/shard_map/pallas_call | solution.py:181
  446.8 27.7 %all_to_all.51.refs_1_ = bf16[16,128,384]{2,1,0:T(8,128)(2,1)} all-to-all(bf16[16,128,384]{2,1,0:T(8,128)(2,1)} %bitcast.108), channel_id=1, replica_groups=mesh['grp'=8,'inner'=16] {'inner'}, dimensions={0} | all-to-all | bytes 3145728 | tf_op jit(solution)/shard_map/all_to_all | solution.py:459
  474.5 3.7 assemble.1
  (117 shorter events, 50.0 us)
Async XLA Ops:
  7.2 236.4 %copy-start = (bf16[1,768,2048]{2,1,0:T(8,128)(2,1)S(1)}, bf16[1,768,2048]{2,1,0:T(8,128)(2,1)}, u32[]{:S(2)}) copy-start(bf16[1,768,2048]{2,1,0:T(8,128)(2,1)} %param.21) | copy-start | bytes 9437188
  7.2 41.7 %all-gather.8.cloned.1.call-start = ((), (), s32[]{:S(2)}) async-start(), calls=%async_computation.11 | async-start | bytes 4718592 | tf_op jit(solution)/shard_map/all_gather | solution.py:338
  10.7 70.9 %all-gather.6.cloned.1.call-start = ((), (), s32[]{:S(2)}) async-start(), calls=%async_computation.10 | async-start | bytes 4718592 | tf_op jit(solution)/shard_map/all_gather | solution.py:339
  11.4 232.1 %all-gather.10.cloned.1.call-start = ((), (), s32[]{:S(2)}) async-start(), calls=%async_computation.12 | async-start | bytes 18874368 | tf_op jit(solution)/shard_map/all_gather | solution.py:348
  12.6 36.4 %copy-start.21 = (s32[128,8]{0,1:T(8,128)S(1)}, s32[128,8]{0,1:T(8,128)}, u32[]{:S(2)}) copy-start(s32[128,8]{0,1:T(8,128)} %param.17) | copy-start | bytes 12292
  12.6 36.4 %copy-start.22 = (f32[128,8]{0,1:T(8,128)S(1)}, f32[128,8]{0,1:T(8,128)}, u32[]{:S(2)}) copy-start(f32[128,8]{0,1:T(8,128)} %param.18) | copy-start | bytes 12292
  76.2 84.6 %all-to-all-start.2 = ((bf16[16,80,2048]{2,1,0:T(8,128)(2,1)}), bf16[16,80,2048]{2,1,0:T(8,128)(2,1)}, u32[]{:S(2)}, u32[]{:S(2)}) async-start(bf16[16,80,2048]{2,1,0:T(8,128)(2,1)} %gather.1), calls=%async_computation.2 | async-start | bytes 10485760 | tf_op jit(solution)/shard_map/all_to_all | solution.py:373
  160.8 82.8 %all-to-all-start = ((bf16[16,80,2048]{2,1,0:T(8,128)(2,1)}), bf16[16,80,2048]{2,1,0:T(8,128)(2,1)}, u32[]{:S(2)}, u32[]{:S(2)}) async-start(bf16[16,80,2048]{2,1,0:T(8,128)(2,1)} %bitcast.112), calls=%async_computation | async-start | bytes 10485760 | tf_op jit(solution)/shard_map/all_to_all | solution.py:373
  243.5 8.4 %copy-start.13 = (bf16[1024,1536]{1,0:T(8,128)(2,1)S(1)}, bf16[1024,1536]{1,0:T(8,128)(2,1)}, u32[]{:S(2)}) copy-start(bf16[1024,1536]{1,0:T(8,128)(2,1)} %get-tuple-element.33) | copy-start | bytes 9437188
  251.9 5.7 %copy-start.23 = (bf16[1280,768]{1,0:T(8,128)(2,1)}, bf16[1280,768]{1,0:T(8,128)(2,1)S(1)}, u32[]{:S(2)}) copy-start(bf16[1280,768]{1,0:T(8,128)(2,1)S(1)} %get-tuple-element.54) | copy-start | bytes 5898244
  257.6 41.6 %all-to-all-start.3 = ((bf16[16,80,1024]{2,1,0:T(8,128)(2,1)}), bf16[16,80,1024]{2,1,0:T(8,128)(2,1)}, u32[]{:S(2)}, u32[]{:S(2)}) async-start(bf16[16,80,1024]{2,1,0:T(8,128)(2,1)} %bitcast.118), calls=%async_computation.3 | async-start | bytes 5242880 | tf_op jit(solution)/shard_map/all_to_all | solution.py:424
  270.9 32.8 %copy-start.14 = (bf16[1280,1024]{1,0:T(8,128)(2,1)S(1)}, bf16[1280,1024]{1,0:T(8,128)(2,1)}, u32[]{:S(2)}) copy-start(bf16[1280,1024]{1,0:T(8,128)(2,1)} %select_convert_fusion.picks_ref) | copy-start | bytes 7864324
  299.2 40.9 %all-to-all-start.4 = ((bf16[16,80,1024]{2,1,0:T(8,128)(2,1)}), bf16[16,80,1024]{2,1,0:T(8,128)(2,1)}, u32[]{:S(2)}, u32[]{:S(2)}) async-start(bf16[16,80,1024]{2,1,0:T(8,128)(2,1)} %bitcast.117), calls=%async_computation.4 | async-start | bytes 5242880 | tf_op jit(solution)/shard_map/all_to_all | solution.py:424
  311.0 36.5 %collective-permute-start = (bf16[4,128,1024]{2,1,0:T(8,128)(2,1)}, bf16[4,128,1024]{2,1,0:T(8,128)(2,1)}, u32[]{:S(2)}, u32[]{:S(2)}) collective-permute-start(bf16[4,128,1024]{2,1,0:T(8,128)(2,1)} %dynamic-slice_bitcast_fusion.1), channel_id=1, source_target_pairs={{0,16},{16,0},{32,48},{48,32},{64,80},{80,64},{96,112},{112,96},{1... | collective-permute-start | bytes 3145736 | tf_op jit(solution)/shard_map/ppermute | solution.py:293
  347.4 10.7 %collective-permute-start.4 = (bf16[4,128,1024]{2,1,0:T(8,128)(2,1)}, bf16[4,128,1024]{2,1,0:T(8,128)(2,1)}, u32[]{:S(2)}, u32[]{:S(2)}) collective-permute-start(bf16[4,128,1024]{2,1,0:T(8,128)(2,1)} %dynamic-slice_bitcast_fusion), channel_id=1, source_target_pairs={{0,16},{16,0},{32,48},{48,32},{64,80},{80,64},{96,112},{112,96},{1... | collective-permute-start | bytes 3145736 | tf_op jit(solution)/shard_map/ppermute | solution.py:293
  349.4 8.7 %copy-start.9 = (bf16[4,128,1024]{2,1,0:T(8,128)(2,1)}, bf16[4,128,1024]{2,1,0:T(8,128)(2,1)S(1)}, u32[]{:S(2)}) copy-start(bf16[4,128,1024]{2,1,0:T(8,128)(2,1)S(1)} %fusion.9) | copy-start | bytes 3145732
  349.4 40.2 %all-to-all-start.5 = ((bf16[16,128,512]{2,1,0:T(8,128)(2,1)}), bf16[16,128,512]{2,1,0:T(8,128)(2,1)S(1)}, u32[]{:S(2)}, u32[]{:S(2)}) async-start(bf16[16,128,512]{2,1,0:T(8,128)(2,1)} %pad_maximum_fusion.5), calls=%async_computation.5 | async-start | bytes 4194304 | tf_op jit(solution)/shard_map/all_to_all | solution.py:429
  353.2 10.2 %collective-permute-start.1 = (bf16[128,1024]{1,0:T(8,128)(2,1)S(1)}, bf16[128,1024]{1,0:T(8,128)(2,1)S(1)}, u32[]{:S(2)}, u32[]{:S(2)}) collective-permute-start(bf16[128,1024]{1,0:T(8,128)(2,1)S(1)} %get-tuple-element.60), channel_id=1, source_target_pairs={{0,32},{16,48},{32,64},{48,80},{64,96},{80,112},{96,0},{112,16},{1... | collective-permute-start | bytes 786440 | tf_op jit(solution)/shard_map/ppermute | solution.py:299
  355.3 15.4 %collective-permute-start.2 = (bf16[128,1024]{1,0:T(8,128)(2,1)S(1)}, bf16[128,1024]{1,0:T(8,128)(2,1)S(1)}, u32[]{:S(2)}, u32[]{:S(2)}) collective-permute-start(bf16[128,1024]{1,0:T(8,128)(2,1)S(1)} %get-tuple-element.62), channel_id=1, source_target_pairs={{0,64},{16,80},{32,96},{48,112},{64,0},{80,16},{96,32},{112,48},{1... | collective-permute-start | bytes 786440 | tf_op jit(solution)/shard_map/ppermute | solution.py:299
  357.9 12.8 %collective-permute-start.3 = (bf16[128,1024]{1,0:T(8,128)(2,1)S(1)}, bf16[128,1024]{1,0:T(8,128)(2,1)S(1)}, u32[]{:S(2)}, u32[]{:S(2)}) collective-permute-start(bf16[128,1024]{1,0:T(8,128)(2,1)S(1)} %get-tuple-element.61), channel_id=1, source_target_pairs={{0,96},{16,112},{32,0},{48,16},{64,32},{80,48},{96,64},{112,80},{1... | collective-permute-start | bytes 786440 | tf_op jit(solution)/shard_map/ppermute | solution.py:299
  360.1 21.6 %copy-start.8 = (bf16[128,2048]{1,0:T(8,128)(2,1)S(1)}, bf16[128,2048]{1,0:T(8,128)(2,1)}, u32[]{:S(2)}) copy-start(bf16[128,2048]{1,0:T(8,128)(2,1)} %param.15) | copy-start | bytes 1572868
  360.1 21.6 %copy-start.20 = (f32[2048]{0:T(1024)S(1)}, f32[2048]{0:T(1024)}, u32[]{:S(2)}) copy-start(f32[2048]{0:T(1024)} %param.16) | copy-start | bytes 24580
  360.1 21.8 %copy-start.15 = (bf16[128,2048]{1,0:T(8,128)(2,1)S(1)}, bf16[128,2048]{1,0:T(8,128)(2,1)}, u32[]{:S(2)}) copy-start(bf16[128,2048]{1,0:T(8,128)(2,1)} %param.14) | copy-start | bytes 1572868
  360.2 15.1 %collective-permute-start.5 = (bf16[128,1024]{1,0:T(8,128)(2,1)S(1)}, bf16[128,1024]{1,0:T(8,128)(2,1)S(1)}, u32[]{:S(2)}, u32[]{:S(2)}) collective-permute-start(bf16[128,1024]{1,0:T(8,128)(2,1)S(1)} %get-tuple-element.63), channel_id=1, source_target_pairs={{0,32},{16,48},{32,64},{48,80},{64,96},{80,112},{96,0},{112,16},{1... | collective-permute-start | bytes 786440 | tf_op jit(solution)/shard_map/ppermute | solution.py:299
  362.0 19.4 %collective-permute-start.6 = (bf16[128,1024]{1,0:T(8,128)(2,1)S(1)}, bf16[128,1024]{1,0:T(8,128)(2,1)S(1)}, u32[]{:S(2)}, u32[]{:S(2)}) collective-permute-start(bf16[128,1024]{1,0:T(8,128)(2,1)S(1)} %get-tuple-element.65), channel_id=1, source_target_pairs={{0,64},{16,80},{32,96},{48,112},{64,0},{80,16},{96,32},{112,48},{1... | collective-permute-start | bytes 786440 | tf_op jit(solution)/shard_map/ppermute | solution.py:299
  363.4 18.1 %collective-permute-start.7 = (bf16[128,1024]{1,0:T(8,128)(2,1)S(1)}, bf16[128,1024]{1,0:T(8,128)(2,1)S(1)}, u32[]{:S(2)}, u32[]{:S(2)}) collective-permute-start(bf16[128,1024]{1,0:T(8,128)(2,1)S(1)} %get-tuple-element.64), channel_id=1, source_target_pairs={{0,96},{16,112},{32,0},{48,16},{64,32},{80,48},{96,64},{112,80},{1... | collective-permute-start | bytes 786440 | tf_op jit(solution)/shard_map/ppermute | solution.py:299
  389.6 22.9 %copy-start.2 = (bf16[16,128,512]{2,1,0:T(8,128)(2,1)}, bf16[16,128,512]{2,1,0:T(8,128)(2,1)S(1)}, u32[]{:S(2)}) copy-start(bf16[16,128,512]{2,1,0:T(8,128)(2,1)S(1)} %all-to-all-done.5) | copy-start | bytes 6291460
  389.6 18.6 %all-to-all-start.6 = ((bf16[16,144,128]{2,1,0:T(8,128)(2,1)}), bf16[16,144,128]{2,1,0:T(8,128)(2,1)S(1)}, u32[]{:S(2)}, u32[]{:S(2)}) async-start(bf16[16,144,128]{2,1,0:T(8,128)(2,1)} %shard_map.165), calls=%async_computation.6 | async-start | bytes 1179648 | tf_op jit(solution)/shard_map/all_to_all | solution.py:448
  396.5 16.0 %copy-start.6 = (f32[2,2048]{1,0:T(2,128)S(1)}, f32[2,2048]{1,0:T(2,128)}, u32[]{:S(2)}) copy-start(f32[2,2048]{1,0:T(2,128)} %lse_ref.3) | copy-start | bytes 49156
  408.3 16.5 %all-to-all-start.7 = ((bf16[16,144,128]{2,1,0:T(8,128)(2,1)}), bf16[16,144,128]{2,1,0:T(8,128)(2,1)}, u32[]{:S(2)}, u32[]{:S(2)}) async-start(bf16[16,144,128]{2,1,0:T(8,128)(2,1)} %shard_map.167), calls=%async_computation.7 | async-start | bytes 1179648 | tf_op jit(solution)/shard_map/all_to_all | solution.py:448
  424.8 22.0 %all-to-all-start.8 = ((bf16[16,128,128]{2,1,0:T(8,128)(2,1)}), bf16[16,128,128]{2,1,0:T(8,128)(2,1)}, u32[]{:S(2)}, u32[]{:S(2)}) async-start(bf16[16,128,128]{2,1,0:T(8,128)(2,1)} %bitcast.109), calls=%async_computation.8 | async-start | bytes 1048576 | tf_op jit(solution)/shard_map/all_to_all | solution.py:455
  433.6 44.7 %copy-start.1 = (bf16[1,768,2048]{2,1,0:T(8,128)(2,1)S(1)}, bf16[1,768,2048]{2,1,0:T(8,128)(2,1)}, u32[]{:S(2)}) copy-start(bf16[1,768,2048]{2,1,0:T(8,128)(2,1)} %param.21) | copy-start | bytes 9437188
  (12 other events, 33.2 us)
Sparse Core Ops, SparseCore 0:
  10.8 34.5 all-gather.7
  47.1 32.0 all-gather.5
  80.9 84.7 all-gather.9

commit v4 on v3

v4 whole, which is shorter than its diff:
```python
import math

import jax
import jax.numpy as jnp
from jax import lax
from jax.experimental import pallas as pl
from jax.experimental.pallas import tpu as pltpu
from jax.sharding import PartitionSpec as P

KEY_VALUE_HEADS = 4
HEAD_SIZE = 128
EPSILON = 1e-06
BLOCK = 512
SHARES = (5, 3)
DELTA_ROWS = 16
DIGITS = 8


def dot_nn(left, right):
    return lax.dot_general(
        left, right, (((1,), (0,)), ((), ())), preferred_element_type=jnp.float32
    )


def contract_last(left, right):
    return lax.dot_general(
        left, right, (((1,), (1,)), ((), ())), preferred_element_type=jnp.float32
    )


def contract_first(left, right):
    return lax.dot_general(
        left, right, (((0,), (0,)), ((), ())), preferred_element_type=jnp.float32
    )


def project_kernel(resid_ref, weight_ref, output_ref, out_ref):
    parts, devices, heads, _, piece = weight_ref.shape
    head_width = heads * HEAD_SIZE
    total = None
    for part in range(parts):
        weight = weight_ref[part].reshape(devices * head_width, piece)
        term = contract_last(weight, resid_ref[:, part * piece : (part + 1) * piece])
        total = term if total is None else total + term
    row_at = lax.broadcasted_iota(jnp.int32, (DELTA_ROWS, resid_ref.shape[0]), 0)
    for device in range(devices):
        held = jnp.zeros(row_at.shape, jnp.float32)
        for head in range(heads):
            start = device * head_width + head * HEAD_SIZE
            grad = total[start : start + HEAD_SIZE].astype(jnp.bfloat16)
            output = output_ref[:, start : start + HEAD_SIZE].astype(jnp.float32).T
            rest = jnp.sum(grad.astype(jnp.float32) * output, axis=0, keepdims=True)
            for row in range(3):
                digit = rest.astype(jnp.bfloat16).astype(jnp.float32)
                held = jnp.where(row_at == DIGITS * head + row, digit, held)
                rest = rest - digit
            out_ref[device, head * HEAD_SIZE : (head + 1) * HEAD_SIZE] = grad
        out_ref[device, head_width:] = held.astype(jnp.bfloat16)


def project(resid, weights, attn_out):
    tokens, width = resid.shape
    parts, devices, heads, _, piece = weights.shape
    step = min(4, devices)
    out_rows = heads * HEAD_SIZE + DELTA_ROWS
    return pl.pallas_call(
        project_kernel,
        grid=(devices // step,),
        in_specs=[
            pl.BlockSpec((tokens, width), lambda n: (0, 0)),
            pl.BlockSpec((parts, step, heads, HEAD_SIZE, piece), lambda n: (0, n, 0, 0, 0)),
            pl.BlockSpec((tokens, step * heads * HEAD_SIZE), lambda n: (0, n)),
        ],
        out_specs=pl.BlockSpec((step, out_rows, tokens), lambda n: (n, 0, 0)),
        out_shape=jax.ShapeDtypeStruct((devices, out_rows, tokens), jnp.bfloat16),
        cost_estimate=pl.CostEstimate(
            flops=2 * tokens * width * devices * heads * HEAD_SIZE,
            bytes_accessed=2 * devices * heads * HEAD_SIZE * (width + 3 * tokens),
            transcendentals=0,
        ),
        name="project",
    )(resid, weights, attn_out)


def attention_kernel(packed_ref, grad_ref, lse_ref, out_ref, delta_ref, grad_t_ref, dqt_ref):
    j = pl.program_id(0)
    steps = pl.num_programs(0)
    heads = lse_ref.shape[0]
    length = packed_ref.shape[0]
    devices, _, tokens = grad_ref.shape
    block = min(BLOCK, length)
    scale = float(HEAD_SIZE) ** (-0.5)
    log2e = math.log2(math.e)
    key_from = heads * HEAD_SIZE
    value_from = key_from + HEAD_SIZE

    @pl.when(j == 0)
    def _():
        dqt_ref[...] = jnp.zeros_like(dqt_ref)
        for device in range(devices):
            cols = slice(device * tokens, (device + 1) * tokens)
            grad_t_ref[:, cols] = grad_ref[device, :key_from]
            digits = grad_ref[device, key_from:].astype(jnp.float32)
            for head in range(heads):
                rows = digits[DIGITS * head : DIGITS * (head + 1)]
                delta_ref[DIGITS * head : DIGITS * (head + 1), cols] = jnp.broadcast_to(
                    jnp.sum(rows, axis=0, keepdims=True), (DIGITS, tokens)
                )

    key_rows = pl.ds(pl.multiple_of(j * block, block), block)
    key = packed_ref[key_rows, key_from:value_from]
    value = packed_ref[key_rows, value_from : value_from + HEAD_SIZE]
    key_t = key.astype(jnp.float32).T.astype(jnp.bfloat16)

    def body(i, carry):
        dkey, dvalue = carry
        rows = pl.ds(pl.multiple_of(i * block, block), block)
        for head in range(heads):
            head_cols = slice(head * HEAD_SIZE, (head + 1) * HEAD_SIZE)
            query = packed_ref[rows, head_cols]
            grad_t = grad_t_ref[head_cols, rows]
            lse = lse_ref[head : head + 1, rows] * log2e
            delta = delta_ref[DIGITS * head : DIGITS * head + 1, rows]
            scores = contract_last(key, query)
            probs = jnp.exp2(scores * (scale * log2e) - lse)
            key_at = j * block + lax.broadcasted_iota(jnp.int32, scores.shape, 0)
            query_at = i * block + lax.broadcasted_iota(jnp.int32, scores.shape, 1)
            probs = jnp.where(key_at <= query_at, probs, 0.0)
            grad_probs = dot_nn(value, grad_t)
            grad_scores = (probs * (grad_probs - delta)).astype(jnp.bfloat16)
            dkey = dkey + dot_nn(grad_scores, query)
            dvalue = dvalue + contract_last(probs.astype(jnp.bfloat16), grad_t)
            dqt_ref[head_cols, rows] += dot_nn(key_t, grad_scores)
        return dkey, dvalue

    zero = jnp.zeros((block, HEAD_SIZE), jnp.float32)
    dkey, dvalue = lax.fori_loop(j, steps, body, (zero, zero))
    out_ref[key_rows, key_from:value_from] = (dkey * scale).astype(jnp.bfloat16)
    out_ref[key_rows, value_from:] = dvalue.astype(jnp.bfloat16)

    @pl.when(j == steps - 1)
    def _():
        for head in range(heads):
            head_cols = slice(head * HEAD_SIZE, (head + 1) * HEAD_SIZE)
            out_ref[:, head_cols] = (dqt_ref[head_cols, :].T * scale).astype(jnp.bfloat16)


def attention(packed, grad, lse):
    length, packed_width = packed.shape
    heads = lse.shape[0]
    block = min(BLOCK, length)

    def whole(shape):
        return pl.BlockSpec(shape, lambda j: (0,) * len(shape))

    return pl.pallas_call(
        attention_kernel,
        grid=(length // block,),
        in_specs=[whole(packed.shape), whole(grad.shape), whole(lse.shape)],
        out_specs=whole(packed.shape),
        out_shape=jax.ShapeDtypeStruct(packed.shape, jnp.bfloat16),
        scratch_shapes=[
            pltpu.VMEM((DIGITS * heads, length), jnp.float32),
            pltpu.VMEM((heads * HEAD_SIZE, length), jnp.bfloat16),
            pltpu.VMEM((heads * HEAD_SIZE, length), jnp.float32),
        ],
        compiler_params=pltpu.CompilerParams(
            dimension_semantics=("arbitrary",), vmem_limit_bytes=48 * 1024 * 1024
        ),
        cost_estimate=pl.CostEstimate(
            flops=10 * heads * length * length * HEAD_SIZE // 2,
            bytes_accessed=2 * length * (2 * packed_width + heads * HEAD_SIZE),
            transcendentals=heads * length * length // 2,
        ),
        name="attention",
    )(packed, grad, lse)


def assemble_kernel(packed_ref, query_ref, key_ref, value_ref):
    devices = packed_ref.shape[0]
    head_width = query_ref.shape[1] // devices
    total = packed_ref[0, :, head_width:].astype(jnp.float32)
    for device in range(1, devices):
        total = total + packed_ref[device, :, head_width:].astype(jnp.float32)
    key_ref[...] = total[:, :HEAD_SIZE].astype(jnp.bfloat16)
    value_ref[...] = total[:, HEAD_SIZE:].astype(jnp.bfloat16)
    for device in range(devices):
        cols = slice(device * head_width, (device + 1) * head_width)
        query_ref[:, cols] = packed_ref[device, :, :head_width]


def assemble(packed):
    devices, rows, packed_width = packed.shape
    shared = devices // KEY_VALUE_HEADS
    query_width = shared * (packed_width - 2 * HEAD_SIZE)
    widths = (query_width, HEAD_SIZE, HEAD_SIZE)
    return pl.pallas_call(
        assemble_kernel,
        grid=(KEY_VALUE_HEADS,),
        in_specs=[pl.BlockSpec((shared, rows, packed_width), lambda n: (n, 0, 0))],
        out_specs=[pl.BlockSpec((rows, width), lambda n: (0, n)) for width in widths],
        out_shape=[
            jax.ShapeDtypeStruct((rows, KEY_VALUE_HEADS * width), jnp.bfloat16)
            for width in widths
        ],
        name="assemble",
    )(packed)


def pick(array, index, axis):
    starts = [jnp.int32(0)] * array.ndim
    starts[axis] = index.astype(jnp.int32)
    sizes = list(array.shape)
    sizes[axis] = 1
    piece = lax.dynamic_slice(array, starts, sizes, allow_negative_indices=False)
    return lax.squeeze(piece, (axis,))


def scatter_sum(partial, groups, rows):
    grp_at = lax.axis_index("grp")
    core = lax.rem(grp_at, 2)
    place = lax.div(grp_at, 2)
    chips = groups // 2
    f32 = jnp.float32
    parts = partial.reshape(chips, 2, rows, partial.shape[1])
    keep = pick(parts, core, 1)
    send = pick(parts, 1 - core, 1)
    other = lax.ppermute(send, "grp", [(g, g ^ 1) for g in range(groups)])
    pair = (keep.astype(f32) + other.astype(f32)).astype(jnp.bfloat16)
    total = pick(pair, place, 0).astype(f32)
    for step in range(1, chips):
        block = pick(pair, lax.rem(place + step, chips), 0)
        moves = [(g, (g // 2 + step) % chips * 2 + g % 2) for g in range(groups)]
        block = lax.ppermute(block, "grp", moves)
        total = total + block.astype(f32)
    return total


def per_device(
    grad_out,
    hidden,
    norm_gain,
    expert_ids,
    gate_weights,
    w_gate,
    w_up,
    w_down,
    w_out,
    queries,
    keys,
    values,
    attn_out,
    lse,
):
    bf16, f32 = jnp.bfloat16, jnp.float32
    rows, width = hidden.shape
    topk = expert_ids.shape[1]
    groups = lax.axis_size("grp")
    inner = lax.axis_size("inner")
    grp_at = lax.axis_index("grp")
    experts = groups * inner
    capacity = max(2, 5 * rows * topk // (4 * experts))
    slots = groups * capacity
    column = groups * rows
    ff = w_gate.shape[2]
    head_width = queries.shape[1] // inner
    shared = inner // KEY_VALUE_HEADS

    hidden_f = hidden.astype(f32)
    inverse = lax.rsqrt(jnp.mean(hidden_f * hidden_f, axis=1, keepdims=True) + EPSILON)
    normed = (hidden_f * inverse * norm_gain).astype(bf16)

    normed_all = lax.all_gather(normed, "grp", axis=0, tiled=True)
    upstream_all = lax.all_gather(grad_out, "grp", axis=0, tiled=True)
    routing = jnp.concatenate([expert_ids.astype(f32).T, gate_weights.T], axis=0)
    routing = lax.all_gather(routing, "grp", axis=0, tiled=False)

    piece = width // groups
    w_piece = lax.dynamic_slice_in_dim(w_out, grp_at * piece, piece, axis=1)
    w_piece = jnp.broadcast_to(w_piece[None], (inner,) + w_piece.shape)
    w_piece = lax.all_to_all(w_piece, "inner", 0, 0, tiled=True)
    normed_all, w_piece = lax.optimization_barrier((normed_all, w_piece))
    w_whole = lax.all_gather(w_piece, "grp", axis=0, tiled=False)
    w_whole = w_whole.reshape(groups, inner, head_width // HEAD_SIZE, HEAD_SIZE, piece)

    ids_all = routing[:, :topk]
    gates_all = routing[:, topk:]
    mine = (grp_at * inner + lax.broadcasted_iota(jnp.int32, (1, inner, 1, 1), 1)).astype(f32)
    match = ids_all[:, None] == mine
    named = jnp.any(match, axis=2)
    gate = jnp.sum(jnp.where(match, gates_all[:, None], 0.0), axis=2)
    before = (
        lax.broadcasted_iota(jnp.int32, (rows, rows), 0)
        < lax.broadcasted_iota(jnp.int32, (rows, rows), 1)
    ).astype(bf16)
    rank = dot_nn(named.astype(bf16).reshape(groups * inner, rows), before)
    rank = rank.reshape(groups, inner, rows)
    block_at = lax.broadcasted_iota(jnp.int32, (groups, 1, 1), 0).astype(f32)
    slot = jnp.where(named, block_at * capacity + rank, -1.0)
    slot = slot.transpose(1, 0, 2).reshape(inner, 1, column)
    gate = gate.transpose(1, 0, 2).reshape(inner, 1, column)
    slot_at = lax.broadcasted_iota(jnp.int32, (1, slots, 1), 1).astype(f32)
    chosen = slot == slot_at
    picks = jnp.where(slot == slot_at, 1.0, 0.0).astype(bf16).reshape(inner * slots, column)
    picks = lax.optimization_barrier(picks)

    def to_experts(array):
        return lax.all_to_all(array, "inner", 0, 0, tiled=True).reshape(inner * slots, width)

    slot_gate = jnp.sum(jnp.where(chosen, gate, 0.0), axis=2)
    inputs = to_experts(dot_nn(picks, normed_all).astype(bf16).reshape(inner, slots, width))
    slot_gate = slot_gate.reshape(inner * slots, 1)
    upstream_rows = (dot_nn(picks, upstream_all) * slot_gate).astype(bf16)
    upstream_rows = to_experts(upstream_rows.reshape(inner, slots, width))

    kv = jnp.stack(
        [
            keys.reshape(rows, KEY_VALUE_HEADS, HEAD_SIZE),
            values.reshape(rows, KEY_VALUE_HEADS, HEAD_SIZE),
        ],
        axis=2,
    ).reshape(rows, KEY_VALUE_HEADS, 2 * HEAD_SIZE)
    kv = jnp.repeat(kv.transpose(1, 0, 2), shared, axis=0)
    packed = jnp.concatenate(
        [queries.reshape(rows, inner, head_width).transpose(1, 0, 2), kv], axis=2
    )

    w_gate_up = jnp.concatenate([w_gate[0], w_up[0]], axis=1)
    pre = dot_nn(inputs, w_gate_up)
    gate_pre = pre[:, :ff]
    up_pre = pre[:, ff:]
    sigmoid = jax.nn.sigmoid(gate_pre)
    gate_slope = (up_pre * sigmoid * (1.0 + gate_pre * (1.0 - sigmoid))).astype(bf16)
    up_slope = (gate_pre * sigmoid).astype(bf16)
    share = width // sum(SHARES)
    cuts = [share * sum(SHARES[:part]) for part in range(len(SHARES))] + [width]
    w_shares = [
        jnp.concatenate([w[0, low:high] for w in (w_gate, w_up)], axis=1)
        for low, high in zip(cuts[:-1], cuts[1:])
    ]
    upstream_rows, w_whole, packed, gate_slope, up_slope, w_shares = lax.optimization_barrier(
        (upstream_rows, w_whole, packed, gate_slope, up_slope, w_shares)
    )
    back_hidden = contract_last(upstream_rows, w_down[0])
    grad_gate = (back_hidden * gate_slope).astype(bf16)
    grad_up = (back_hidden * up_slope).astype(bf16)
    grad_both = jnp.concatenate([grad_gate, grad_up], axis=1)

    def add_up(rows_back):
        rows_back = rows_back.reshape(inner * slots, rows_back.shape[2])
        return contract_first(picks, rows_back).astype(bf16)

    sums = []
    grads = []
    for part in range(len(SHARES)):
        grads.append(contract_last(grad_both, w_shares[part]))
        grads[part] = grads[part].astype(bf16).reshape(inner, slots, -1)
    for part in range(len(SHARES)):
        if part > 0:
            returned, grads[part] = lax.optimization_barrier((returned, grads[part]))
        arrived = lax.all_to_all(grads[part], "inner", 0, 0, tiled=True)
        if part > 0:
            sums.append(scatter_sum(add_up(returned), groups, rows))
        returned = arrived
    packed, returned = lax.optimization_barrier((packed, returned))
    packed = lax.all_to_all(packed, "inner", 0, 0, tiled=True)
    packed = packed.reshape(inner * rows, head_width + 2 * HEAD_SIZE)
    sums.append(scatter_sum(add_up(returned), groups, rows))
    grad_normed = jnp.concatenate(sums, axis=1)

    gained = grad_normed * norm_gain
    statistic = jnp.mean(gained * hidden_f, axis=1, keepdims=True)
    grad_resid = (
        grad_out.astype(f32)
        + inverse * gained
        - hidden_f * inverse * inverse * inverse * statistic
    ).astype(bf16)

    head_grad = project(grad_resid, w_whole, attn_out)
    head_grad, packed = lax.optimization_barrier((head_grad, packed))
    head_grad = lax.all_to_all(head_grad, "inner", 0, 0, tiled=True)
    packed_grads = attention(packed, head_grad, lse)
    packed_grads = packed_grads.reshape(inner, rows, head_width + 2 * HEAD_SIZE)
    packed_grads = lax.all_to_all(packed_grads, "inner", 0, 0, tiled=True)
    queries_gradient, keys_gradient, values_gradient = assemble(packed_grads)
    return (grad_resid, queries_gradient, keys_gradient, values_gradient)


def solution(mesh):
    token = P(("grp", "inner"), None)
    expert = P(("grp", "inner"), None, None)
    placed = (
        token,
        token,
        P(),
        token,
        token,
        expert,
        expert,
        expert,
        P("inner", None),
        token,
        token,
        token,
        token,
        P("inner", "grp"),
    )

    return jax.shard_map(
        per_device,
        mesh=mesh,
        in_specs=placed,
        out_specs=(token, token, token, token),
        check_vma=False,
    )
```

time: 487 us -> 468 us (0.961)
  blocking collectives: 77.2 us -> 102 us
  Pallas kernels: 50.1 us -> 30.5 us
  starting transfers between devices: 51.5 us -> 32.4 us
  waiting for transfers between devices: 201 us -> 189 us
  matrix products: 51.7 us -> 62 us
    all_to_all x0 -> x1, blocking collectives: none -> 21 us  [per_device(): head_grad = lax.all_to_all(head_grad, 'inner', 0, 0, tiled=True)]
    pallas_call x5 -> x2, Pallas kernels: 46.3 us -> 26.8 us  [the longest x1 17.3 us: attention(): pl.pallas_call(attention_kernel, grid=(length // block,), in_specs=[whole...]
    all_to_all x3 -> x0, starting transfers between devices: 18.3 us -> none  [the longest x2 11.1 us: per_device(): grads.append(lax.all_to_all(grad, 'inner', 0, 0, tiled=True))]
    dot_general x3 -> x4, matrix products: 20.2 us -> 30.8 us  [dot_nn(): lax.dot_general(left, right, (((1,), (0,)), ((), ())), preferred_element_...]
    unnamed x52 -> x54, local copies, waits for them, and re-layouts: 10.5 us -> 3.61 us
    all_to_all x3 -> x0, waiting for transfers between devices: 5.27 us -> none  [the longest x2 5.27 us: per_device(): grads.append(lax.all_to_all(grad, 'inner', 0, 0, tiled=True))]
  transfers between devices with their start and end apart: 19 -> 16, of which waited for: 9 -> 8; matrix products, arithmetic and copies ran while one was open for 13% -> 17% of each run, Pallas kernels for 10% -> 2%
where the time goes in v4:
time: 468 us; the launch traced here: 467 us
  waiting for transfers between devices  189 us (40%)
  blocking collectives  102 us (22%)
  matrix products  62 us (13%)
  starting transfers between devices  32.4 us (7%)
  Pallas kernels  30.5 us (7%)
  other arithmetic  21.7 us (5%)
  local copies, waits for them, and re-layouts  15.1 us (3%)
  between operations  14.3 us (3%)
    all_to_all x2, waiting for transfers between devices, to_experts(): lax.all_to_all(array, 'inner', 0, 0, tiled=True)  118 us
    all_to_all x2, waiting for transfers between devices, per_device(): arrived = lax.all_to_all(grads[part], 'inner', 0, 0, tiled=True)  56.7 us
    all_to_all x1, blocking collectives, per_device(): w_piece = lax.all_to_all(w_piece, 'inner', 0, 0, tiled=True)  36.3 us
    all_to_all x1, blocking collectives, per_device(): packed_grads = lax.all_to_all(packed_grads, 'inner', 0, 0, tiled=True)  31.5 us
    dot_general x4, matrix products, dot_nn(): lax.dot_general(left, right, (((1,), (0,)), ((), ())), preferred_element_...  30.8 us
    dot_general x3, matrix products, contract_last(): lax.dot_general(left, right, (((1,), (1,)), ((), ())), preferred_element_...  21.4 us
    all_to_all x1, blocking collectives, per_device(): head_grad = lax.all_to_all(head_grad, 'inner', 0, 0, tiled=True)  21 us
    pallas_call x1, Pallas kernels, attention(): pl.pallas_call(attention_kernel, grid=(length // block,), in_specs=[whole...  17.3 us
  transfers between devices with their start and end apart: 16, of which 8 were waited for; matrix products, arithmetic and copies ran while one was open for 17% of the time, Pallas kernels for 2%

profile of v4, /device:TPU:0, one launch (start us, length us, event | category | flops | bytes accessed | tf_op | source)
XLA Modules:
  0.0 467.5 jit_solution(1661757142547432188)
XLA Ops:
  13.1 36.3 %all_to_all.40 = bf16[16,256,256]{2,1,0:T(8,128)(2,1)} all-to-all(bf16[16,256,256]{2,1,0:T(8,128)(2,1)S(1)} %broadcast_in_dim.61), channel_id=1, replica_groups=mesh['grp'=8,'inner'=16] {'inner'}, dimensions={0} | all-to-all | bytes 4194304 | tf_op jit(solution)/shard_map/all_to_all | solution.py:281
  49.6 13.3 %all-gather = f32[128,128]{1,0:T(8,128)S(1)} all-gather(f32[16,128]{1,0:T(8,128)S(1)} %pad_maximum_fusion.7), channel_id=2, replica_groups=mesh['grp'=8,'inner'=16] {'grp'}, dimensions={0}, use_global_device_ids=true | all-gather | bytes 73728 | tf_op jit(solution)/shard_map/all_gather | solution.py:276
  64.0 10.4 %convolution_convert_fusion.1 = bf16[1280,2048]{1,0:T(8,128)(2,1)} fusion(bf16[1280,1024]{1,0:T(8,128)(2,1)S(1)} %select_convert_fusion, bf16[1024,2048]{1,0:T(8,128)(2,1)} %all-gather.8.cloned.1.call-done), kind=kOutput, calls=%fused_computation.2 | convolution fusion | flops 5371330560 | bytes 12058624 | tf_op jit(solution)/shard_map/dot_general | solution.py:20
  74.5 4.7 %all-to-all-start.2 = ((bf16[16,80,2048]{2,1,0:T(8,128)(2,1)}), bf16[16,80,2048]{2,1,0:T(8,128)(2,1)}, u32[]{:S(2)}, u32[]{:S(2)}) async-start(bf16[16,80,2048]{2,1,0:T(8,128)(2,1)} %bitcast.112), calls=%async_computation.2 | async-start | bytes 10485760 | tf_op jit(solution)/shard_map/all_to_all | solution.py:308
  82.0 2.3 copy.67
  84.3 3.2 slice_bitcast_fusion.2
  87.6 10.0 %multiply_convert_fusion = bf16[1280,2048]{1,0:T(8,128)(2,1)} fusion(bf16[1280,1024]{1,0:T(8,128)(2,1)} %copy-done.10, bf16[1024,2048]{1,0:T(8,128)(2,1)} %all-gather.6.cloned.1.call-done, f32[1280]{0:T(1024)S(1)} %mul.104), kind=kOutput, calls=%fused_computation | convolution fusion | flops 5373952000 | bytes 12063744 | tf_op jit(solution)/shard_map/dot_general | solution.py:20
  97.6 61.9 %all-to-all-done.2 = bf16[16,80,2048]{2,1,0:T(8,128)(2,1)} async-done(((bf16[16,80,2048]{2,1,0:T(8,128)(2,1)}), bf16[16,80,2048]{2,1,0:T(8,128)(2,1)}, u32[]{:S(2)}, u32[]{:S(2)}) %all-to-all-start.2) | async-done | bytes 5242912 | tf_op jit(solution)/shard_map/all_to_all | solution.py:308
  159.5 4.8 %all-to-all-start = ((bf16[16,80,2048]{2,1,0:T(8,128)(2,1)}), bf16[16,80,2048]{2,1,0:T(8,128)(2,1)}, u32[]{:S(2)}, u32[]{:S(2)}) async-start(bf16[16,80,2048]{2,1,0:T(8,128)(2,1)} %bitcast.111), calls=%async_computation | async-start | bytes 10485760 | tf_op jit(solution)/shard_map/all_to_all | solution.py:308
  164.4 3.0 pad_maximum_fusion.5
  172.8 10.2 %fusion = f32[1280,1536]{1,0:T(8,128)S(1)} fusion(bf16[1280,2048]{1,0:T(8,128)(2,1)} %bitcast.17, bf16[2048,768]{1,0:T(8,128)(2,1)S(1)} %bitcast.116, bf16[2048,768]{1,0:T(8,128)(2,1)S(1)} %bitcast.117), kind=kOutput, calls=%fused_computation.3 | convolution fusion | flops 8065646592 | bytes 19398656 | tf_op jit(solution)/shard_map/dot_general | solution.py:20
  183.0 2.9 multiply_convert_fusion.3
  185.9 56.3 %all-to-all-done = bf16[16,80,2048]{2,1,0:T(8,128)(2,1)} async-done(((bf16[16,80,2048]{2,1,0:T(8,128)(2,1)}), bf16[16,80,2048]{2,1,0:T(8,128)(2,1)}, u32[]{:S(2)}, u32[]{:S(2)}) %all-to-all-start) | async-done | bytes 5242912 | tf_op jit(solution)/shard_map/all_to_all | solution.py:308
  242.2 8.0 %multiply_convert_fusion.2 = (bf16[1280,768]{1,0:T(8,128)(2,1)S(1)}, bf16[1280,768]{1,0:T(8,128)(2,1)S(1)}) fusion(bf16[1280,768]{1,0:T(8,128)(2,1)} %get-tuple-element.25, bf16[1280,768]{1,0:T(8,128)(2,1)} %get-tuple-element.26, bf16[1280,2048]{1,0:T(8,128)(2,1)} %bitcast.8, bf16[1,768,2048]{2,1,0:T(8,128)(2,1)S(1)} %copy-done), kind=kOutput, calls=%fused_computation.16 | convolution fusion | flops 4032430080 | bytes 16252928 | tf_op jit(solution)/shard_map/dot_general | solution.py:26
  250.3 6.7 %convolution_convert_fusion = bf16[1280,1280]{1,0:T(8,128)(2,1)} fusion(bf16[1280,1536]{1,0:T(8,128)(2,1)S(1)} %copy-done.7, bf16[1280,768]{1,0:T(8,128)(2,1)S(1)} %get-tuple-element.43, bf16[1280,768]{1,0:T(8,128)(2,1)S(1)} %get-tuple-element.42), kind=kOutput, calls=%fused_computation.1 | convolution fusion | flops 5042667520 | bytes 11141120 | tf_op jit(solution)/shard_map/dot_general | solution.py:26
  257.0 5.4 %all-to-all-start.3 = ((bf16[16,80,1280]{2,1,0:T(8,128)(2,1)}), bf16[16,80,1280]{2,1,0:T(8,128)(2,1)}, u32[]{:S(2)}, u32[]{:S(2)}) async-start(bf16[16,80,1280]{2,1,0:T(8,128)(2,1)} %bitcast.115), calls=%async_computation.3 | async-start | bytes 6553600 | tf_op jit(solution)/shard_map/all_to_all | solution.py:361
  262.4 6.7 %convolution_convert_fusion.3 = bf16[1280,768]{1,0:T(8,128)(2,1)} fusion(bf16[768,1536]{1,0:T(8,128)(2,1)S(1)} %copy-done.14, bf16[1280,768]{1,0:T(8,128)(2,1)} %copy-done.25, bf16[1280,768]{1,0:T(8,128)(2,1)} %copy-done.24), kind=kOutput, calls=%fused_computation.20 | convolution fusion | flops 3028746240 | bytes 8257536 | tf_op jit(solution)/shard_map/dot_general | solution.py:26
  269.1 39.4 %all-to-all-done.3 = bf16[16,80,1280]{2,1,0:T(8,128)(2,1)} async-done(((bf16[16,80,1280]{2,1,0:T(8,128)(2,1)}), bf16[16,80,1280]{2,1,0:T(8,128)(2,1)}, u32[]{:S(2)}, u32[]{:S(2)}) %all-to-all-start.3) | async-done | bytes 3276832 | tf_op jit(solution)/shard_map/all_to_all | solution.py:361
  308.5 4.7 all-to-all-start.4
  313.2 5.8 %convolution_convert_fusion.2 = bf16[1024,1280]{1,0:T(8,128)(2,1)S(1)} fusion(bf16[1280,1024]{1,0:T(8,128)(2,1)S(1)} %copy-done.11, bf16[1280,1280]{1,0:T(8,128)(2,1)} %bitcast.27), kind=kOutput, calls=%fused_computation.19 | convolution fusion | flops 3356753920 | bytes 8519680 | tf_op jit(solution)/shard_map/dot_general | solution.py:32
  321.7 17.3 %all-to-all-done.4 = bf16[16,80,768]{2,1,0:T(8,128)(2,1)} async-done(((bf16[16,80,768]{2,1,0:T(8,128)(2,1)}), bf16[16,80,768]{2,1,0:T(8,128)(2,1)}, u32[]{:S(2)}, u32[]{:S(2)}) %all-to-all-start.4) | async-done | bytes 1966112 | tf_op jit(solution)/shard_map/all_to_all | solution.py:361
  339.0 4.0 convolution_convert_fusion.4
  348.4 2.5 collective-permute-start.2
  351.2 3.7 all-to-all-start.5
  361.2 5.6 %collective-permute-done.2 = bf16[128,1280]{1,0:T(8,128)(2,1)} collective-permute-done((bf16[128,1280]{1,0:T(8,128)(2,1)}, bf16[128,1280]{1,0:T(8,128)(2,1)}, u32[]{:S(2)}, u32[]{:S(2)}) %collective-permute-start.2) | collective-permute-done | bytes 327712 | tf_op jit(solution)/shard_map/ppermute | solution.py:234
  368.2 2.7 collective-permute-done.5
  370.8 3.8 collective-permute-done.6
  376.3 9.6 %project.1 = bf16[16,272,128]{2,1,0:T(8,128)(2,1)} custom-call(bf16[128,2048]{1,0:T(8,128)(2,1)} %fusion.18.resid_ref, bf16[8,16,2,128,256]{4,3,2,1,0:T(8,128)(2,1)} %bitcast.110, bf16[128,4096]{1,0:T(8,128)(2,1)} %output_ref.1), custom_call_target="tpu_custom_call" | custom-call | flops 2147483648 | bytes 19922944 | tf_op jit(solution)/shard_map/project/pallas_call | solution.py:66
  387.5 21.0 %all_to_all.41.grad_ref = bf16[16,272,128]{2,1,0:T(8,128)(2,1)S(1)} all-to-all(bf16[16,272,128]{2,1,0:T(8,128)(2,1)} %project.1), channel_id=1, replica_groups=mesh['grp'=8,'inner'=16] {'inner'}, dimensions={0} | all-to-all | bytes 2228224 | tf_op jit(solution)/shard_map/all_to_all | solution.py:381
  408.5 17.3 %attention.1 = bf16[2048,512]{1,0:T(8,128)(2,1)S(1)} custom-call(bf16[2048,512]{1,0:T(8,128)(2,1)S(1)} %bitcast.108, bf16[16,272,128]{2,1,0:T(8,128)(2,1)S(1)} %all_to_all.41.grad_ref, f32[2,2048]{1,0:T(2,128)S(1)} %copy-done.2), custom_call_target="tpu_custom_call" | custom-call | flops 5368709120 | bytes 5242880 | tf_op jit(solution)/shard_map/attention/pallas_call | solution.py:156
  425.8 31.5 %all_to_all.42.packed_ref = bf16[16,128,512]{2,1,0:T(8,128)(2,1)} all-to-all(bf16[16,128,512]{2,1,0:T(8,128)(2,1)S(1)} %bitcast.109), channel_id=1, replica_groups=mesh['grp'=8,'inner'=16] {'inner'}, dimensions={0} | all-to-all | bytes 4194304 | tf_op jit(solution)/shard_map/all_to_all | solution.py:384
  457.3 3.6 assemble.1
  (113 shorter events, 34.5 us)
Async XLA Ops:
  7.2 235.0 %copy-start = (bf16[1,768,2048]{2,1,0:T(8,128)(2,1)S(1)}, bf16[1,768,2048]{2,1,0:T(8,128)(2,1)}, u32[]{:S(2)}) copy-start(bf16[1,768,2048]{2,1,0:T(8,128)(2,1)} %param.21) | copy-start | bytes 9437188
  7.2 42.2 %all-gather.8.cloned.1.call-start = ((), (), s32[]{:S(2)}) async-start(), calls=%async_computation.9 | async-start | bytes 4718592 | tf_op jit(solution)/shard_map/all_gather | solution.py:273
  11.2 76.4 %all-gather.6.cloned.1.call-start = ((), (), s32[]{:S(2)}) async-start(), calls=%async_computation.8 | async-start | bytes 4718592 | tf_op jit(solution)/shard_map/all_gather | solution.py:274
  11.9 230.3 %all-gather.10.cloned.1.call-start = ((), (), s32[]{:S(2)}) async-start(), calls=%async_computation.10 | async-start | bytes 18874368 | tf_op jit(solution)/shard_map/all_gather | solution.py:283
  13.1 36.4 %copy-start.20 = (s32[128,8]{0,1:T(8,128)S(1)}, s32[128,8]{0,1:T(8,128)}, u32[]{:S(2)}) copy-start(s32[128,8]{0,1:T(8,128)} %param.17) | copy-start | bytes 12292
  13.1 36.4 %copy-start.21 = (f32[128,8]{0,1:T(8,128)S(1)}, f32[128,8]{0,1:T(8,128)}, u32[]{:S(2)}) copy-start(f32[128,8]{0,1:T(8,128)} %param.18) | copy-start | bytes 12292
  64.0 10.5 %copy-start.10 = (bf16[1280,1024]{1,0:T(8,128)(2,1)}, bf16[1280,1024]{1,0:T(8,128)(2,1)S(1)}, u32[]{:S(2)}) copy-start(bf16[1280,1024]{1,0:T(8,128)(2,1)S(1)} %select_convert_fusion) | copy-start | bytes 7864324
  74.5 5.6 %copy-start.18 = (bf16[128,512]{1,0:T(8,128)(2,1)S(1)}, bf16[128,512]{1,0:T(8,128)(2,1)}, u32[]{:S(2)}) copy-start(bf16[128,512]{1,0:T(8,128)(2,1)} %param.25) | copy-start | bytes 393220
  74.5 85.0 %all-to-all-start.2 = ((bf16[16,80,2048]{2,1,0:T(8,128)(2,1)}), bf16[16,80,2048]{2,1,0:T(8,128)(2,1)}, u32[]{:S(2)}, u32[]{:S(2)}) async-start(bf16[16,80,2048]{2,1,0:T(8,128)(2,1)} %bitcast.112), calls=%async_computation.2 | async-start | bytes 10485760 | tf_op jit(solution)/shard_map/all_to_all | solution.py:308
  159.5 82.7 %all-to-all-start = ((bf16[16,80,2048]{2,1,0:T(8,128)(2,1)}), bf16[16,80,2048]{2,1,0:T(8,128)(2,1)}, u32[]{:S(2)}, u32[]{:S(2)}) async-start(bf16[16,80,2048]{2,1,0:T(8,128)(2,1)} %bitcast.111), calls=%async_computation | async-start | bytes 10485760 | tf_op jit(solution)/shard_map/all_to_all | solution.py:308
  242.2 8.1 %copy-start.7 = (bf16[1280,1536]{1,0:T(8,128)(2,1)S(1)}, bf16[1280,1536]{1,0:T(8,128)(2,1)}, u32[]{:S(2)}) copy-start(bf16[1280,1536]{1,0:T(8,128)(2,1)} %pad_maximum_fusion) | copy-start | bytes 11796484
  250.3 6.7 %copy-start.24 = (bf16[1280,768]{1,0:T(8,128)(2,1)}, bf16[1280,768]{1,0:T(8,128)(2,1)S(1)}, u32[]{:S(2)}) copy-start(bf16[1280,768]{1,0:T(8,128)(2,1)S(1)} %get-tuple-element.42) | copy-start | bytes 5898244
  250.3 6.7 %copy-start.25 = (bf16[1280,768]{1,0:T(8,128)(2,1)}, bf16[1280,768]{1,0:T(8,128)(2,1)S(1)}, u32[]{:S(2)}) copy-start(bf16[1280,768]{1,0:T(8,128)(2,1)S(1)} %get-tuple-element.43) | copy-start | bytes 5898244
  257.0 51.5 %all-to-all-start.3 = ((bf16[16,80,1280]{2,1,0:T(8,128)(2,1)}), bf16[16,80,1280]{2,1,0:T(8,128)(2,1)}, u32[]{:S(2)}, u32[]{:S(2)}) async-start(bf16[16,80,1280]{2,1,0:T(8,128)(2,1)} %bitcast.115), calls=%async_computation.3 | async-start | bytes 6553600 | tf_op jit(solution)/shard_map/all_to_all | solution.py:361
  269.1 44.1 %copy-start.11 = (bf16[1280,1024]{1,0:T(8,128)(2,1)S(1)}, bf16[1280,1024]{1,0:T(8,128)(2,1)}, u32[]{:S(2)}) copy-start(bf16[1280,1024]{1,0:T(8,128)(2,1)} %copy-done.10) | copy-start | bytes 7864324
  308.5 30.5 %all-to-all-start.4 = ((bf16[16,80,768]{2,1,0:T(8,128)(2,1)}), bf16[16,80,768]{2,1,0:T(8,128)(2,1)}, u32[]{:S(2)}, u32[]{:S(2)}) async-start(bf16[16,80,768]{2,1,0:T(8,128)(2,1)} %bitcast.120), calls=%async_computation.4 | async-start | bytes 3932160 | tf_op jit(solution)/shard_map/all_to_all | solution.py:361
  321.7 22.3 %collective-permute-start = (bf16[4,128,1280]{2,1,0:T(8,128)(2,1)}, bf16[4,128,1280]{2,1,0:T(8,128)(2,1)}, u32[]{:S(2)}, u32[]{:S(2)}) collective-permute-start(bf16[4,128,1280]{2,1,0:T(8,128)(2,1)} %dynamic-slice_bitcast_fusion), channel_id=1, source_target_pairs={{0,16},{16,0},{32,48},{48,32},{64,80},{80,64},{96,112},{112,96},{1... | collective-permute-start | bytes 3932168 | tf_op jit(solution)/shard_map/ppermute | solution.py:228
  344.0 10.9 %collective-permute-start.4 = (bf16[4,128,768]{2,1,0:T(8,128)(2,1)}, bf16[4,128,768]{2,1,0:T(8,128)(2,1)}, u32[]{:S(2)}, u32[]{:S(2)}) collective-permute-start(bf16[4,128,768]{2,1,0:T(8,128)(2,1)} %dynamic-slice_bitcast_fusion.1), channel_id=1, source_target_pairs={{0,16},{16,0},{32,48},{48,32},{64,80},{80,64},{96,112},{112,96},{1... | collective-permute-start | bytes 2359304 | tf_op jit(solution)/shard_map/ppermute | solution.py:228
  345.7 5.5 %copy-start.4 = (bf16[4,128,1280]{2,1,0:T(8,128)(2,1)}, bf16[4,128,1280]{2,1,0:T(8,128)(2,1)S(1)}, u32[]{:S(2)}) copy-start(bf16[4,128,1280]{2,1,0:T(8,128)(2,1)S(1)} %fusion.8) | copy-start | bytes 3932164
  346.7 12.7 %collective-permute-start.1 = (bf16[128,1280]{1,0:T(8,128)(2,1)}, bf16[128,1280]{1,0:T(8,128)(2,1)S(1)}, u32[]{:S(2)}, u32[]{:S(2)}) collective-permute-start(bf16[128,1280]{1,0:T(8,128)(2,1)} %get-tuple-element.44), channel_id=1, source_target_pairs={{0,32},{16,48},{32,64},{48,80},{64,96},{80,112},{96,0},{112,16},{1... | collective-permute-start | bytes 983048 | tf_op jit(solution)/shard_map/ppermute | solution.py:234
  348.4 18.5 %collective-permute-start.2 = (bf16[128,1280]{1,0:T(8,128)(2,1)}, bf16[128,1280]{1,0:T(8,128)(2,1)}, u32[]{:S(2)}, u32[]{:S(2)}) collective-permute-start(bf16[128,1280]{1,0:T(8,128)(2,1)} %get-tuple-element.46), channel_id=1, source_target_pairs={{0,64},{16,80},{32,96},{48,112},{64,0},{80,16},{96,32},{112,48},{1... | collective-permute-start | bytes 983048 | tf_op jit(solution)/shard_map/ppermute | solution.py:234
  350.9 15.9 %collective-permute-start.3 = (bf16[128,1280]{1,0:T(8,128)(2,1)S(1)}, bf16[128,1280]{1,0:T(8,128)(2,1)}, u32[]{:S(2)}, u32[]{:S(2)}) collective-permute-start(bf16[128,1280]{1,0:T(8,128)(2,1)S(1)} %get-tuple-element.45), channel_id=1, source_target_pairs={{0,96},{16,112},{32,0},{48,16},{64,32},{80,48},{96,64},{112,80},{1... | collective-permute-start | bytes 983048 | tf_op jit(solution)/shard_map/ppermute | solution.py:234
  351.2 36.3 %all-to-all-start.5 = ((bf16[16,128,512]{2,1,0:T(8,128)(2,1)}), bf16[16,128,512]{2,1,0:T(8,128)(2,1)S(1)}, u32[]{:S(2)}, u32[]{:S(2)}) async-start(bf16[16,128,512]{2,1,0:T(8,128)(2,1)} %pad_maximum_fusion.5), calls=%async_computation.5 | async-start | bytes 4194304 | tf_op jit(solution)/shard_map/all_to_all | solution.py:366
  354.9 19.9 %copy-start.3 = (bf16[128,2048]{1,0:T(8,128)(2,1)S(1)}, bf16[128,2048]{1,0:T(8,128)(2,1)}, u32[]{:S(2)}) copy-start(bf16[128,2048]{1,0:T(8,128)(2,1)} %param.15) | copy-start | bytes 1572868
  354.9 19.9 %copy-start.19 = (f32[2048]{0:T(1024)S(1)}, f32[2048]{0:T(1024)}, u32[]{:S(2)}) copy-start(f32[2048]{0:T(1024)} %param.16) | copy-start | bytes 24580
  356.6 18.5 %copy-start.15 = (bf16[128,2048]{1,0:T(8,128)(2,1)S(1)}, bf16[128,2048]{1,0:T(8,128)(2,1)}, u32[]{:S(2)}) copy-start(bf16[128,2048]{1,0:T(8,128)(2,1)} %param.14) | copy-start | bytes 1572868
  356.6 18.5 %copy-start.23 = (f32[128]{0:T(128)S(1)}, f32[128]{0:T(128)}, u32[]{:S(2)}) copy-start(f32[128]{0:T(128)} %copy-done.22) | copy-start | bytes 1540
  356.6 14.2 %collective-permute-start.5 = (bf16[128,768]{1,0:T(8,128)(2,1)S(1)}, bf16[128,768]{1,0:T(8,128)(2,1)S(1)}, u32[]{:S(2)}, u32[]{:S(2)}) collective-permute-start(bf16[128,768]{1,0:T(8,128)(2,1)S(1)} %get-tuple-element.47), channel_id=1, source_target_pairs={{0,32},{16,48},{32,64},{48,80},{64,96},{80,112},{96,0},{112,16},{1... | collective-permute-start | bytes 589832 | tf_op jit(solution)/shard_map/ppermute | solution.py:234
  358.4 16.2 %collective-permute-start.6 = (bf16[128,768]{1,0:T(8,128)(2,1)S(1)}, bf16[128,768]{1,0:T(8,128)(2,1)S(1)}, u32[]{:S(2)}, u32[]{:S(2)}) collective-permute-start(bf16[128,768]{1,0:T(8,128)(2,1)S(1)} %get-tuple-element.49), channel_id=1, source_target_pairs={{0,64},{16,80},{32,96},{48,112},{64,0},{80,16},{96,32},{112,48},{1... | collective-permute-start | bytes 589832 | tf_op jit(solution)/shard_map/ppermute | solution.py:234
  359.4 15.2 %collective-permute-start.7 = (bf16[128,768]{1,0:T(8,128)(2,1)S(1)}, bf16[128,768]{1,0:T(8,128)(2,1)S(1)}, u32[]{:S(2)}, u32[]{:S(2)}) collective-permute-start(bf16[128,768]{1,0:T(8,128)(2,1)S(1)} %get-tuple-element.48), channel_id=1, source_target_pairs={{0,96},{16,112},{32,0},{48,16},{64,32},{80,48},{96,64},{112,80},{1... | collective-permute-start | bytes 589832 | tf_op jit(solution)/shard_map/ppermute | solution.py:234
  376.3 32.2 %copy-start.2 = (f32[2,2048]{1,0:T(2,128)S(1)}, f32[2,2048]{1,0:T(2,128)}, u32[]{:S(2)}) copy-start(f32[2,2048]{1,0:T(2,128)} %lse_ref.1) | copy-start | bytes 49156
  425.7 35.2 %copy-start.1 = (bf16[1,768,2048]{2,1,0:T(8,128)(2,1)S(1)}, bf16[1,768,2048]{2,1,0:T(8,128)(2,1)}, u32[]{:S(2)}) copy-start(bf16[1,768,2048]{2,1,0:T(8,128)(2,1)} %param.21) | copy-start | bytes 9437188
  (10 other events, 35.6 us)
Sparse Core Ops, SparseCore 0:
  11.3 34.5 all-gather.7
  47.6 32.0 all-gather.5
  81.4 84.7 all-gather.9

commit v5 on v4

--- a/solution.py
+++ b/solution.py
@@ -279,10 +279,6 @@
     w_piece = lax.dynamic_slice_in_dim(w_out, grp_at * piece, piece, axis=1)
     w_piece = jnp.broadcast_to(w_piece[None], (inner,) + w_piece.shape)
     w_piece = lax.all_to_all(w_piece, "inner", 0, 0, tiled=True)
-    normed_all, w_piece = lax.optimization_barrier((normed_all, w_piece))
-    w_whole = lax.all_gather(w_piece, "grp", axis=0, tiled=False)
-    w_whole = w_whole.reshape(groups, inner, head_width // HEAD_SIZE, HEAD_SIZE, piece)
-
     ids_all = routing[:, :topk]
     gates_all = routing[:, topk:]
     mine = (grp_at * inner + lax.broadcasted_iota(jnp.int32, (1, inner, 1, 1), 1)).astype(f32)
@@ -308,7 +304,11 @@
         return lax.all_to_all(array, "inner", 0, 0, tiled=True).reshape(inner * slots, width)
 
     slot_gate = jnp.sum(jnp.where(chosen, gate, 0.0), axis=2)
-    inputs = to_experts(dot_nn(picks, normed_all).astype(bf16).reshape(inner, slots, width))
+    input_rows = dot_nn(picks, normed_all).astype(bf16)
+    input_rows, w_piece = lax.optimization_barrier((input_rows, w_piece))
+    w_whole = lax.all_gather(w_piece, "grp", axis=0, tiled=False)
+    w_whole = w_whole.reshape(groups, inner, head_width // HEAD_SIZE, HEAD_SIZE, piece)
+    inputs = to_experts(input_rows.reshape(inner, slots, width))
     slot_gate = slot_gate.reshape(inner * slots, 1)
     upstream_rows = (dot_nn(picks, upstream_all) * slot_gate).astype(bf16)
     upstream_rows = to_experts(upstream_rows.reshape(inner, slots, width))

time: 468 us -> 449 us (0.959)
  blocking collectives: 102 us -> 66 us
  starting transfers between devices: 32.4 us -> 40.2 us
  waiting for transfers between devices: 189 us -> 196 us
    all_to_all x1 -> x0, blocking collectives: 36.3 us -> none  [per_device(): w_piece = lax.all_to_all(w_piece, 'inner', 0, 0, tiled=True)]
    all_to_all x2, waiting for transfers between devices: 118 us -> 108 us  [to_experts(): lax.all_to_all(array, 'inner', 0, 0, tiled=True)]
    all_gather x1, waiting for transfers between devices: 0.01 us -> 8.26 us  [per_device(): upstream_all = lax.all_gather(grad_out, 'grp', axis=0, tiled=True)]
    all_to_all x0 -> x1, starting transfers between devices: none -> 8.04 us  [per_device(): w_piece = lax.all_to_all(w_piece, 'inner', 0, 0, tiled=True)]
    all_gather x1, waiting for transfers between devices: 0.01 us -> 7.32 us  [per_device(): normed_all = lax.all_gather(normed, 'grp', axis=0, tiled=True)]
  transfers between devices with their start and end apart: 16 -> 17, of which waited for: 8 -> 11; matrix products, arithmetic and copies ran while one was open for 17% -> 18% of each run, Pallas kernels for 2% -> 2%
where the time goes in v5:
time: 449 us; the launch traced here: 448 us
  waiting for transfers between devices  196 us (44%)
  blocking collectives  66 us (15%)
  matrix products  61.3 us (14%)
  starting transfers between devices  40.2 us (9%)
  Pallas kernels  30.5 us (7%)
  other arithmetic  23.1 us (5%)
  local copies, waits for them, and re-layouts  16.7 us (4%)
  between operations  14.3 us (3%)
    all_to_all x2, waiting for transfers between devices, to_experts(): lax.all_to_all(array, 'inner', 0, 0, tiled=True)  108 us
    all_to_all x2, waiting for transfers between devices, per_device(): arrived = lax.all_to_all(grads[part], 'inner', 0, 0, tiled=True)  56.2 us
    all_to_all x1, blocking collectives, per_device(): packed_grads = lax.all_to_all(packed_grads, 'inner', 0, 0, tiled=True)  31.6 us
    dot_general x4, matrix products, dot_nn(): lax.dot_general(left, right, (((1,), (0,)), ((), ())), preferred_element_...  30 us
    dot_general x3, matrix products, contract_last(): lax.dot_general(left, right, (((1,), (1,)), ((), ())), preferred_element_...  21.4 us
    all_to_all x1, blocking collectives, per_device(): head_grad = lax.all_to_all(head_grad, 'inner', 0, 0, tiled=True)  20.8 us
    pallas_call x1, Pallas kernels, attention(): pl.pallas_call(attention_kernel, grid=(length // block,), in_specs=[whole...  17.3 us
    ppermute x6, waiting for transfers between devices, scatter_sum(): block = lax.ppermute(block, 'grp', moves)  14.5 us
  transfers between devices with their start and end apart: 17, of which 11 were waited for; matrix products, arithmetic and copies ran while one was open for 18% of the time, Pallas kernels for 2%

profile of v5, /device:TPU:0, one launch (start us, length us, event | category | flops | bytes accessed | tf_op | source)
XLA Modules:
  0.0 447.9 jit_solution(12912938575698957053)
XLA Ops:
  14.4 8.0 %all-to-all-start.1 = ((bf16[16,256,256]{2,1,0:T(8,128)(2,1)}), bf16[16,256,256]{2,1,0:T(8,128)(2,1)}, u32[]{:S(2)}, u32[]{:S(2)}) async-start(bf16[16,256,256]{2,1,0:T(8,128)(2,1)} %broadcast_in_dim.61), calls=%async_computation.1 | async-start | bytes 4194304 | tf_op jit(solution)/shard_map/all_to_all | solution.py:281
  22.7 13.5 %all-gather = f32[128,128]{1,0:T(8,128)S(1)} all-gather(f32[16,128]{1,0:T(8,128)S(1)} %pad_maximum_fusion.7), channel_id=2, replica_groups=mesh['grp'=8,'inner'=16] {'grp'}, dimensions={0}, use_global_device_ids=true | all-gather | bytes 73728 | tf_op jit(solution)/shard_map/all_gather | solution.py:276
  38.8 7.3 %all-gather.8.cloned.1.call-done = bf16[1024,2048]{1,0:T(8,128)(2,1)} async-done(((bf16[128,2048]{1,0:T(8,128)(2,1)}), bf16[1024,2048]{1,0:T(8,128)(2,1)}) %all-gather.8.cloned.1.call-update) | async-done | bytes 4194320 | tf_op jit(solution)/shard_map/all_gather | solution.py:273
  46.2 9.8 %convolution_convert_fusion.1 = bf16[1280,2048]{1,0:T(8,128)(2,1)} fusion(bf16[1280,1024]{1,0:T(8,128)(2,1)} %select_convert_fusion, bf16[1024,2048]{1,0:T(8,128)(2,1)} %all-gather.8.cloned.1.call-done), kind=kOutput, calls=%fused_computation.2 | convolution fusion | flops 5371330560 | bytes 12058624 | tf_op jit(solution)/shard_map/dot_general | solution.py:20
  56.0 7.1 %all-to-all-start.2 = ((bf16[16,80,2048]{2,1,0:T(8,128)(2,1)}), bf16[16,80,2048]{2,1,0:T(8,128)(2,1)}, u32[]{:S(2)}, u32[]{:S(2)}) async-start(bf16[16,80,2048]{2,1,0:T(8,128)(2,1)} %bitcast.111), calls=%async_computation.2 | async-start | bytes 10485760 | tf_op jit(solution)/shard_map/all_to_all | solution.py:304
  66.1 2.3 copy.67
  68.4 3.3 slice_bitcast_fusion.2
  71.6 8.3 %all-gather.6.cloned.1.call-done = bf16[1024,2048]{1,0:T(8,128)(2,1)} async-done(((bf16[128,2048]{1,0:T(8,128)(2,1)}), bf16[1024,2048]{1,0:T(8,128)(2,1)}) %all-gather.6.cloned.1.call-update) | async-done | bytes 4194320 | tf_op jit(solution)/shard_map/all_gather | solution.py:274
  79.9 9.9 %multiply_convert_fusion = bf16[1280,2048]{1,0:T(8,128)(2,1)} fusion(bf16[1280,1024]{1,0:T(8,128)(2,1)} %select_convert_fusion, bf16[1024,2048]{1,0:T(8,128)(2,1)} %all-gather.6.cloned.1.call-done, f32[1280]{0:T(1024)S(1)} %mul.104), kind=kOutput, calls=%fused_computation | convolution fusion | flops 5373952000 | bytes 12063744 | tf_op jit(solution)/shard_map/dot_general | solution.py:20
  89.8 52.2 %all-to-all-done.2 = bf16[16,80,2048]{2,1,0:T(8,128)(2,1)} async-done(((bf16[16,80,2048]{2,1,0:T(8,128)(2,1)}), bf16[16,80,2048]{2,1,0:T(8,128)(2,1)}, u32[]{:S(2)}, u32[]{:S(2)}) %all-to-all-start.2) | async-done | bytes 5242912 | tf_op jit(solution)/shard_map/all_to_all | solution.py:304
  142.0 5.4 %all-to-all-start = ((bf16[16,80,2048]{2,1,0:T(8,128)(2,1)}), bf16[16,80,2048]{2,1,0:T(8,128)(2,1)}, u32[]{:S(2)}, u32[]{:S(2)}) async-start(bf16[16,80,2048]{2,1,0:T(8,128)(2,1)} %bitcast.112), calls=%async_computation | async-start | bytes 10485760 | tf_op jit(solution)/shard_map/all_to_all | solution.py:304
  147.5 2.9 pad_maximum_fusion.5
  155.8 10.2 %fusion = f32[1280,1536]{1,0:T(8,128)S(1)} fusion(bf16[1280,2048]{1,0:T(8,128)(2,1)} %bitcast.17, bf16[2048,768]{1,0:T(8,128)(2,1)S(1)} %bitcast.116, bf16[2048,768]{1,0:T(8,128)(2,1)S(1)} %bitcast.117), kind=kOutput, calls=%fused_computation.3 | convolution fusion | flops 8065646592 | bytes 19398656 | tf_op jit(solution)/shard_map/dot_general | solution.py:20
  166.0 2.9 multiply_convert_fusion.3
  168.9 55.5 %all-to-all-done = bf16[16,80,2048]{2,1,0:T(8,128)(2,1)} async-done(((bf16[16,80,2048]{2,1,0:T(8,128)(2,1)}), bf16[16,80,2048]{2,1,0:T(8,128)(2,1)}, u32[]{:S(2)}, u32[]{:S(2)}) %all-to-all-start) | async-done | bytes 5242912 | tf_op jit(solution)/shard_map/all_to_all | solution.py:304
  224.5 8.0 %multiply_convert_fusion.2 = (bf16[1280,768]{1,0:T(8,128)(2,1)S(1)}, bf16[1280,768]{1,0:T(8,128)(2,1)S(1)}) fusion(bf16[1280,768]{1,0:T(8,128)(2,1)} %get-tuple-element.25, bf16[1280,768]{1,0:T(8,128)(2,1)} %get-tuple-element.26, bf16[1280,2048]{1,0:T(8,128)(2,1)} %bitcast.8, bf16[1,768,2048]{2,1,0:T(8,128)(2,1)S(1)} %copy-done), kind=kOutput, calls=%fused_computation.16 | convolution fusion | flops 4032430080 | bytes 16252928 | tf_op jit(solution)/shard_map/dot_general | solution.py:26
  232.5 6.7 %convolution_convert_fusion = bf16[1280,1280]{1,0:T(8,128)(2,1)} fusion(bf16[1280,1536]{1,0:T(8,128)(2,1)S(1)} %copy-done.7, bf16[1280,768]{1,0:T(8,128)(2,1)S(1)} %get-tuple-element.43, bf16[1280,768]{1,0:T(8,128)(2,1)S(1)} %get-tuple-element.42), kind=kOutput, calls=%fused_computation.1 | convolution fusion | flops 5042667520 | bytes 11141120 | tf_op jit(solution)/shard_map/dot_general | solution.py:26
  239.2 4.8 %all-to-all-start.3 = ((bf16[16,80,1280]{2,1,0:T(8,128)(2,1)}), bf16[16,80,1280]{2,1,0:T(8,128)(2,1)}, u32[]{:S(2)}, u32[]{:S(2)}) async-start(bf16[16,80,1280]{2,1,0:T(8,128)(2,1)} %bitcast.115), calls=%async_computation.3 | async-start | bytes 6553600 | tf_op jit(solution)/shard_map/all_to_all | solution.py:361
  244.1 6.7 %convolution_convert_fusion.3 = bf16[1280,768]{1,0:T(8,128)(2,1)} fusion(bf16[768,1536]{1,0:T(8,128)(2,1)S(1)} %copy-done.13, bf16[1280,768]{1,0:T(8,128)(2,1)} %copy-done.24, bf16[1280,768]{1,0:T(8,128)(2,1)} %copy-done.23), kind=kOutput, calls=%fused_computation.20 | convolution fusion | flops 3028746240 | bytes 8257536 | tf_op jit(solution)/shard_map/dot_general | solution.py:26
  250.8 37.6 %all-to-all-done.3 = bf16[16,80,1280]{2,1,0:T(8,128)(2,1)} async-done(((bf16[16,80,1280]{2,1,0:T(8,128)(2,1)}), bf16[16,80,1280]{2,1,0:T(8,128)(2,1)}, u32[]{:S(2)}, u32[]{:S(2)}) %all-to-all-start.3) | async-done | bytes 3276832 | tf_op jit(solution)/shard_map/all_to_all | solution.py:361
  288.4 4.7 %all-to-all-start.4 = ((bf16[16,80,768]{2,1,0:T(8,128)(2,1)}), bf16[16,80,768]{2,1,0:T(8,128)(2,1)}, u32[]{:S(2)}, u32[]{:S(2)}) async-start(bf16[16,80,768]{2,1,0:T(8,128)(2,1)} %bitcast.120), calls=%async_computation.4 | async-start | bytes 3932160 | tf_op jit(solution)/shard_map/all_to_all | solution.py:361
  293.0 5.8 %convolution_convert_fusion.2 = bf16[1024,1280]{1,0:T(8,128)(2,1)S(1)} fusion(bf16[1280,1024]{1,0:T(8,128)(2,1)S(1)} %copy-done.10, bf16[1280,1280]{1,0:T(8,128)(2,1)} %bitcast.27), kind=kOutput, calls=%fused_computation.19 | convolution fusion | flops 3356753920 | bytes 8519680 | tf_op jit(solution)/shard_map/dot_general | solution.py:32
  301.6 18.6 %all-to-all-done.4 = bf16[16,80,768]{2,1,0:T(8,128)(2,1)} async-done(((bf16[16,80,768]{2,1,0:T(8,128)(2,1)}), bf16[16,80,768]{2,1,0:T(8,128)(2,1)}, u32[]{:S(2)}, u32[]{:S(2)}) %all-to-all-start.4) | async-done | bytes 1966112 | tf_op jit(solution)/shard_map/all_to_all | solution.py:361
  320.2 4.0 convolution_convert_fusion.4
  332.2 3.7 all-to-all-start.5
  339.7 7.2 %collective-permute-done.1 = bf16[128,1280]{1,0:T(8,128)(2,1)S(1)} collective-permute-done((bf16[128,1280]{1,0:T(8,128)(2,1)}, bf16[128,1280]{1,0:T(8,128)(2,1)S(1)}, u32[]{:S(2)}, u32[]{:S(2)}) %collective-permute-start.1) | collective-permute-done | bytes 327712 | tf_op jit(solution)/shard_map/ppermute | solution.py:234
  349.3 5.6 %collective-permute-done.5 = bf16[128,768]{1,0:T(8,128)(2,1)S(1)} collective-permute-done((bf16[128,768]{1,0:T(8,128)(2,1)S(1)}, bf16[128,768]{1,0:T(8,128)(2,1)S(1)}, u32[]{:S(2)}, u32[]{:S(2)}) %collective-permute-start.5) | collective-permute-done | bytes 196640 | tf_op jit(solution)/shard_map/ppermute | solution.py:234
  357.2 9.6 %project.1 = bf16[16,272,128]{2,1,0:T(8,128)(2,1)} custom-call(bf16[128,2048]{1,0:T(8,128)(2,1)} %fusion.18.resid_ref, bf16[8,16,2,128,256]{4,3,2,1,0:T(8,128)(2,1)} %bitcast.110, bf16[128,4096]{1,0:T(8,128)(2,1)} %output_ref.1), custom_call_target="tpu_custom_call" | custom-call | flops 2147483648 | bytes 19922944 | tf_op jit(solution)/shard_map/project/pallas_call | solution.py:66
  368.0 20.8 %all_to_all.40.grad_ref = bf16[16,272,128]{2,1,0:T(8,128)(2,1)S(1)} all-to-all(bf16[16,272,128]{2,1,0:T(8,128)(2,1)} %project.1), channel_id=1, replica_groups=mesh['grp'=8,'inner'=16] {'inner'}, dimensions={0} | all-to-all | bytes 2228224 | tf_op jit(solution)/shard_map/all_to_all | solution.py:381
  388.9 17.3 %attention.1 = bf16[2048,512]{1,0:T(8,128)(2,1)S(1)} custom-call(bf16[2048,512]{1,0:T(8,128)(2,1)S(1)} %bitcast.108, bf16[16,272,128]{2,1,0:T(8,128)(2,1)S(1)} %all_to_all.40.grad_ref, f32[2,2048]{1,0:T(2,128)S(1)} %copy-done.2), custom_call_target="tpu_custom_call" | custom-call | flops 5368709120 | bytes 5242880 | tf_op jit(solution)/shard_map/attention/pallas_call | solution.py:156
  406.2 31.6 %all_to_all.41.packed_ref = bf16[16,128,512]{2,1,0:T(8,128)(2,1)} all-to-all(bf16[16,128,512]{2,1,0:T(8,128)(2,1)S(1)} %bitcast.109), channel_id=1, replica_groups=mesh['grp'=8,'inner'=16] {'inner'}, dimensions={0} | all-to-all | bytes 4194304 | tf_op jit(solution)/shard_map/all_to_all | solution.py:384
  437.8 3.6 assemble.1
  (112 shorter events, 38.6 us)
Async XLA Ops:
  7.2 217.3 %copy-start = (bf16[1,768,2048]{2,1,0:T(8,128)(2,1)S(1)}, bf16[1,768,2048]{2,1,0:T(8,128)(2,1)}, u32[]{:S(2)}) copy-start(bf16[1,768,2048]{2,1,0:T(8,128)(2,1)} %param.21) | copy-start | bytes 9437188
  7.2 39.0 %all-gather.8.cloned.1.call-start = ((), (), s32[]{:S(2)}) async-start(), calls=%async_computation.9 | async-start | bytes 4718592 | tf_op jit(solution)/shard_map/all_gather | solution.py:273
  11.2 68.7 %all-gather.6.cloned.1.call-start = ((), (), s32[]{:S(2)}) async-start(), calls=%async_computation.8 | async-start | bytes 4718592 | tf_op jit(solution)/shard_map/all_gather | solution.py:274
  12.9 9.8 %copy-start.19 = (s32[128,8]{0,1:T(8,128)S(1)}, s32[128,8]{0,1:T(8,128)}, u32[]{:S(2)}) copy-start(s32[128,8]{0,1:T(8,128)} %param.17) | copy-start | bytes 12292
  12.9 9.8 %copy-start.20 = (f32[128,8]{0,1:T(8,128)S(1)}, f32[128,8]{0,1:T(8,128)}, u32[]{:S(2)}) copy-start(f32[128,8]{0,1:T(8,128)} %param.18) | copy-start | bytes 12292
  14.4 41.5 %all-to-all-start.1 = ((bf16[16,256,256]{2,1,0:T(8,128)(2,1)}), bf16[16,256,256]{2,1,0:T(8,128)(2,1)}, u32[]{:S(2)}, u32[]{:S(2)}) async-start(bf16[16,256,256]{2,1,0:T(8,128)(2,1)} %broadcast_in_dim.61), calls=%async_computation.1 | async-start | bytes 4194304 | tf_op jit(solution)/shard_map/all_to_all | solution.py:281
  22.5 202.0 %all-gather.10.cloned.1.call-start = ((), (), s32[]{:S(2)}) async-start(), calls=%async_computation.10 | async-start | bytes 18874368 | tf_op jit(solution)/shard_map/all_gather | solution.py:309
  56.0 7.9 %copy-start.16 = (bf16[128,512]{1,0:T(8,128)(2,1)S(1)}, bf16[128,512]{1,0:T(8,128)(2,1)}, u32[]{:S(2)}) copy-start(bf16[128,512]{1,0:T(8,128)(2,1)} %param.24) | copy-start | bytes 393220
  56.0 8.0 %copy-start.17 = (bf16[128,512]{1,0:T(8,128)(2,1)S(1)}, bf16[128,512]{1,0:T(8,128)(2,1)}, u32[]{:S(2)}) copy-start(bf16[128,512]{1,0:T(8,128)(2,1)} %param.25) | copy-start | bytes 393220
  56.0 86.0 %all-to-all-start.2 = ((bf16[16,80,2048]{2,1,0:T(8,128)(2,1)}), bf16[16,80,2048]{2,1,0:T(8,128)(2,1)}, u32[]{:S(2)}, u32[]{:S(2)}) async-start(bf16[16,80,2048]{2,1,0:T(8,128)(2,1)} %bitcast.111), calls=%async_computation.2 | async-start | bytes 10485760 | tf_op jit(solution)/shard_map/all_to_all | solution.py:304
  142.0 82.5 %all-to-all-start = ((bf16[16,80,2048]{2,1,0:T(8,128)(2,1)}), bf16[16,80,2048]{2,1,0:T(8,128)(2,1)}, u32[]{:S(2)}, u32[]{:S(2)}) async-start(bf16[16,80,2048]{2,1,0:T(8,128)(2,1)} %bitcast.112), calls=%async_computation | async-start | bytes 10485760 | tf_op jit(solution)/shard_map/all_to_all | solution.py:304
  224.5 8.1 %copy-start.7 = (bf16[1280,1536]{1,0:T(8,128)(2,1)S(1)}, bf16[1280,1536]{1,0:T(8,128)(2,1)}, u32[]{:S(2)}) copy-start(bf16[1280,1536]{1,0:T(8,128)(2,1)} %pad_maximum_fusion) | copy-start | bytes 11796484
  232.5 6.7 %copy-start.23 = (bf16[1280,768]{1,0:T(8,128)(2,1)}, bf16[1280,768]{1,0:T(8,128)(2,1)S(1)}, u32[]{:S(2)}) copy-start(bf16[1280,768]{1,0:T(8,128)(2,1)S(1)} %get-tuple-element.42) | copy-start | bytes 5898244
  232.5 6.7 %copy-start.24 = (bf16[1280,768]{1,0:T(8,128)(2,1)}, bf16[1280,768]{1,0:T(8,128)(2,1)S(1)}, u32[]{:S(2)}) copy-start(bf16[1280,768]{1,0:T(8,128)(2,1)S(1)} %get-tuple-element.43) | copy-start | bytes 5898244
  239.2 49.1 %all-to-all-start.3 = ((bf16[16,80,1280]{2,1,0:T(8,128)(2,1)}), bf16[16,80,1280]{2,1,0:T(8,128)(2,1)}, u32[]{:S(2)}, u32[]{:S(2)}) async-start(bf16[16,80,1280]{2,1,0:T(8,128)(2,1)} %bitcast.115), calls=%async_computation.3 | async-start | bytes 6553600 | tf_op jit(solution)/shard_map/all_to_all | solution.py:361
  250.8 42.3 %copy-start.10 = (bf16[1280,1024]{1,0:T(8,128)(2,1)S(1)}, bf16[1280,1024]{1,0:T(8,128)(2,1)}, u32[]{:S(2)}) copy-start(bf16[1280,1024]{1,0:T(8,128)(2,1)} %select_convert_fusion) | copy-start | bytes 7864324
  288.4 31.8 %all-to-all-start.4 = ((bf16[16,80,768]{2,1,0:T(8,128)(2,1)}), bf16[16,80,768]{2,1,0:T(8,128)(2,1)}, u32[]{:S(2)}, u32[]{:S(2)}) async-start(bf16[16,80,768]{2,1,0:T(8,128)(2,1)} %bitcast.120), calls=%async_computation.4 | async-start | bytes 3932160 | tf_op jit(solution)/shard_map/all_to_all | solution.py:361
  301.6 23.6 %collective-permute-start = (bf16[4,128,1280]{2,1,0:T(8,128)(2,1)}, bf16[4,128,1280]{2,1,0:T(8,128)(2,1)}, u32[]{:S(2)}, u32[]{:S(2)}) collective-permute-start(bf16[4,128,1280]{2,1,0:T(8,128)(2,1)} %dynamic-slice_bitcast_fusion), channel_id=1, source_target_pairs={{0,16},{16,0},{32,48},{48,32},{64,80},{80,64},{96,112},{112,96},{1... | collective-permute-start | bytes 3932168 | tf_op jit(solution)/shard_map/ppermute | solution.py:228
  325.2 10.8 %collective-permute-start.4 = (bf16[4,128,768]{2,1,0:T(8,128)(2,1)}, bf16[4,128,768]{2,1,0:T(8,128)(2,1)}, u32[]{:S(2)}, u32[]{:S(2)}) collective-permute-start(bf16[4,128,768]{2,1,0:T(8,128)(2,1)} %dynamic-slice_bitcast_fusion.1), channel_id=1, source_target_pairs={{0,16},{16,0},{32,48},{48,32},{64,80},{80,64},{96,112},{112,96},{1... | collective-permute-start | bytes 2359304 | tf_op jit(solution)/shard_map/ppermute | solution.py:228
  327.9 19.0 %collective-permute-start.1 = (bf16[128,1280]{1,0:T(8,128)(2,1)}, bf16[128,1280]{1,0:T(8,128)(2,1)S(1)}, u32[]{:S(2)}, u32[]{:S(2)}) collective-permute-start(bf16[128,1280]{1,0:T(8,128)(2,1)} %get-tuple-element.44), channel_id=1, source_target_pairs={{0,32},{16,48},{32,64},{48,80},{64,96},{80,112},{96,0},{112,16},{1... | collective-permute-start | bytes 983048 | tf_op jit(solution)/shard_map/ppermute | solution.py:234
  328.4 18.6 %collective-permute-start.2 = (bf16[128,1280]{1,0:T(8,128)(2,1)}, bf16[128,1280]{1,0:T(8,128)(2,1)}, u32[]{:S(2)}, u32[]{:S(2)}) collective-permute-start(bf16[128,1280]{1,0:T(8,128)(2,1)} %get-tuple-element.46), channel_id=1, source_target_pairs={{0,64},{16,80},{32,96},{48,112},{64,0},{80,16},{96,32},{112,48},{1... | collective-permute-start | bytes 983048 | tf_op jit(solution)/shard_map/ppermute | solution.py:234
  330.2 17.7 %collective-permute-start.3 = (bf16[128,1280]{1,0:T(8,128)(2,1)S(1)}, bf16[128,1280]{1,0:T(8,128)(2,1)}, u32[]{:S(2)}, u32[]{:S(2)}) collective-permute-start(bf16[128,1280]{1,0:T(8,128)(2,1)S(1)} %get-tuple-element.45), channel_id=1, source_target_pairs={{0,96},{16,112},{32,0},{48,16},{64,32},{80,48},{96,64},{112,80},{1... | collective-permute-start | bytes 983048 | tf_op jit(solution)/shard_map/ppermute | solution.py:234
  332.2 35.8 %all-to-all-start.5 = ((bf16[16,128,512]{2,1,0:T(8,128)(2,1)}), bf16[16,128,512]{2,1,0:T(8,128)(2,1)S(1)}, u32[]{:S(2)}, u32[]{:S(2)}) async-start(bf16[16,128,512]{2,1,0:T(8,128)(2,1)} %pad_maximum_fusion.5), calls=%async_computation.5 | async-start | bytes 4194304 | tf_op jit(solution)/shard_map/all_to_all | solution.py:366
  336.0 19.7 %copy-start.3 = (bf16[128,2048]{1,0:T(8,128)(2,1)S(1)}, bf16[128,2048]{1,0:T(8,128)(2,1)}, u32[]{:S(2)}) copy-start(bf16[128,2048]{1,0:T(8,128)(2,1)} %param.15) | copy-start | bytes 1572868
  336.0 19.7 %copy-start.18 = (f32[2048]{0:T(1024)S(1)}, f32[2048]{0:T(1024)}, u32[]{:S(2)}) copy-start(f32[2048]{0:T(1024)} %param.16) | copy-start | bytes 24580
  337.6 18.3 %copy-start.14 = (bf16[128,2048]{1,0:T(8,128)(2,1)S(1)}, bf16[128,2048]{1,0:T(8,128)(2,1)}, u32[]{:S(2)}) copy-start(bf16[128,2048]{1,0:T(8,128)(2,1)} %param.14) | copy-start | bytes 1572868
  337.6 18.3 %copy-start.22 = (f32[128]{0:T(128)S(1)}, f32[128]{0:T(128)}, u32[]{:S(2)}) copy-start(f32[128]{0:T(128)} %copy-done.21) | copy-start | bytes 1540
  337.7 17.2 %collective-permute-start.5 = (bf16[128,768]{1,0:T(8,128)(2,1)S(1)}, bf16[128,768]{1,0:T(8,128)(2,1)S(1)}, u32[]{:S(2)}, u32[]{:S(2)}) collective-permute-start(bf16[128,768]{1,0:T(8,128)(2,1)S(1)} %get-tuple-element.47), channel_id=1, source_target_pairs={{0,32},{16,48},{32,64},{48,80},{64,96},{80,112},{96,0},{112,16},{1... | collective-permute-start | bytes 589832 | tf_op jit(solution)/shard_map/ppermute | solution.py:234
  337.8 17.1 %collective-permute-start.6 = (bf16[128,768]{1,0:T(8,128)(2,1)S(1)}, bf16[128,768]{1,0:T(8,128)(2,1)S(1)}, u32[]{:S(2)}, u32[]{:S(2)}) collective-permute-start(bf16[128,768]{1,0:T(8,128)(2,1)S(1)} %get-tuple-element.49), channel_id=1, source_target_pairs={{0,64},{16,80},{32,96},{48,112},{64,0},{80,16},{96,32},{112,48},{1... | collective-permute-start | bytes 589832 | tf_op jit(solution)/shard_map/ppermute | solution.py:234
  346.9 8.6 %collective-permute-start.7 = (bf16[128,768]{1,0:T(8,128)(2,1)S(1)}, bf16[128,768]{1,0:T(8,128)(2,1)S(1)}, u32[]{:S(2)}, u32[]{:S(2)}) collective-permute-start(bf16[128,768]{1,0:T(8,128)(2,1)S(1)} %get-tuple-element.48), channel_id=1, source_target_pairs={{0,96},{16,112},{32,0},{48,16},{64,32},{80,48},{96,64},{112,80},{1... | collective-permute-start | bytes 589832 | tf_op jit(solution)/shard_map/ppermute | solution.py:234
  357.2 31.7 %copy-start.2 = (f32[2,2048]{1,0:T(2,128)S(1)}, f32[2,2048]{1,0:T(2,128)}, u32[]{:S(2)}) copy-start(f32[2,2048]{1,0:T(2,128)} %lse_ref.1) | copy-start | bytes 49156
  406.2 35.3 %copy-start.1 = (bf16[1,768,2048]{2,1,0:T(8,128)(2,1)S(1)}, bf16[1,768,2048]{2,1,0:T(8,128)(2,1)}, u32[]{:S(2)}) copy-start(bf16[1,768,2048]{2,1,0:T(8,128)(2,1)} %param.21) | copy-start | bytes 9437188
  (10 other events, 34.7 us)
Sparse Core Ops, SparseCore 0:
  11.3 34.8 all-gather.7
  47.9 31.9 all-gather.5
  81.6 84.8 all-gather.9

commit v6 on v5

--- a/solution.py
+++ b/solution.py
@@ -305,12 +305,17 @@
 
     slot_gate = jnp.sum(jnp.where(chosen, gate, 0.0), axis=2)
     input_rows = dot_nn(picks, normed_all).astype(bf16)
-    input_rows, w_piece = lax.optimization_barrier((input_rows, w_piece))
+    input_rows, w_piece, slot_gate = lax.optimization_barrier((input_rows, w_piece, slot_gate))
     w_whole = lax.all_gather(w_piece, "grp", axis=0, tiled=False)
     w_whole = w_whole.reshape(groups, inner, head_width // HEAD_SIZE, HEAD_SIZE, piece)
     inputs = to_experts(input_rows.reshape(inner, slots, width))
+    marker = jnp.minimum(jnp.abs(inputs[:8, :128].astype(f32)), 0.0)
+    slot_gate = slot_gate + jnp.sum(marker)
     slot_gate = slot_gate.reshape(inner * slots, 1)
     upstream_rows = (dot_nn(picks, upstream_all) * slot_gate).astype(bf16)
+    upstream_rows, queries, keys, values, w_gate, w_up = lax.optimization_barrier(
+        (upstream_rows, queries, keys, values, w_gate, w_up)
+    )
     upstream_rows = to_experts(upstream_rows.reshape(inner, slots, width))
 
     kv = jnp.stack(

time: 449 us -> 448 us (level)
  blocking collectives: 66 us -> 135 us
  waiting for transfers between devices: 196 us -> 135 us
  starting transfers between devices: 40.2 us -> 32.3 us
    all_to_all x0 -> x1, blocking collectives: none -> 69.5 us  [to_experts(): lax.all_to_all(array, 'inner', 0, 0, tiled=True)]
    all_to_all x2 -> x1, waiting for transfers between devices: 108 us -> 55.7 us  [to_experts(): lax.all_to_all(array, 'inner', 0, 0, tiled=True)]
    all_gather x1, waiting for transfers between devices: 8.26 us -> 0.02 us  [per_device(): upstream_all = lax.all_gather(grad_out, 'grp', axis=0, tiled=True)]
    all_to_all x2 -> x1, starting transfers between devices: 12.5 us -> 4.76 us  [to_experts(): lax.all_to_all(array, 'inner', 0, 0, tiled=True)]
  transfers between devices with their start and end apart: 17 -> 16, of which waited for: 11 -> 9; matrix products, arithmetic and copies ran while one was open for 18% -> 17% of each run, Pallas kernels for 2% -> 2%
where the time goes in v6:
time: 448 us
  waiting for transfers between devices  135 us (30%)
  blocking collectives  135 us (30%)
  matrix products  59.4 us (13%)
  starting transfers between devices  32.3 us (7%)
  Pallas kernels  30.5 us (7%)
  other arithmetic  24.6 us (5%)
  local copies, waits for them, and re-layouts  16.3 us (4%)
  between operations  14.3 us (3%)
    all_to_all x1, blocking collectives, to_experts(): lax.all_to_all(array, 'inner', 0, 0, tiled=True)  69.5 us
    all_to_all x2, waiting for transfers between devices, per_device(): arrived = lax.all_to_all(grads[part], 'inner', 0, 0, tiled=True)  56.4 us
    all_to_all x1, waiting for transfers between devices, to_experts(): lax.all_to_all(array, 'inner', 0, 0, tiled=True)  55.7 us
    all_to_all x1, blocking collectives, per_device(): packed_grads = lax.all_to_all(packed_grads, 'inner', 0, 0, tiled=True)  31.6 us
    dot_general x4, matrix products, dot_nn(): lax.dot_general(left, right, (((1,), (0,)), ((), ())), preferred_element_...  28.1 us
    dot_general x3, matrix products, contract_last(): lax.dot_general(left, right, (((1,), (1,)), ((), ())), preferred_element_...  21.4 us
    all_to_all x1, blocking collectives, per_device(): head_grad = lax.all_to_all(head_grad, 'inner', 0, 0, tiled=True)  20.8 us
    pallas_call x1, Pallas kernels, attention(): pl.pallas_call(attention_kernel, grid=(length // block,), in_specs=[whole...  17.3 us
  transfers between devices with their start and end apart: 16, of which 9 were waited for; matrix products, arithmetic and copies ran while one was open for 17% of the time, Pallas kernels for 2%

profile of v6, /device:TPU:0, one launch (start us, length us, event | category | flops | bytes accessed | tf_op | source)
XLA Modules:
  0.0 447.6 jit_solution(12787950463152036634)
XLA Ops:
  8.6 2.0 fusion.14
  14.0 8.0 %all-to-all-start = ((bf16[16,256,256]{2,1,0:T(8,128)(2,1)}), bf16[16,256,256]{2,1,0:T(8,128)(2,1)}, u32[]{:S(2)}, u32[]{:S(2)}) async-start(bf16[16,256,256]{2,1,0:T(8,128)(2,1)} %broadcast_in_dim.56), calls=%async_computation | async-start | bytes 4194304 | tf_op jit(solution)/shard_map/all_to_all | solution.py:281
  22.2 13.5 %all-gather = f32[128,128]{1,0:T(8,128)S(1)} all-gather(f32[16,128]{1,0:T(8,128)S(1)} %pad_maximum_fusion.7), channel_id=2, replica_groups=mesh['grp'=8,'inner'=16] {'grp'}, dimensions={0}, use_global_device_ids=true | all-gather | bytes 73728 | tf_op jit(solution)/shard_map/all_gather | solution.py:276
  39.1 6.6 %all-gather.8.cloned.1.call-done = bf16[1024,2048]{1,0:T(8,128)(2,1)} async-done(((bf16[128,2048]{1,0:T(8,128)(2,1)}), bf16[1024,2048]{1,0:T(8,128)(2,1)}) %all-gather.8.cloned.1.call-update) | async-done | bytes 4194320 | tf_op jit(solution)/shard_map/all_gather | solution.py:273
  45.6 9.8 %convolution_convert_fusion.1 = bf16[1280,2048]{1,0:T(8,128)(2,1)} fusion(bf16[1280,1024]{1,0:T(8,128)(2,1)} %select_convert_fusion, bf16[1024,2048]{1,0:T(8,128)(2,1)} %all-gather.8.cloned.1.call-done), kind=kOutput, calls=%fused_computation.2 | convolution fusion | flops 5371330560 | bytes 12058624 | tf_op jit(solution)/shard_map/dot_general | solution.py:20
  55.5 69.5 %all_to_all.40 = bf16[16,80,2048]{2,1,0:T(8,128)(2,1)S(1)} all-to-all(bf16[16,80,2048]{2,1,0:T(8,128)(2,1)} %bitcast.116), channel_id=1, replica_groups=mesh['grp'=8,'inner'=16] {'inner'}, dimensions={0} | all-to-all | bytes 10485760 | tf_op jit(solution)/shard_map/all_to_all | solution.py:304
  124.9 2.2 copy-done.4
  128.6 9.9 %multiply_convert_fusion = bf16[1280,2048]{1,0:T(8,128)(2,1)} fusion(bf16[1280,1024]{1,0:T(8,128)(2,1)} %select_convert_fusion, bf16[1024,2048]{1,0:T(8,128)(2,1)} %all-gather.6.cloned.1.call-done, f32[1280]{0:T(1024)S(1)} %mul.108), kind=kOutput, calls=%fused_computation | convolution fusion | flops 5373952000 | bytes 12063744 | tf_op jit(solution)/shard_map/dot_general | solution.py:20
  140.6 2.3 copy.67
  142.9 4.8 %all-to-all-start.2 = ((bf16[16,80,2048]{2,1,0:T(8,128)(2,1)}), bf16[16,80,2048]{2,1,0:T(8,128)(2,1)}, u32[]{:S(2)}, u32[]{:S(2)}) async-start(bf16[16,80,2048]{2,1,0:T(8,128)(2,1)} %bitcast.115), calls=%async_computation.2 | async-start | bytes 10485760 | tf_op jit(solution)/shard_map/all_to_all | solution.py:304
  147.8 3.0 pad_maximum_fusion.5
  153.8 2.3 pad_maximum_fusion
  157.6 8.3 %fusion = f32[1280,1536]{1,0:T(8,128)S(1)} fusion(bf16[1280,2048]{1,0:T(8,128)(2,1)S(1)} %bitcast.114, bf16[2048,768]{1,0:T(8,128)(2,1)S(1)} %bitcast.120, bf16[2048,768]{1,0:T(8,128)(2,1)S(1)} %bitcast.121), kind=kOutput, calls=%fused_computation.3 | convolution fusion | flops 8065646592 | bytes 19398656 | tf_op jit(solution)/shard_map/dot_general | solution.py:20
  165.9 2.9 multiply_convert_fusion.3
  168.8 55.7 %all-to-all-done.2 = bf16[16,80,2048]{2,1,0:T(8,128)(2,1)} async-done(((bf16[16,80,2048]{2,1,0:T(8,128)(2,1)}), bf16[16,80,2048]{2,1,0:T(8,128)(2,1)}, u32[]{:S(2)}, u32[]{:S(2)}) %all-to-all-start.2) | async-done | bytes 5242912 | tf_op jit(solution)/shard_map/all_to_all | solution.py:304
  224.5 8.0 %multiply_convert_fusion.2 = (bf16[1280,768]{1,0:T(8,128)(2,1)S(1)}, bf16[1280,768]{1,0:T(8,128)(2,1)S(1)}) fusion(bf16[1280,768]{1,0:T(8,128)(2,1)} %get-tuple-element.39, bf16[1280,768]{1,0:T(8,128)(2,1)} %get-tuple-element.40, bf16[1280,2048]{1,0:T(8,128)(2,1)} %bitcast.10, bf16[1,768,2048]{2,1,0:T(8,128)(2,1)S(1)} %copy-done), kind=kOutput, calls=%fused_computation.16 | convolution fusion | flops 4032430080 | bytes 16252928 | tf_op jit(solution)/shard_map/dot_general | solution.py:26
  232.5 6.7 %convolution_convert_fusion = bf16[1280,1280]{1,0:T(8,128)(2,1)} fusion(bf16[1280,1536]{1,0:T(8,128)(2,1)S(1)} %copy-done.6, bf16[1280,768]{1,0:T(8,128)(2,1)S(1)} %get-tuple-element.57, bf16[1280,768]{1,0:T(8,128)(2,1)S(1)} %get-tuple-element.56), kind=kOutput, calls=%fused_computation.1 | convolution fusion | flops 5042667520 | bytes 11141120 | tf_op jit(solution)/shard_map/dot_general | solution.py:26
  239.3 4.9 %all-to-all-start.3 = ((bf16[16,80,1280]{2,1,0:T(8,128)(2,1)}), bf16[16,80,1280]{2,1,0:T(8,128)(2,1)}, u32[]{:S(2)}, u32[]{:S(2)}) async-start(bf16[16,80,1280]{2,1,0:T(8,128)(2,1)} %bitcast.119), calls=%async_computation.3 | async-start | bytes 6553600 | tf_op jit(solution)/shard_map/all_to_all | solution.py:366
  244.2 6.7 %convolution_convert_fusion.3 = bf16[1280,768]{1,0:T(8,128)(2,1)} fusion(bf16[768,1536]{1,0:T(8,128)(2,1)S(1)} %copy-done.12, bf16[1280,768]{1,0:T(8,128)(2,1)} %copy-done.21, bf16[1280,768]{1,0:T(8,128)(2,1)} %copy-done.20), kind=kOutput, calls=%fused_computation.20 | convolution fusion | flops 3028746240 | bytes 8257536 | tf_op jit(solution)/shard_map/dot_general | solution.py:26
  250.9 37.4 %all-to-all-done.3 = bf16[16,80,1280]{2,1,0:T(8,128)(2,1)} async-done(((bf16[16,80,1280]{2,1,0:T(8,128)(2,1)}), bf16[16,80,1280]{2,1,0:T(8,128)(2,1)}, u32[]{:S(2)}, u32[]{:S(2)}) %all-to-all-start.3) | async-done | bytes 3276832 | tf_op jit(solution)/shard_map/all_to_all | solution.py:366
  288.3 4.4 all-to-all-start.4
  292.8 5.8 %convolution_convert_fusion.2 = bf16[1024,1280]{1,0:T(8,128)(2,1)S(1)} fusion(bf16[1280,1024]{1,0:T(8,128)(2,1)S(1)} %copy-done.9, bf16[1280,1280]{1,0:T(8,128)(2,1)} %bitcast.27), kind=kOutput, calls=%fused_computation.19 | convolution fusion | flops 3356753920 | bytes 8519680 | tf_op jit(solution)/shard_map/dot_general | solution.py:32
  301.4 19.0 %all-to-all-done.4 = bf16[16,80,768]{2,1,0:T(8,128)(2,1)} async-done(((bf16[16,80,768]{2,1,0:T(8,128)(2,1)}), bf16[16,80,768]{2,1,0:T(8,128)(2,1)}, u32[]{:S(2)}, u32[]{:S(2)}) %all-to-all-start.4) | async-done | bytes 1966112 | tf_op jit(solution)/shard_map/all_to_all | solution.py:366
  320.3 4.0 convolution_convert_fusion.4
  331.9 3.7 all-to-all-start.5
  339.8 7.3 %collective-permute-done.1 = bf16[128,1280]{1,0:T(8,128)(2,1)S(1)} collective-permute-done((bf16[128,1280]{1,0:T(8,128)(2,1)}, bf16[128,1280]{1,0:T(8,128)(2,1)S(1)}, u32[]{:S(2)}, u32[]{:S(2)}) %collective-permute-start.1) | collective-permute-done | bytes 327712 | tf_op jit(solution)/shard_map/ppermute | solution.py:234
  349.4 5.6 %collective-permute-done.5 = bf16[128,768]{1,0:T(8,128)(2,1)S(1)} collective-permute-done((bf16[128,768]{1,0:T(8,128)(2,1)S(1)}, bf16[128,768]{1,0:T(8,128)(2,1)S(1)}, u32[]{:S(2)}, u32[]{:S(2)}) %collective-permute-start.5) | collective-permute-done | bytes 196640 | tf_op jit(solution)/shard_map/ppermute | solution.py:234
  357.3 9.6 %project.1 = bf16[16,272,128]{2,1,0:T(8,128)(2,1)} custom-call(bf16[128,2048]{1,0:T(8,128)(2,1)} %fusion.18.resid_ref, bf16[8,16,2,128,256]{4,3,2,1,0:T(8,128)(2,1)} %bitcast.110, bf16[128,4096]{1,0:T(8,128)(2,1)} %output_ref.1), custom_call_target="tpu_custom_call" | custom-call | flops 2147483648 | bytes 19922944 | tf_op jit(solution)/shard_map/project/pallas_call | solution.py:66
  367.7 20.8 %all_to_all.41.grad_ref = bf16[16,272,128]{2,1,0:T(8,128)(2,1)S(1)} all-to-all(bf16[16,272,128]{2,1,0:T(8,128)(2,1)} %project.1), channel_id=1, replica_groups=mesh['grp'=8,'inner'=16] {'inner'}, dimensions={0} | all-to-all | bytes 2228224 | tf_op jit(solution)/shard_map/all_to_all | solution.py:386
  388.5 17.3 %attention.1 = bf16[2048,512]{1,0:T(8,128)(2,1)S(1)} custom-call(bf16[2048,512]{1,0:T(8,128)(2,1)S(1)} %bitcast.108, bf16[16,272,128]{2,1,0:T(8,128)(2,1)S(1)} %all_to_all.41.grad_ref, f32[2,2048]{1,0:T(2,128)S(1)} %copy-done.2), custom_call_target="tpu_custom_call" | custom-call | flops 5368709120 | bytes 5242880 | tf_op jit(solution)/shard_map/attention/pallas_call | solution.py:156
  405.8 31.6 %all_to_all.42.packed_ref = bf16[16,128,512]{2,1,0:T(8,128)(2,1)} all-to-all(bf16[16,128,512]{2,1,0:T(8,128)(2,1)S(1)} %bitcast.109), channel_id=1, replica_groups=mesh['grp'=8,'inner'=16] {'inner'}, dimensions={0} | all-to-all | bytes 4194304 | tf_op jit(solution)/shard_map/all_to_all | solution.py:389
  437.4 3.6 assemble.1
  (114 shorter events, 35.9 us)
Async XLA Ops:
  7.2 217.3 %copy-start = (bf16[1,768,2048]{2,1,0:T(8,128)(2,1)S(1)}, bf16[1,768,2048]{2,1,0:T(8,128)(2,1)}, u32[]{:S(2)}) copy-start(bf16[1,768,2048]{2,1,0:T(8,128)(2,1)} %param.21) | copy-start | bytes 9437188
  7.2 38.5 %all-gather.8.cloned.1.call-start = ((), (), s32[]{:S(2)}) async-start(), calls=%async_computation.9 | async-start | bytes 4718592 | tf_op jit(solution)/shard_map/all_gather | solution.py:273
  10.7 117.9 %all-gather.6.cloned.1.call-start = ((), (), s32[]{:S(2)}) async-start(), calls=%async_computation.8 | async-start | bytes 4718592 | tf_op jit(solution)/shard_map/all_gather | solution.py:274
  12.4 9.8 %copy-start.18 = (s32[128,8]{0,1:T(8,128)S(1)}, s32[128,8]{0,1:T(8,128)}, u32[]{:S(2)}) copy-start(s32[128,8]{0,1:T(8,128)} %param.17) | copy-start | bytes 12292
  12.4 9.8 %copy-start.19 = (f32[128,8]{0,1:T(8,128)S(1)}, f32[128,8]{0,1:T(8,128)}, u32[]{:S(2)}) copy-start(f32[128,8]{0,1:T(8,128)} %param.18) | copy-start | bytes 12292
  14.0 41.5 %all-to-all-start = ((bf16[16,256,256]{2,1,0:T(8,128)(2,1)}), bf16[16,256,256]{2,1,0:T(8,128)(2,1)}, u32[]{:S(2)}, u32[]{:S(2)}) async-start(bf16[16,256,256]{2,1,0:T(8,128)(2,1)} %broadcast_in_dim.56), calls=%async_computation | async-start | bytes 4194304 | tf_op jit(solution)/shard_map/all_to_all | solution.py:281
  22.0 202.5 %all-gather.10.cloned.1.call-start = ((), (), s32[]{:S(2)}) async-start(), calls=%async_computation.10 | async-start | bytes 18874368 | tf_op jit(solution)/shard_map/all_gather | solution.py:309
  128.5 10.0 %copy-start.15 = (bf16[128,512]{1,0:T(8,128)(2,1)S(1)}, bf16[128,512]{1,0:T(8,128)(2,1)}, u32[]{:S(2)}) copy-start(bf16[128,512]{1,0:T(8,128)(2,1)} %param.24) | copy-start | bytes 393220
  128.5 10.1 %copy-start.16 = (bf16[128,512]{1,0:T(8,128)(2,1)S(1)}, bf16[128,512]{1,0:T(8,128)(2,1)}, u32[]{:S(2)}) copy-start(bf16[128,512]{1,0:T(8,128)(2,1)} %param.25) | copy-start | bytes 393220
  142.9 81.6 %all-to-all-start.2 = ((bf16[16,80,2048]{2,1,0:T(8,128)(2,1)}), bf16[16,80,2048]{2,1,0:T(8,128)(2,1)}, u32[]{:S(2)}, u32[]{:S(2)}) async-start(bf16[16,80,2048]{2,1,0:T(8,128)(2,1)} %bitcast.115), calls=%async_computation.2 | async-start | bytes 10485760 | tf_op jit(solution)/shard_map/all_to_all | solution.py:304
  224.5 8.1 %copy-start.6 = (bf16[1280,1536]{1,0:T(8,128)(2,1)S(1)}, bf16[1280,1536]{1,0:T(8,128)(2,1)}, u32[]{:S(2)}) copy-start(bf16[1280,1536]{1,0:T(8,128)(2,1)} %pad_maximum_fusion) | copy-start | bytes 11796484
  232.5 6.7 %copy-start.20 = (bf16[1280,768]{1,0:T(8,128)(2,1)}, bf16[1280,768]{1,0:T(8,128)(2,1)S(1)}, u32[]{:S(2)}) copy-start(bf16[1280,768]{1,0:T(8,128)(2,1)S(1)} %get-tuple-element.56) | copy-start | bytes 5898244
  232.5 6.7 %copy-start.21 = (bf16[1280,768]{1,0:T(8,128)(2,1)}, bf16[1280,768]{1,0:T(8,128)(2,1)S(1)}, u32[]{:S(2)}) copy-start(bf16[1280,768]{1,0:T(8,128)(2,1)S(1)} %get-tuple-element.57) | copy-start | bytes 5898244
  239.3 4.9 %copy-start.12 = (bf16[768,1536]{1,0:T(8,128)(2,1)S(1)}, bf16[768,1536]{1,0:T(8,128)(2,1)}, u32[]{:S(2)}) copy-start(bf16[768,1536]{1,0:T(8,128)(2,1)} %pad_maximum_fusion.4) | copy-start | bytes 7077892
  239.3 49.1 %all-to-all-start.3 = ((bf16[16,80,1280]{2,1,0:T(8,128)(2,1)}), bf16[16,80,1280]{2,1,0:T(8,128)(2,1)}, u32[]{:S(2)}, u32[]{:S(2)}) async-start(bf16[16,80,1280]{2,1,0:T(8,128)(2,1)} %bitcast.119), calls=%async_computation.3 | async-start | bytes 6553600 | tf_op jit(solution)/shard_map/all_to_all | solution.py:366
  250.9 41.9 %copy-start.9 = (bf16[1280,1024]{1,0:T(8,128)(2,1)S(1)}, bf16[1280,1024]{1,0:T(8,128)(2,1)}, u32[]{:S(2)}) copy-start(bf16[1280,1024]{1,0:T(8,128)(2,1)} %select_convert_fusion) | copy-start | bytes 7864324
  288.3 32.0 %all-to-all-start.4 = ((bf16[16,80,768]{2,1,0:T(8,128)(2,1)}), bf16[16,80,768]{2,1,0:T(8,128)(2,1)}, u32[]{:S(2)}, u32[]{:S(2)}) async-start(bf16[16,80,768]{2,1,0:T(8,128)(2,1)} %bitcast.124), calls=%async_computation.4 | async-start | bytes 3932160 | tf_op jit(solution)/shard_map/all_to_all | solution.py:366
  301.3 24.0 %collective-permute-start = (bf16[4,128,1280]{2,1,0:T(8,128)(2,1)}, bf16[4,128,1280]{2,1,0:T(8,128)(2,1)}, u32[]{:S(2)}, u32[]{:S(2)}) collective-permute-start(bf16[4,128,1280]{2,1,0:T(8,128)(2,1)} %dynamic-slice_bitcast_fusion), channel_id=1, source_target_pairs={{0,16},{16,0},{32,48},{48,32},{64,80},{80,64},{96,112},{112,96},{1... | collective-permute-start | bytes 3932168 | tf_op jit(solution)/shard_map/ppermute | solution.py:228
  320.3 5.0 %copy-start.11 = (bf16[1024,1280]{1,0:T(8,128)(2,1)S(1)}, bf16[1024,1280]{1,0:T(8,128)(2,1)}, u32[]{:S(2)}) copy-start(bf16[1024,1280]{1,0:T(8,128)(2,1)} %copy-done.10) | copy-start | bytes 7864324
  325.4 10.3 %collective-permute-start.4 = (bf16[4,128,768]{2,1,0:T(8,128)(2,1)}, bf16[4,128,768]{2,1,0:T(8,128)(2,1)}, u32[]{:S(2)}, u32[]{:S(2)}) collective-permute-start(bf16[4,128,768]{2,1,0:T(8,128)(2,1)} %dynamic-slice_bitcast_fusion.1), channel_id=1, source_target_pairs={{0,16},{16,0},{32,48},{48,32},{64,80},{80,64},{96,112},{112,96},{1... | collective-permute-start | bytes 2359304 | tf_op jit(solution)/shard_map/ppermute | solution.py:228
  328.0 19.0 %collective-permute-start.1 = (bf16[128,1280]{1,0:T(8,128)(2,1)}, bf16[128,1280]{1,0:T(8,128)(2,1)S(1)}, u32[]{:S(2)}, u32[]{:S(2)}) collective-permute-start(bf16[128,1280]{1,0:T(8,128)(2,1)} %get-tuple-element.58), channel_id=1, source_target_pairs={{0,32},{16,48},{32,64},{48,80},{64,96},{80,112},{96,0},{112,16},{1... | collective-permute-start | bytes 983048 | tf_op jit(solution)/shard_map/ppermute | solution.py:234
  328.4 18.7 %collective-permute-start.2 = (bf16[128,1280]{1,0:T(8,128)(2,1)}, bf16[128,1280]{1,0:T(8,128)(2,1)}, u32[]{:S(2)}, u32[]{:S(2)}) collective-permute-start(bf16[128,1280]{1,0:T(8,128)(2,1)} %get-tuple-element.60), channel_id=1, source_target_pairs={{0,64},{16,80},{32,96},{48,112},{64,0},{80,16},{96,32},{112,48},{1... | collective-permute-start | bytes 983048 | tf_op jit(solution)/shard_map/ppermute | solution.py:234
  330.4 17.7 %collective-permute-start.3 = (bf16[128,1280]{1,0:T(8,128)(2,1)S(1)}, bf16[128,1280]{1,0:T(8,128)(2,1)}, u32[]{:S(2)}, u32[]{:S(2)}) collective-permute-start(bf16[128,1280]{1,0:T(8,128)(2,1)S(1)} %get-tuple-element.59), channel_id=1, source_target_pairs={{0,96},{16,112},{32,0},{48,16},{64,32},{80,48},{96,64},{112,80},{1... | collective-permute-start | bytes 983048 | tf_op jit(solution)/shard_map/ppermute | solution.py:234
  331.9 35.8 %all-to-all-start.5 = ((bf16[16,128,512]{2,1,0:T(8,128)(2,1)}), bf16[16,128,512]{2,1,0:T(8,128)(2,1)S(1)}, u32[]{:S(2)}, u32[]{:S(2)}) async-start(bf16[16,128,512]{2,1,0:T(8,128)(2,1)} %pad_maximum_fusion.5), calls=%async_computation.5 | async-start | bytes 4194304 | tf_op jit(solution)/shard_map/all_to_all | solution.py:371
  335.6 20.2 %copy-start.3 = (bf16[128,2048]{1,0:T(8,128)(2,1)S(1)}, bf16[128,2048]{1,0:T(8,128)(2,1)}, u32[]{:S(2)}) copy-start(bf16[128,2048]{1,0:T(8,128)(2,1)} %param.15) | copy-start | bytes 1572868
  335.6 20.2 %copy-start.17 = (f32[2048]{0:T(1024)S(1)}, f32[2048]{0:T(1024)}, u32[]{:S(2)}) copy-start(f32[2048]{0:T(1024)} %param.16) | copy-start | bytes 24580
  337.3 18.8 %copy-start.13 = (bf16[128,2048]{1,0:T(8,128)(2,1)S(1)}, bf16[128,2048]{1,0:T(8,128)(2,1)}, u32[]{:S(2)}) copy-start(bf16[128,2048]{1,0:T(8,128)(2,1)} %param.14) | copy-start | bytes 1572868
  337.3 17.7 %collective-permute-start.5 = (bf16[128,768]{1,0:T(8,128)(2,1)S(1)}, bf16[128,768]{1,0:T(8,128)(2,1)S(1)}, u32[]{:S(2)}, u32[]{:S(2)}) collective-permute-start(bf16[128,768]{1,0:T(8,128)(2,1)S(1)} %get-tuple-element.61), channel_id=1, source_target_pairs={{0,32},{16,48},{32,64},{48,80},{64,96},{80,112},{96,0},{112,16},{1... | collective-permute-start | bytes 589832 | tf_op jit(solution)/shard_map/ppermute | solution.py:234
  337.9 17.1 %collective-permute-start.6 = (bf16[128,768]{1,0:T(8,128)(2,1)S(1)}, bf16[128,768]{1,0:T(8,128)(2,1)S(1)}, u32[]{:S(2)}, u32[]{:S(2)}) collective-permute-start(bf16[128,768]{1,0:T(8,128)(2,1)S(1)} %get-tuple-element.63), channel_id=1, source_target_pairs={{0,64},{16,80},{32,96},{48,112},{64,0},{80,16},{96,32},{112,48},{1... | collective-permute-start | bytes 589832 | tf_op jit(solution)/shard_map/ppermute | solution.py:234
  347.1 8.6 %collective-permute-start.7 = (bf16[128,768]{1,0:T(8,128)(2,1)S(1)}, bf16[128,768]{1,0:T(8,128)(2,1)S(1)}, u32[]{:S(2)}, u32[]{:S(2)}) collective-permute-start(bf16[128,768]{1,0:T(8,128)(2,1)S(1)} %get-tuple-element.62), channel_id=1, source_target_pairs={{0,96},{16,112},{32,0},{48,16},{64,32},{80,48},{96,64},{112,80},{1... | collective-permute-start | bytes 589832 | tf_op jit(solution)/shard_map/ppermute | solution.py:234
  357.3 31.2 %copy-start.2 = (f32[2,2048]{1,0:T(2,128)S(1)}, f32[2,2048]{1,0:T(2,128)}, u32[]{:S(2)}) copy-start(f32[2,2048]{1,0:T(2,128)} %lse_ref.1) | copy-start | bytes 49156
  405.8 35.2 %copy-start.1 = (bf16[1,768,2048]{2,1,0:T(8,128)(2,1)S(1)}, bf16[1,768,2048]{2,1,0:T(8,128)(2,1)}, u32[]{:S(2)}) copy-start(bf16[1,768,2048]{2,1,0:T(8,128)(2,1)} %param.21) | copy-start | bytes 9437188
  (8 other events, 27.0 us)
Sparse Core Ops, SparseCore 0:
  10.8 34.8 all-gather.7
  47.4 31.9 all-gather.5
  81.1 84.8 all-gather.9
